TPU v7x, 512 devices: a whole 4x8x8 slice. The times are simulated.
512 devices in a mesh: dp: 32 (over x, y), expert: 16 (over z, core).
Axes of the slice: x: 4, y: 8, z: 8, core: 2. Of those that a mesh axis runs over, the one named last changes fastest.
Arguments:
- grad_out: bfloat16 [8192, 2048], P('dp', 'expert'), may hold values from -48 to 48
- saved_inputs: bfloat16 [8192, 2048], P('dp', 'expert'), may hold values from -6 to 6
- router_probs: float32 [16, 8192], P('expert', 'dp'), may hold values from 0 to 1, as said below
- chosen: int32 [16, 512], replicated, may hold values from 0 to 8191, as said below
- gate_pre: bfloat16 [16, 512, 7168], P('expert', None, 'dp'), may hold values from -6 to 6
- up_pre: bfloat16 [16, 512, 7168], P('expert', None, 'dp'), may hold values from -6 to 6
- w_down: bfloat16 [16, 7168, 2048], P('expert', 'dp'), may hold values from -0.0625 to 0.0625
- w_up: bfloat16 [16, 7168, 2048], P('expert', 'dp'), may hold values from -0.125 to 0.125
Outputs:
- grad_tokens: bfloat16 [8192, 2048], P('dp', 'expert')
- grad_logits: float32 [16, 8192], P('expert', 'dp')
- grad_down: bfloat16 [16, 7168, 2048], P('expert', 'dp')
- grad_up: bfloat16 [16, 7168, 2048], P('expert', 'dp')
- grad_gate_pre: bfloat16 [16, 512, 7168], P('expert', None, 'dp')
Inputs may be any that keep to these rules, and one draw needn't show every extreme that they name: `chosen`: every row lists 512 different tokens in increasing order. Among the 256 consecutive tokens of one index of dp, an expert chooses at most 24, and every expert chooses exactly 24 from some index of dp. `router_probs`: each token's probabilities over the 16 experts are positive and sum to one.
All inputs are finite; a program needn't handle non-finite values.
Results may differ from a plain program's by a relative error of at most 0.04.
Values may be sent and summed in bfloat16 or wider, within the bound.
No kernel may reach another device: no remote copies, remote signals or barrier semaphores. Data moves between devices by JAX's collectives and lax.ppermute only.
A program may use at most 64 MiB of HBM per device.

v0:
```python
import jax
import jax.numpy as jnp
from jax import lax
from jax.sharding import Mesh
from jax.sharding import PartitionSpec as P

DP = ("dp_0", "dp_1")


def in_one_piece(arrays, axis, split_dim, concat_dim, along):
    widths = [a.shape[along] for a in arrays]
    both = jnp.concatenate(arrays, axis=along)
    result = lax.all_to_all(both, axis, split_axis=split_dim, concat_axis=concat_dim, tiled=True)
    return tuple(jnp.split(result, [sum(widths[:k]) for k in range(1, len(widths))], axis=along))


def sent_together(arrays, axis, dim, along):
    columns = [a.reshape(*a.shape[:along], -1) for a in arrays]
    both = jnp.concatenate(columns, axis=along)
    result, at, finished = (lax.all_gather(both, axis, axis=dim, tiled=True), 0, [])
    for a, column in zip(arrays, columns):
        share = result[..., at : at + column.shape[along]]
        finished.append(share.reshape(*share.shape[:along], *a.shape[along:]))
        at += column.shape[along]
    return tuple(finished)


def own_block(parts, axes, sequence):
    inside = parts.shape[1:]
    parts = parts.reshape(*(lax.axis_size(a) for a in axes), *inside)
    parts = jnp.moveaxis(parts, sequence, range(len(axes))).reshape(-1, *inside)
    for k in sequence:
        parts = lax.psum_scatter(parts, axes[k], scatter_dimension=0, tiled=True)
    return parts[0]


def cut_along(x, dim, size):
    shape = x.shape
    parts = x.reshape(*shape[:dim], size, shape[dim] // size, *shape[dim + 1 :])
    return jnp.moveaxis(parts, dim, 0)


def scatter_axes(x, axes, sequence, dim):
    size = lax.axis_size(axes)
    return own_block(cut_along(x, dim, size), axes, sequence)


def sum_at_owner(x, axis, dim):
    size = lax.axis_size(axis)
    parts = lax.all_to_all(cut_along(x, dim, size), axis, 0, 0, tiled=True)
    return jnp.sum(parts.astype(jnp.float32), axis=0)


def from_everyone(x, axis):
    size = lax.axis_size(axis)
    return lax.all_to_all(jnp.broadcast_to(x[None], (size, *x.shape)), axis, 0, 0, tiled=True)


def over_copies(x, axis):
    everything = from_everyone(x, axis)
    return jnp.sum(everything, axis=0)


def shard_slots(chosen, shard_index, capacity, tok_dev):
    owners = chosen // tok_dev
    firsts = jnp.sum((owners < shard_index).astype(jnp.int32), axis=1)
    counts = jnp.sum((owners == shard_index).astype(jnp.int32), axis=1)
    offsets = jnp.arange(capacity, dtype=jnp.int32)
    places = jnp.clip(firsts[:, None] + offsets[None, :], 0, chosen.shape[1] - 1)
    picked = jnp.take_along_axis(chosen, places, axis=1)
    return jnp.where(offsets[None, :] < counts[:, None], picked - shard_index * tok_dev, -1)


def grad_block(dout_rows, gate_rows, gate_piece, up_piece, down_block):
    gate_value = gate_piece.astype(jnp.float32)
    up_value = up_piece.astype(jnp.float32)
    sigmoid_gate = jax.nn.sigmoid(gate_value)
    active = gate_value * sigmoid_gate
    hidden = active * up_value
    raw_grad = lax.dot_general(
        dout_rows, down_block, (((1,), (1,)), ((), ())), preferred_element_type=jnp.float32
    )
    dot_sums = jnp.sum(hidden * raw_grad, axis=1)
    hid_grad = gate_rows.astype(jnp.float32)[:, None] * raw_grad
    up_grad = (hid_grad * active).astype(jnp.bfloat16)
    gate_grad = (
        hid_grad * up_value * sigmoid_gate * (1.0 + gate_value * (1.0 - sigmoid_gate))
    ).astype(jnp.bfloat16)
    out_grad = gate_rows[:, None] * dout_rows
    down_term = lax.dot_general(
        hidden.astype(jnp.bfloat16),
        out_grad,
        (((0,), (0,)), ((), ())),
        preferred_element_type=jnp.float32,
    )
    return (down_term, up_grad, gate_grad, dot_sums)


def local(grad_out, saved_inputs, router_probs, chosen, gate_pre, up_pre, w_down, w_up):
    tok_dev = grad_out.shape[0]
    width_dev = grad_out.shape[1]
    shard_count = lax.axis_size(DP)
    shard_index = lax.axis_index(DP)
    expert = lax.axis_index("expert")
    experts_all, slot_total = chosen.shape
    capacity = 3 * slot_total // (2 * shard_count)
    local_rows = shard_slots(chosen, shard_index, capacity, tok_dev)
    token_iota = jnp.arange(tok_dev, dtype=jnp.int32)
    picker = local_rows.reshape(-1)[:, None] == token_iota[None, :]
    stacked = jnp.concatenate([grad_out, saved_inputs], axis=1)
    packed = jnp.dot(
        picker.astype(jnp.bfloat16), stacked, preferred_element_type=jnp.float32
    ).astype(jnp.bfloat16)
    packed = packed.reshape(experts_all, capacity, 2 * width_dev)
    sent_grad = packed[:, :, :width_dev]
    sent_input = packed[:, :, width_dev:]
    dout_rows, input_rows = in_one_piece((sent_grad, sent_input), "expert", 0, 2, 1)
    own_rows = lax.dynamic_index_in_dim(local_rows, expert, 0, keepdims=False)
    router_gate = router_probs[0]
    own_hit = own_rows[:, None] == token_iota[None, :]
    gate_slot = jnp.sum(jnp.where(own_hit, router_gate[None, :], 0.0), axis=1).astype(jnp.bfloat16)
    chosen_row = lax.dynamic_index_in_dim(chosen, expert, 0, keepdims=False)
    row_owners = chosen_row // tok_dev
    shard_ids = jnp.arange(shard_count, dtype=jnp.int32)
    firsts = jnp.sum((row_owners[None, :] < shard_ids[:, None]).astype(jnp.int32), axis=1)
    counts = jnp.sum((row_owners[None, :] == shard_ids[:, None]).astype(jnp.int32), axis=1)
    rows_all = shard_count * capacity
    padded_ids = jnp.arange(rows_all, dtype=jnp.int32)
    source = padded_ids // capacity
    within = padded_ids % capacity
    is_valid = within < counts[source]
    compact = jnp.clip(firsts[source] + within, 0, slot_total - 1)
    gate_rows_all = jnp.where(is_valid[:, None], gate_pre[0][compact], jnp.zeros((), jnp.bfloat16))
    up_rows_all = jnp.where(is_valid[:, None], up_pre[0][compact], jnp.zeros((), jnp.bfloat16))
    down_block = w_down[0]
    upw_block = w_up[0]
    dout_all, input_all, gate_all = sent_together(
        (dout_rows[0], input_rows[0], gate_slot), DP, 0, 1
    )
    down_sum, up_grad_all, gate_grad_all, dots_all = grad_block(
        dout_all, gate_all, gate_rows_all, up_rows_all, down_block
    )
    up_sum = lax.dot_general(
        up_grad_all, input_all, (((0,), (0,)), ((), ())), preferred_element_type=jnp.float32
    )
    dx_back = scatter_axes(
        jnp.dot(up_grad_all, upw_block, preferred_element_type=jnp.float32).astype(jnp.bfloat16),
        DP,
        (1, 0),
        0,
    ).astype(jnp.float32)
    dots_back = sum_at_owner(dots_all.astype(jnp.bfloat16), DP, 0)
    spread = lax.all_to_all(
        dx_back[None].astype(jnp.bfloat16), "expert", split_axis=2, concat_axis=0, tiled=True
    ).astype(jnp.float32)
    placer = picker.astype(jnp.float32)
    grad_tokens = lax.dot_general(
        placer,
        spread.reshape(experts_all * capacity, -1),
        (((0,), (0,)), ((), ())),
        precision=lax.Precision.HIGHEST,
        preferred_element_type=jnp.float32,
    ).astype(jnp.bfloat16)
    gate_tokens = jnp.sum(jnp.where(own_hit, dots_back[:, None], 0.0), axis=0)
    weighted = over_copies(router_gate * gate_tokens, "expert")
    grad_logits = (router_gate * (gate_tokens - weighted))[None, :]
    slot_iota = jnp.arange(slot_total, dtype=jnp.int32)
    slot_place = row_owners * capacity + slot_iota - firsts[row_owners]
    grad_gate_pre = gate_grad_all[slot_place][None]
    return (
        grad_tokens,
        grad_logits,
        down_sum.astype(jnp.bfloat16)[None],
        up_sum.astype(jnp.bfloat16)[None],
        grad_gate_pre,
    )


def solution(mesh):
    split = Mesh(mesh.devices.reshape(4, 8, mesh.shape["expert"]), ("dp_0", "dp_1", "expert"))
    return jax.shard_map(
        local,
        mesh=split,
        in_specs=(
            P(DP, "expert"),
            P(DP, "expert"),
            P("expert", DP),
            P(),
            P("expert", None, DP),
            P("expert", None, DP),
            P("expert", DP, None),
            P("expert", DP, None),
        ),
        out_specs=(
            P(DP, "expert"),
            P("expert", DP),
            P("expert", DP, None),
            P("expert", DP, None),
            P("expert", None, DP),
        ),
        check_vma=False,
    )
```

profile of v0, /device:TPU:1, one launch (start us, length us, event | category | flops | bytes accessed | tf_op | source)
XLA Modules:
  0.0 252.8 jit_solution(8211939573065765963)
XLA Ops:
  7.2 1.0 convert_reduce_fusion.2
  8.2 0.1 fusion.41
  8.3 0.1 iota_compare_fusion.6
  8.3 0.1 lt.132
  8.4 0.1 reshape.508
  8.6 3.5 %gather_fusion.3 = s32[384]{0:T(512)S(1)} fusion(s32[16,512]{1,0:T(8,128)S(1)} %copy-done.1, s32[384]{0:T(512)S(1)} %reshape.508), kind=kCustom, calls=%fused_computation.3 | custom fusion | bytes 6144 | tf_op jit(solution)/shard_map/jit(take_along_axis)/gather | solution.py:70
  12.0 0.1 add.191
  12.1 0.1 add.192
  12.2 0.1 lt.135
  12.3 0.3 convolution_convert_fusion.1
  12.6 0.7 pad_maximum_fusion.1
  13.3 11.8 %all-to-all-start = ((bf16[16,48,128]{2,1,0:T(8,128)(2,1)}), bf16[16,48,128]{2,1,0:T(8,128)(2,1)S(1)}, u32[]{:S(2)}, u32[]{:S(2)}) async-start(bf16[16,48,128]{2,1,0:T(8,128)(2,1)} %pad_maximum_fusion.1), calls=%async_computation | async-start | bytes 393216 | tf_op jit(solution)/shard_map/all_to_all | solution.py:13
  25.2 0.1 reshape.511
  25.3 0.1 fusion.42
  25.4 0.2 select_reduce_fusion.1
  25.6 0.1 copy.69
  25.7 9.7 %all-to-all-done = bf16[16,48,128]{2,1,0:T(8,128)(2,1)S(1)} async-done(((bf16[16,48,128]{2,1,0:T(8,128)(2,1)}), bf16[16,48,128]{2,1,0:T(8,128)(2,1)S(1)}, u32[]{:S(2)}, u32[]{:S(2)}) %all-to-all-start) | async-done | bytes 196640 | tf_op jit(solution)/shard_map/all_to_all | solution.py:13
  35.4 0.7 pad_maximum_fusion
  36.2 0.1 copy.70
  37.3 0.1 convert_reduce_fusion.1
  37.4 0.7 fusion.59
  38.1 4.3 %fusion.49 = s32[768]{0:T(1024)S(1)} fusion(s32[]{:T(128)} %bitcast.68, s32[]{:T(128)} %bitcast.69, s32[]{:T(128)} %bitcast.70, s32[]{:T(128)} %bitcast.71, s32[]{:T(128)} %bitcast.72, s32[]{:T(128)} %bitcast.74, s32[]{:T(128)} %bitcast.73), kind=kLoop, calls=%fused_computation.172 | loop fusion | flops 17664 | bytes 3100 | tf_op jit(solution)/shard_map/gather | solution.py:132
  42.4 0.7 fusion.58
  43.1 15.7 %select_select_fusion = s32[768]{0:T(1024)S(1)} fusion(pred[768]{0:T(1024)(128)(4,1)S(1)} %compare_reduce_fusion, pred[768]{0:T(1024)(128)(4,1)S(1)} %compare_reduce_fusion.1, pred[768]{0:T(1024)(128)(4,1)S(1)} %compare_reduce_fusion.2, pred[768]{0:T(1024)(128)(4,1)S(1)} %compare_reduce_fusion.3, pred[768]{0:T(1024)(128)(4,1)S(1)} %compare_reduce_fusion.4, ...), kind=kLoop, calls=%fused_computation.166 | loop fusion | flops 19200 | bytes 25444 | tf_op jit(solution)/shard_map/gather | solution.py:132
  58.9 2.7 %gather_fusion = bf16[768,224]{1,0:T(8,128)(2,1)S(1)} fusion(bf16[512,224]{1,0:T(8,128)(2,1)S(1)} %bitcast.138, s32[1024]{0:T(1024)S(1)} %pad_clamp_fusion.1), kind=kCustom, calls=%fused_computation | custom fusion | bytes 691200 | tf_op jit(solution)/shard_map/gather | solution.py:133
  61.5 0.2 copy.71
  61.7 0.1 copy.76
  61.9 2.7 %gather_fusion.1 = bf16[768,224]{1,0:T(8,128)(2,1)S(1)} fusion(bf16[512,224]{1,0:T(8,128)(2,1)S(1)} %bitcast.139, s32[1024]{0:T(1024)S(1)} %pad_clamp_fusion.1), kind=kCustom, calls=%fused_computation.1 | custom fusion | bytes 691200 | tf_op jit(solution)/shard_map/gather | solution.py:134
  64.5 0.2 copy.77
  64.7 0.7 fusion.57
  65.4 4.4 %fusion.50 = s32[768]{0:T(1024)S(1)} fusion(s32[]{:T(128)} %bitcast.35, s32[]{:T(128)} %bitcast.36, s32[]{:T(128)} %bitcast.37, s32[]{:T(128)} %bitcast.38, s32[]{:T(128)} %bitcast.39, s32[]{:T(128)} %bitcast.41, s32[]{:T(128)} %bitcast.40), kind=kLoop, calls=%fused_computation.173 | loop fusion | flops 17664 | bytes 3100 | tf_op jit(solution)/shard_map/gather | solution.py:131
  69.8 0.7 fusion.56
  70.6 15.7 %fusion.44 = pred[768]{0:T(1024)(128)(4,1)S(1)} fusion(pred[768]{0:T(1024)(128)(4,1)S(1)} %compare_reduce_fusion, pred[768]{0:T(1024)(128)(4,1)S(1)} %compare_reduce_fusion.1, pred[768]{0:T(1024)(128)(4,1)S(1)} %compare_reduce_fusion.2, pred[768]{0:T(1024)(128)(4,1)S(1)} %compare_reduce_fusion.3, pred[768]{0:T(1024)(128)(4,1)S(1)} %compare_reduce_fusion.4, ...), kind=kLoop, calls=%fused_computation.163 | loop fusion | flops 24576 | bytes 23140 | tf_op jit(solution)/shard_map/lt | solution.py:131
  86.3 40.2 %all-gather.2.cloned.1.call-done = bf16[768,4097]{1,0:T(8,128)(2,1)} async-done(((bf16[24,4097]{1,0:T(8,128)(2,1)}), bf16[768,4097]{1,0:T(8,128)(2,1)}) %all-gather.2.cloned.1.call-update) | async-done | bytes 6293008 | tf_op jit(solution)/shard_map/all_gather | solution.py:20
  126.4 1.1 slice_reduce_fusion
  127.5 3.3 %fusion.24 = (bf16[768,224]{0,1:T(8,128)(2,1)S(1)}, bf16[768]{0:T(1024)(128)(2,1)S(1)}, bf16[768,224]{0,1:T(8,128)(2,1)S(1)}) fusion(f32[768]{0:T(1024)S(1)} %mul.77, bf16[768,224]{0,1:T(8,128)(2,1)S(1)} %copy.71, pred[768]{0:T(1024)(128)(4,1)S(1)} %fusion.44, bf16[768,224]{0,1:T(8,128)(2,1)S(1)} %copy.77, bf16[1,224,2048]{2,1,0:T(8,128)(2,1)S(1)} %copy-done.5, ...), kind=kOutput, calls=%fused_computation.28 | convolution fusion | flops 708254976 | bytes 5444864 | tf_op jit(solution)/shard_map/dot_general | solution.py:80
  130.9 1.0 convolution_convert_fusion
  131.9 2.1 copy.72
  134.1 4.3 %compare_select_fusion.5 = (s32[512,1]{0,1:T(1,128)S(1)}, s32[512,1]{0,1:T(1,128)S(1)}, s32[512,1]{0,1:T(1,128)S(1)}) fusion(s32[]{:T(128)} %bitcast.68, s32[]{:T(128)} %bitcast.69, s32[]{:T(128)} %bitcast.70, s32[]{:T(128)} %bitcast.71, s32[]{:T(128)} %bitcast.72, s32[]{:T(128)} %bitcast.74, s32[]{:T(128)} %bitcast.73, s32[16,512]{1,0:T(8,128)S(1)} %copy-done.1, ...), kind=kLoop, calls=%fused_computation.131 | loop fusion | flops 15360 | bytes 8224 | tf_op jit(solution)/shard_map/gather | solution.py:168
  138.4 0.2 compare_reduce_fusion.49
  138.6 15.7 %select_select_fusion.1 = s32[512]{0:T(512)S(1)} fusion(pred[512]{0:T(512)(128)(4,1)S(1)} %get-tuple-element.61, pred[512]{0:T(512)(128)(4,1)S(1)} %get-tuple-element.60, pred[512]{0:T(512)(128)(4,1)S(1)} %get-tuple-element.59, pred[512]{0:T(512)(128)(4,1)S(1)} %get-tuple-element.58, pred[512]{0:T(512)(128)(4,1)S(1)} %get-tuple-element.57, ...), kind=kLoop, calls=%fused_computation.177 | loop fusion | flops 12800 | bytes 16996 | tf_op jit(solution)/shard_map/gather | solution.py:168
  154.3 0.7 convert_element_type.102
  155.0 5.7 %all-to-all-start.2 = ((bf16[32,1,24]{2,1,0:T(2,128)(2,1)}), bf16[32,1,24]{2,1,0:T(2,128)(2,1)S(1)}, u32[]{:S(2)}, u32[]{:S(2)}) async-start(bf16[32,1,24]{2,1,0:T(2,128)(2,1)} %convert_element_type.102), calls=%async_computation.4 | async-start | bytes 32768 | tf_op jit(solution)/shard_map/all_to_all | solution.py:50
  160.7 18.2 %reduce-scatter.3.cloned.1.call-done = bf16[4,24,2048]{2,1,0:T(8,128)(2,1)} async-done(((bf16[32,24,2048]{2,1,0:T(8,128)(2,1)}), bf16[4,24,2048]{2,1,0:T(8,128)(2,1)}) %reduce-scatter.3.cloned.1.call-update) | async-done | bytes 393232 | tf_op jit(solution)/shard_map/reduce_scatter | solution.py:33
  178.9 3.9 %fusion.16 = bf16[1,224,2048]{2,1,0:T(8,128)(2,1)} fusion(bf16[768,4097]{1,0:T(8,128)(2,1)} %all-gather.2.cloned.1.call-done, bf16[768]{0:T(1024)(128)(2,1)S(1)} %slice_reduce_fusion, bf16[768,224]{0,1:T(8,128)(2,1)S(1)} %copy.77, pred[768]{0:T(1024)(128)(4,1)S(1)} %fusion.44, bf16[768,224]{0,1:T(8,128)(2,1)S(1)} %copy.71), kind=kOutput, calls=%fused_computation.15 | convolution fusion | flops 708395008 | bytes 4753664 | tf_op jit(solution)/shard_map/dot_general | solution.py:90
  182.9 0.1 select_reduce_fusion
  183.0 0.6 broadcast_in_dim.100
  183.6 11.1 %all-to-all-start.3 = ((f32[16,1,256]{2,1,0:T(1,128)}), f32[16,1,256]{2,1,0:T(1,128)S(1)}, u32[]{:S(2)}, u32[]{:S(2)}) async-start(f32[16,1,256]{2,1,0:T(1,128)} %broadcast_in_dim.100), calls=%async_computation.5 | async-start | bytes 32768 | tf_op jit(solution)/shard_map/all_to_all | solution.py:56
  194.7 3.7 %fusion.13 = bf16[1,224,2048]{2,1,0:T(8,128)(2,1)} fusion(bf16[768,224]{0,1:T(8,128)(2,1)S(1)} %get-tuple-element.69, bf16[768,4097]{1,0:T(8,128)(2,1)} %all-gather.2.cloned.1.call-done), kind=kOutput, calls=%fused_computation.14 | convolution fusion | flops 705101824 | bytes 4407296 | tf_op jit(solution)/shard_map/dot_general | solution.py:143
  198.4 0.2 copy.80
  198.6 2.0 gather_fusion.2
  200.6 0.8 copy.81
  201.4 0.7 all-to-all-done.3
  202.1 6.8 %reduce-scatter.5.cloned.1.call-done = bf16[1,24,2048]{2,1,0:T(8,128)(2,1)} async-done(((bf16[4,24,2048]{2,1,0:T(8,128)(2,1)}), bf16[1,24,2048]{2,1,0:T(8,128)(2,1)}) %reduce-scatter.5.cloned.1.call-update) | async-done | bytes 98320 | tf_op jit(solution)/shard_map/reduce_scatter | solution.py:33
  208.9 2.0 copy.73
  210.9 0.5 broadcast.1058
  211.4 11.5 %reduce.110 = bf16[2048,24]{1,0:T(8,128)(2,1)S(1)} reduce(bf16[2048,1,24]{2,1,0:T(2,128)(2,1)S(1)} %bitcast.142, bf16[]{:T(256)} %broadcast.1058), dimensions={1}, to_apply=%bitcast.127.reduce_sub_computation | reduce | bytes 196610
  223.0 1.3 reshape.736
  224.3 10.5 %all-to-all-start.1 = ((bf16[16,2,1536]{2,1,0:T(2,128)(2,1)}), bf16[16,2,1536]{2,1,0:T(2,128)(2,1)S(1)}, u32[]{:S(2)}, u32[]{:S(2)}) async-start(bf16[16,2,1536]{2,1,0:T(2,128)(2,1)} %reshape.736), calls=%async_computation.3 | async-start | bytes 196608 | tf_op jit(solution)/shard_map/all_to_all | solution.py:153
  234.8 0.6 subtract_multiply_fusion
  235.3 7.9 %all-to-all-done.1 = bf16[16,2,1536]{2,1,0:T(2,128)(2,1)S(1)} async-done(((bf16[16,2,1536]{2,1,0:T(2,128)(2,1)}), bf16[16,2,1536]{2,1,0:T(2,128)(2,1)S(1)}, u32[]{:S(2)}, u32[]{:S(2)}) %all-to-all-start.1) | async-done | bytes 98336 | tf_op jit(solution)/shard_map/all_to_all | solution.py:153
  243.2 1.5 reshape.737
  244.7 0.5 copy.74
  245.3 1.0 convolution_convert_fusion.2
  (66 shorter events, 1.5 us)
Async XLA Ops:
  7.2 123.7 %copy-start = (bf16[1,224,2048]{2,1,0:T(8,128)(2,1)S(1)}, bf16[1,224,2048]{2,1,0:T(8,128)(2,1)}, u32[]{:S(2)}) copy-start(bf16[1,224,2048]{2,1,0:T(8,128)(2,1)} %param.15) | copy-start | bytes 2752516
  7.2 1.3 copy-start.1
  8.5 3.8 %copy-start.6 = (bf16[256,128]{1,0:T(8,128)(2,1)S(1)}, bf16[256,128]{1,0:T(8,128)(2,1)}, u32[]{:S(2)}) copy-start(bf16[256,128]{1,0:T(8,128)(2,1)} %param.9) | copy-start | bytes 196612
  8.5 3.8 %copy-start.7 = (bf16[256,128]{1,0:T(8,128)(2,1)S(1)}, bf16[256,128]{1,0:T(8,128)(2,1)}, u32[]{:S(2)}) copy-start(bf16[256,128]{1,0:T(8,128)(2,1)} %param.8) | copy-start | bytes 196612
  8.6 16.8 %copy-start.4 = (f32[1,256]{1,0:T(1,128)S(1)}, f32[1,256]{1,0:T(1,128)}, u32[]{:S(2)}) copy-start(f32[1,256]{1,0:T(1,128)} %param.10) | copy-start | bytes 3076
  12.0 24.2 %copy-start.2 = (bf16[1,512,224]{1,2,0:T(8,128)(2,1)S(1)}, bf16[1,512,224]{1,2,0:T(8,128)(2,1)}, u32[]{:S(2)}) copy-start(bf16[1,512,224]{1,2,0:T(8,128)(2,1)} %param.12) | copy-start | bytes 688132
  13.3 22.0 %all-to-all-start = ((bf16[16,48,128]{2,1,0:T(8,128)(2,1)}), bf16[16,48,128]{2,1,0:T(8,128)(2,1)S(1)}, u32[]{:S(2)}, u32[]{:S(2)}) async-start(bf16[16,48,128]{2,1,0:T(8,128)(2,1)} %pad_maximum_fusion.1), calls=%async_computation | async-start | bytes 393216 | tf_op jit(solution)/shard_map/all_to_all | solution.py:13
  25.2 101.3 %all-gather.2.cloned.1.call-start = ((), (), s32[]{:S(2)}) async-start(), calls=%async_computation.6 | async-start | bytes 6690816 | tf_op jit(solution)/shard_map/all_gather | solution.py:20
  25.7 36.0 %copy-start.3 = (bf16[1,512,224]{1,2,0:T(8,128)(2,1)S(1)}, bf16[1,512,224]{1,2,0:T(8,128)(2,1)}, u32[]{:S(2)}) copy-start(bf16[1,512,224]{1,2,0:T(8,128)(2,1)} %param.13) | copy-start | bytes 688132
  36.1 142.8 %reduce-scatter.3.cloned.1.call-start = ((), (), s32[]{:S(2)}) async-start(), calls=%async_computation.7 | async-start | bytes 3538944 | tf_op jit(solution)/shard_map/reduce_scatter | solution.py:33
  61.5 66.0 %copy-start.5 = (bf16[1,224,2048]{2,1,0:T(8,128)(2,1)S(1)}, bf16[1,224,2048]{2,1,0:T(8,128)(2,1)}, u32[]{:S(2)}) copy-start(bf16[1,224,2048]{2,1,0:T(8,128)(2,1)} %param.14) | copy-start | bytes 2752516
  155.0 27.9 %all-to-all-start.2 = ((bf16[32,1,24]{2,1,0:T(2,128)(2,1)}), bf16[32,1,24]{2,1,0:T(2,128)(2,1)S(1)}, u32[]{:S(2)}, u32[]{:S(2)}) async-start(bf16[32,1,24]{2,1,0:T(2,128)(2,1)} %convert_element_type.102), calls=%async_computation.4 | async-start | bytes 32768 | tf_op jit(solution)/shard_map/all_to_all | solution.py:50
  160.7 48.2 %reduce-scatter.5.cloned.1.call-start = ((), (), s32[]{:S(2)}) async-start(), calls=%async_computation.8 | async-start | bytes 491520 | tf_op jit(solution)/shard_map/reduce_scatter | solution.py:33
  183.6 18.5 %all-to-all-start.3 = ((f32[16,1,256]{2,1,0:T(1,128)}), f32[16,1,256]{2,1,0:T(1,128)S(1)}, u32[]{:S(2)}, u32[]{:S(2)}) async-start(f32[16,1,256]{2,1,0:T(1,128)} %broadcast_in_dim.100), calls=%async_computation.5 | async-start | bytes 32768 | tf_op jit(solution)/shard_map/all_to_all | solution.py:56
  224.3 19.0 %all-to-all-start.1 = ((bf16[16,2,1536]{2,1,0:T(2,128)(2,1)}), bf16[16,2,1536]{2,1,0:T(2,128)(2,1)S(1)}, u32[]{:S(2)}, u32[]{:S(2)}) async-start(bf16[16,2,1536]{2,1,0:T(2,128)(2,1)} %reshape.736), calls=%async_computation.3 | async-start | bytes 196608 | tf_op jit(solution)/shard_map/all_to_all | solution.py:153
Sparse Core Ops, SparseCore 0:
  36.2 90.1 all-gather.1
  134.2 44.6 reduce-scatter.2
  181.8 27.1 reduce-scatter.4
where the time goes:
time: 254 us; the launch traced here: 253 us
  waiting for transfers between devices  83.5 us (33%)
  other arithmetic  76.5 us (30%)
  starting transfers between devices  39.3 us (15%)
  local copies, waits for them, and re-layouts  26.3 us (10%)
  between operations  14.2 us (6%)
  matrix products  13.2 us (5%)
    all_gather x1, waiting for transfers between devices, sent_together(): lax.all_gather(both, axis, axis=dim, tiled=True)  40.2 us
    reduce_scatter x2, waiting for transfers between devices, own_block(): parts = lax.psum_scatter(parts, axes[k], scatter_dimension=0, tiled=True)  25 us
    gather x3, other arithmetic, local(): slot_place = row_owners * capacity + slot_iota - firsts[row_owners]  20.2 us
    gather x2, other arithmetic, local(): compact = jnp.clip(firsts[source] + within, 0, slot_total - 1)  20 us
    lt x1, other arithmetic, local(): is_valid = within < counts[source]  15.7 us
    all_to_all x1, starting transfers between devices, in_one_piece(): lax.all_to_all(both, axis, split_axis=split_dim, concat_axis=concat_dim,...  11.8 us
    unnamed x1, other arithmetic  11.5 us
    all_to_all x1, starting transfers between devices, from_everyone(): lax.all_to_all(jnp.broadcast_to(x[None], (size, *x.shape)), axis, 0, 0, t...  11.1 us
  transfers between devices with their start and end apart: 7, of which 6 were waited for; matrix products, arithmetic and copies ran while one was open for 33% of the time, Pallas kernels for 0%

commit v1 on v0

v1 whole, which is shorter than its diff:
```python
import jax
import jax.numpy as jnp
from jax import lax
from jax.sharding import Mesh
from jax.sharding import PartitionSpec as P

X, Y, E = "dp_0", "dp_1", "expert"
BF, F32 = jnp.bfloat16, jnp.float32
PAD = 8


def exchange(x, axis):
    return lax.all_to_all(x, axis, 0, 0, tiled=True)


def to_all(x, axis):
    size = lax.axis_size(axis)
    return exchange(jnp.broadcast_to(x[None], (size, *x.shape)), axis)


def dot(a, b, ca, cb):
    return lax.dot_general(a, b, (((ca,), (cb,)), ((), ())), preferred_element_type=F32)


def onehot(mask):
    return mask.astype(BF)


def rows_of(n, m):
    return lax.broadcasted_iota(jnp.int32, (n, m), 0)


def lanes_of(n, m):
    return lax.broadcasted_iota(jnp.int32, (n, m), 1)


def features_to_x(w, nx):
    units, width = w.shape
    parts = w.reshape(units, nx, width // nx).transpose(1, 0, 2)
    return exchange(parts, X).reshape(nx * units, width // nx)


def features_home(g, nx):
    parts = exchange(g.reshape(nx, g.shape[0] // nx, g.shape[1]), X)
    return parts.transpose(1, 0, 2).reshape(parts.shape[1], -1)


def local(grad_out, saved_inputs, router_probs, chosen, gate_pre, up_pre, w_down, w_up):
    tok_dev, width_dev = grad_out.shape
    nx, ny, ne = lax.axis_size(X), lax.axis_size(Y), lax.axis_size(E)
    shards = nx * ny
    xi, yi, ei = lax.axis_index(X), lax.axis_index(Y), lax.axis_index(E)
    shard = xi * ny + yi
    slots = chosen.shape[1]
    cap = 3 * slots // (2 * shards)
    units = gate_pre.shape[2]
    quarter = ne // nx
    part = quarter * width_dev
    lane = 128

    firsts = jnp.sum((chosen < shard * tok_dev).astype(jnp.int32), axis=1)
    ends = jnp.sum((chosen < (shard + 1) * tok_dev).astype(jnp.int32), axis=1)
    offsets = jnp.arange(cap + PAD, dtype=jnp.int32)
    places = firsts[:, None] + offsets[None, :]
    live = (places < ends[:, None]) & (offsets < cap)[None, :]
    slot_iota = jnp.arange(slots, dtype=jnp.int32)
    found = jnp.sum(
        jnp.where(places[:, :, None] == slot_iota[None, None, :], chosen[:, None, :], 0), axis=2
    )
    local_rows = jnp.where(live, found - shard * tok_dev, -1)
    token_iota = jnp.arange(tok_dev, dtype=jnp.int32)
    picker = onehot(local_rows[:, :, None] == token_iota[None, None, :])

    flat_pick = picker.reshape(ne * (cap + PAD), tok_dev)
    sent_grad = dot(flat_pick, grad_out, 1, 0).astype(BF).reshape(ne, cap + PAD, width_dev)
    sent_input = dot(flat_pick, saved_inputs, 1, 0).astype(BF).reshape(ne, cap + PAD, width_dev)
    sent = jnp.concatenate([sent_grad[:, :cap], sent_input[:, :cap]], axis=1)
    rows = exchange(sent, E).reshape(nx, quarter, 2 * cap, width_dev)

    down_part = features_to_x(w_down[0], nx)
    up_part = features_to_x(w_up[0], nx)

    own_rows = lax.dynamic_index_in_dim(local_rows, ei, 0, keepdims=False)
    own_rows = jnp.pad(own_rows, (0, lane - cap - PAD), constant_values=-1)
    own_hit = onehot(own_rows[:, None] == token_iota[None, :])
    gate_row = dot(router_probs.astype(BF), own_hit, 1, 1).astype(BF)
    gate_tile = jnp.broadcast_to(
        jnp.pad(gate_row, ((0, PAD - 1), (0, 0)))[None, None], (nx, quarter, PAD, lane)
    )
    rows = exchange(jnp.concatenate([rows, gate_tile], axis=2), X)
    grads = rows[:, :, :cap].transpose(0, 2, 1, 3).reshape(nx * cap, part)
    inputs = rows[:, :, cap : 2 * cap].transpose(0, 2, 1, 3).reshape(nx * cap, part)
    gates = jnp.pad(rows[:, 0, 2 * cap], ((0, PAD - nx), (0, part - lane)))
    block = nx * cap + PAD
    grads_all = to_all(jnp.concatenate([grads, gates], axis=0), Y)
    inputs_all = to_all(inputs, Y)

    chosen_row = lax.dynamic_index_in_dim(chosen, ei, 0, keepdims=True)
    owner = chosen_row // tok_dev
    shard_col = rows_of(shards, slots)
    before = jnp.sum((owner < shard_col).astype(jnp.int32), axis=1, keepdims=True)
    within = lanes_of(1, slots) - jnp.sum(
        jnp.where(owner == shard_col, before, 0), axis=0, keepdims=True
    )
    owner_x, owner_y = owner // ny, owner % ny
    spot = owner_x * cap + within
    place_block = onehot(rows_of(ny * block, slots) == owner_y * block + spot)
    place_rows = onehot(rows_of(ny * nx * cap, slots) == owner_y * (nx * cap) + spot)
    owner_hit = rows_of(shards, slots) == owner_y * nx + owner_x
    within_hit = onehot(rows_of(lane, slots) == within)

    gate_value = gate_pre[0].T.astype(F32)
    up_value = up_pre[0].T.astype(F32)
    sig = jax.nn.sigmoid(gate_value)
    active = gate_value * sig
    hidden = active * up_value
    hidden_all = to_all(hidden.astype(BF), X).reshape(nx * units, slots)

    grads_slots = dot(place_block, grads_all.reshape(ny * block, part), 0, 0).astype(BF)
    gates_all = grads_all[:, nx * cap : nx * cap + nx, :lane].reshape(shards, lane)
    gate_slot = jnp.sum(
        jnp.where(owner_hit, dot(gates_all, within_hit, 1, 0), 0.0), axis=0, keepdims=True
    )
    raw_part = dot(down_part, grads_slots, 1, 1).astype(BF).reshape(nx, units, slots)
    raw_grad = jnp.sum(exchange(raw_part, X).astype(F32), axis=0)
    dots = jnp.sum(hidden * raw_grad, axis=0, keepdims=True)
    hid_grad = gate_slot * raw_grad
    up_grad = (hid_grad * active).astype(BF)
    gate_grad = (hid_grad * up_value * sig * (1.0 + gate_value * (1.0 - sig))).astype(BF)
    up_all = to_all(up_grad, X).reshape(nx * units, slots)

    dx = dot(up_all, up_part, 0, 0).astype(BF)
    dx_rows = dot(place_rows, dx, 1, 0).astype(BF).reshape(ny, nx * cap, part)
    dots_own = jnp.where(owner_hit, dots, 0.0).astype(BF)
    dots_rows = dot(dots_own, within_hit, 1, 1).astype(BF).reshape(ny, nx, lane)
    dots_rows = jnp.pad(dots_rows, ((0, 0), (0, PAD - nx), (0, part - lane)))
    dx_back = exchange(jnp.concatenate([dx_rows, dots_rows], axis=1), Y)
    dx_sum = jnp.sum(dx_back.astype(F32), axis=0).astype(BF)
    dots_sum = dx_sum[nx * cap : nx * cap + nx].reshape(nx, 1, part)
    dx_sum = jnp.concatenate(
        [dx_sum[: nx * cap].reshape(nx, cap, part), jnp.pad(dots_sum, ((0, 0), (0, PAD - 1), (0, 0)))],
        axis=1,
    )
    dx_own = exchange(dx_sum, X)
    gate_tokens = jnp.sum(dot(dx_own[:, cap, :lane], own_hit, 1, 0), axis=0, keepdims=True)
    product = router_probs * gate_tokens
    high = lax.reduce_precision(product, 8, 7)
    low = product - high
    tail = jnp.concatenate([high, low], axis=0).astype(BF).reshape(-1, lane)
    tail = jnp.pad(tail, ((0, PAD - tail.shape[0]), (0, 0)))
    to_experts = dx_own[:, :cap].reshape(nx, cap, quarter, width_dev).transpose(0, 2, 1, 3)
    to_experts = to_experts.reshape(ne, cap, width_dev)
    spread = exchange(
        jnp.concatenate([to_experts, jnp.broadcast_to(tail[None], (ne, PAD, lane))], axis=1), E
    )
    grad_tokens = dot(flat_pick, spread.reshape(-1, width_dev), 0, 0).astype(BF)
    pieces = jnp.sum(spread[:, cap : cap + 2 * tok_dev // lane].astype(F32), axis=0)
    router_sum = jnp.sum(pieces.reshape(2, 1, tok_dev), axis=0)
    grad_logits = router_probs * (gate_tokens - router_sum)

    hidden_gated = (hidden_all.astype(F32) * gate_slot).astype(BF)
    grad_down = dot(hidden_gated, grads_slots, 1, 0).astype(BF)
    inputs_slots = dot(place_rows, inputs_all.reshape(-1, part), 0, 0).astype(BF)
    grad_up = dot(up_all, inputs_slots, 1, 0).astype(BF)
    grad_down = features_home(grad_down, nx)
    grad_up = features_home(grad_up, nx)
    return grad_tokens, grad_logits, grad_down[None], grad_up[None], gate_grad.T[None]


def solution(mesh):
    split = Mesh(mesh.devices.reshape(4, 8, mesh.shape["expert"]), (X, Y, E))
    dp = (X, Y)
    return jax.shard_map(
        local,
        mesh=split,
        in_specs=(
            P(dp, E),
            P(dp, E),
            P(E, dp),
            P(),
            P(E, None, dp),
            P(E, None, dp),
            P(E, dp, None),
            P(E, dp, None),
        ),
        out_specs=(P(dp, E), P(E, dp), P(E, dp, None), P(E, dp, None), P(E, None, dp)),
        check_vma=False,
    )
```

time: 254 us -> 259 us (1.020)
  other arithmetic: 76.5 us -> 8.94 us
  waiting for transfers between devices: 83.5 us -> 122 us
  blocking collectives: 0 us -> 32.7 us
  starting transfers between devices: 39.3 us -> 65.2 us
  between operations: 14.2 us -> 1.14 us
  local copies, waits for them, and re-layouts: 26.3 us -> 15.6 us
    all_to_all x4 -> x12, waiting for transfers between devices: 18.2 us -> 122 us  [exchange(): return lax.all_to_all(x, axis, 0, 0, tiled=True)]
    gather x34 -> x0, other arithmetic: 45.6 us -> none  [the longest x3 20.2 us: local(): slot_place = row_owners * capacity + slot_iota - firsts[row_owners]]
    all_gather x1 -> x0, waiting for transfers between devices: 40.2 us -> none  [sent_together(): lax.all_gather(both, axis, axis=dim, tiled=True)]
    all_to_all x0 -> x2, blocking collectives: none -> 32.7 us  [exchange(): return lax.all_to_all(x, axis, 0, 0, tiled=True)]
    all_to_all x4 -> x12, starting transfers between devices: 39.2 us -> 65.2 us  [exchange(): return lax.all_to_all(x, axis, 0, 0, tiled=True)]
    reduce_scatter x2 -> x0, waiting for transfers between devices: 25 us -> none  [own_block(): parts = lax.psum_scatter(parts, axes[k], scatter_dimension=0, tiled=True)]
    lt x2, other arithmetic: 15.8 us -> 0.08 us  [local(): live = (places < ends[:, None]) & (offsets < cap)[None, :]]
    gather x12 -> x0, local copies, waits for them, and re-layouts: 14.1 us -> none  [the longest x3 3.62 us: shard_slots(): picked = jnp.take_along_axis(chosen, places, axis=1)]
  transfers between devices with their start and end apart: 7 -> 12, of which waited for: 6 -> 12; matrix products, arithmetic and copies ran while one was open for 33% -> 9% of each run, Pallas kernels for 0% -> 0%
where the time goes in v1:
time: 259 us; the launch traced here: 258 us
  waiting for transfers between devices  122 us (47%)
  starting transfers between devices  65.2 us (25%)
  blocking collectives  32.7 us (13%)
  local copies, waits for them, and re-layouts  15.6 us (6%)
  matrix products  12.7 us (5%)
  other arithmetic  8.94 us (3%)
    all_to_all x12, waiting for transfers between devices, exchange(): return lax.all_to_all(x, axis, 0, 0, tiled=True)  122 us
    all_to_all x12, starting transfers between devices, exchange(): return lax.all_to_all(x, axis, 0, 0, tiled=True)  65.2 us
    all_to_all x2, blocking collectives, exchange(): return lax.all_to_all(x, axis, 0, 0, tiled=True)  32.7 us
    dot_general x12, matrix products, dot(): lax.dot_general(a, b, (((ca,), (cb,)), ((), ())), preferred_element_type=...  12.7 us
  transfers between devices with their start and end apart: 12, of which 12 were waited for; matrix products, arithmetic and copies ran while one was open for 9% of the time, Pallas kernels for 0%

profile of v1, /device:TPU:1, one launch (start us, length us, event | category | flops | bytes accessed | tf_op | source)
XLA Modules:
  0.0 257.9 jit_solution(9521867107560449403)
XLA Ops:
  0.7 0.9 convert_reduce_fusion.3
  1.6 1.2 select_reduce_fusion
  3.3 0.3 convolution_convert_fusion.3
  3.6 1.1 convolution_convert_fusion.4
  4.7 0.7 pad_maximum_fusion.1
  5.4 11.8 %all-to-all-start = ((bf16[16,48,128]{2,1,0:T(8,128)(2,1)}), bf16[16,48,128]{2,1,0:T(8,128)(2,1)S(1)}, u32[]{:S(2)}, u32[]{:S(2)}) async-start(bf16[16,48,128]{2,1,0:T(8,128)(2,1)} %pad_maximum_fusion.1), calls=%async_computation | async-start | bytes 393216 | tf_op jit(solution)/shard_map/all_to_all | solution.py:13
  17.3 0.2 fusion.13
  17.5 9.9 %all-to-all-done = bf16[16,48,128]{2,1,0:T(8,128)(2,1)S(1)} async-done(((bf16[16,48,128]{2,1,0:T(8,128)(2,1)}), bf16[16,48,128]{2,1,0:T(8,128)(2,1)S(1)}, u32[]{:S(2)}, u32[]{:S(2)}) %all-to-all-start) | async-done | bytes 196640 | tf_op jit(solution)/shard_map/all_to_all | solution.py:13
  27.5 10.2 %all_to_all.70 = bf16[4,4,56,128]{3,2,1,0:T(8,128)(2,1)S(1)} all-to-all(bf16[4,4,56,128]{3,2,1,0:T(8,128)(2,1)S(1)} %pad_maximum_fusion), channel_id=1, replica_groups=mesh['dp_0'=4,'dp_1'=8,'expert'=16] {'dp_0'}, dimensions={0} | all-to-all | bytes 458752 | tf_op jit(solution)/shard_map/all_to_all | solution.py:13
  37.6 0.7 slice_bitcast_fusion
  38.4 1.0 broadcast_in_dim.109
  39.4 7.0 %all-to-all-start.2 = ((bf16[8,104,512]{2,1,0:T(8,128)(2,1)}), bf16[8,104,512]{2,1,0:T(8,128)(2,1)S(1)}, u32[]{:S(2)}, u32[]{:S(2)}) async-start(bf16[8,104,512]{2,1,0:T(8,128)(2,1)} %broadcast_in_dim.109), calls=%async_computation.2 | async-start | bytes 1703936 | tf_op jit(solution)/shard_map/all_to_all | solution.py:13
  46.3 0.7 reshape_squeeze.6
  47.0 1.1 copy.43
  48.1 0.7 compare_select_fusion.1
  49.0 22.3 %all-to-all-done.2 = bf16[8,104,512]{2,1,0:T(8,128)(2,1)S(1)} async-done(((bf16[8,104,512]{2,1,0:T(8,128)(2,1)}), bf16[8,104,512]{2,1,0:T(8,128)(2,1)S(1)}, u32[]{:S(2)}, u32[]{:S(2)}) %all-to-all-start.2) | async-done | bytes 852000 | tf_op jit(solution)/shard_map/all_to_all | solution.py:13
  71.3 3.5 %all-to-all-start.3 = ((bf16[4,224,512]{2,1,0:T(8,128)(2,1)}), bf16[4,224,512]{2,1,0:T(8,128)(2,1)S(1)}, u32[]{:S(2)}, u32[]{:S(2)}) async-start(bf16[4,224,512]{2,1,0:T(8,128)(2,1)} %copy.43), calls=%async_computation.3 | async-start | bytes 1835008 | tf_op jit(solution)/shard_map/all_to_all | solution.py:13
  74.9 0.8 fusion.9
  75.6 12.4 %all-to-all-done.3 = bf16[4,224,512]{2,1,0:T(8,128)(2,1)S(1)} async-done(((bf16[4,224,512]{2,1,0:T(8,128)(2,1)}), bf16[4,224,512]{2,1,0:T(8,128)(2,1)S(1)}, u32[]{:S(2)}, u32[]{:S(2)}) %all-to-all-start.3) | async-done | bytes 917536 | tf_op jit(solution)/shard_map/all_to_all | solution.py:13
  88.1 0.7 fusion.6
  88.8 1.3 copy.44
  90.1 3.6 %all-to-all-start.4 = ((bf16[4,224,512]{2,1,0:T(8,128)(2,1)}), bf16[4,224,512]{2,1,0:T(8,128)(2,1)S(1)}, u32[]{:S(2)}, u32[]{:S(2)}) async-start(bf16[4,224,512]{2,1,0:T(8,128)(2,1)} %bitcast.17), calls=%async_computation.4 | async-start | bytes 1835008 | tf_op jit(solution)/shard_map/all_to_all | solution.py:13
  93.8 0.7 reshape_squeeze.7
  94.4 1.1 copy.62
  95.5 10.6 %all-to-all-done.4 = bf16[4,224,512]{2,1,0:T(8,128)(2,1)S(1)} async-done(((bf16[4,224,512]{2,1,0:T(8,128)(2,1)}), bf16[4,224,512]{2,1,0:T(8,128)(2,1)S(1)}, u32[]{:S(2)}, u32[]{:S(2)}) %all-to-all-start.4) | async-done | bytes 917536 | tf_op jit(solution)/shard_map/all_to_all | solution.py:13
  106.2 3.5 %all-to-all-start.6 = ((bf16[4,224,512]{2,1,0:T(8,128)(2,1)}), bf16[4,224,512]{2,1,0:T(8,128)(2,1)S(1)}, u32[]{:S(2)}, u32[]{:S(2)}) async-start(bf16[4,224,512]{2,1,0:T(8,128)(2,1)} %bitcast.140), calls=%async_computation.6 | async-start | bytes 1835008 | tf_op jit(solution)/shard_map/all_to_all | solution.py:13
  109.7 0.8 slice.65
  110.5 0.2 fusion.11
  110.8 0.9 multiply_convert_fusion
  111.7 9.2 %all-to-all-done.6 = bf16[4,224,512]{2,1,0:T(8,128)(2,1)S(1)} async-done(((bf16[4,224,512]{2,1,0:T(8,128)(2,1)}), bf16[4,224,512]{2,1,0:T(8,128)(2,1)S(1)}, u32[]{:S(2)}, u32[]{:S(2)}) %all-to-all-start.6) | async-done | bytes 917536 | tf_op jit(solution)/shard_map/all_to_all | solution.py:13
  120.9 1.1 broadcast_in_dim.111
  122.0 0.1 copy-done.3
  122.2 3.5 %all-to-all-start.5 = ((bf16[4,224,512]{2,1,0:T(8,128)(2,1)}), bf16[4,224,512]{2,1,0:T(8,128)(2,1)S(1)}, u32[]{:S(2)}, u32[]{:S(2)}) async-start(bf16[4,224,512]{2,1,0:T(8,128)(2,1)} %broadcast_in_dim.111), calls=%async_computation.5 | async-start | bytes 1835008 | tf_op jit(solution)/shard_map/all_to_all | solution.py:13
  125.8 10.0 %all-to-all-done.5 = bf16[4,224,512]{2,1,0:T(8,128)(2,1)S(1)} async-done(((bf16[4,224,512]{2,1,0:T(8,128)(2,1)}), bf16[4,224,512]{2,1,0:T(8,128)(2,1)S(1)}, u32[]{:S(2)}, u32[]{:S(2)}) %all-to-all-start.5) | async-done | bytes 917536 | tf_op jit(solution)/shard_map/all_to_all | solution.py:13
  135.8 0.9 broadcast_in_dim.117
  136.7 4.3 %all-to-all-start.12 = ((bf16[8,96,512]{2,1,0:T(8,128)(2,1)}), bf16[8,96,512]{2,1,0:T(8,128)(2,1)}, u32[]{:S(2)}, u32[]{:S(2)}) async-start(bf16[8,96,512]{2,1,0:T(8,128)(2,1)} %broadcast_in_dim.117), calls=%async_computation.12 | async-start | bytes 1572864 | tf_op jit(solution)/shard_map/all_to_all | solution.py:13
  141.1 0.2 convolution_convert_fusion.5
  141.3 1.2 fusion.5
  142.6 18.8 %all-to-all-done.12 = bf16[8,96,512]{2,1,0:T(8,128)(2,1)} async-done(((bf16[8,96,512]{2,1,0:T(8,128)(2,1)}), bf16[8,96,512]{2,1,0:T(8,128)(2,1)}, u32[]{:S(2)}, u32[]{:S(2)}) %all-to-all-start.12) | async-done | bytes 786464 | tf_op jit(solution)/shard_map/all_to_all | solution.py:13
  161.4 22.5 %all_to_all.71 = bf16[8,104,512]{2,1,0:T(8,128)(2,1)S(1)} all-to-all(bf16[8,104,512]{2,1,0:T(8,128)(2,1)S(1)} %fusion.16), channel_id=1, replica_groups=mesh['dp_0'=4,'dp_1'=8,'expert'=16] {'dp_1'}, dimensions={0} | all-to-all | bytes 1703936 | tf_op jit(solution)/shard_map/all_to_all | solution.py:13
  183.9 1.0 broadcast_in_dim.115
  184.9 3.5 %all-to-all-start.10 = ((bf16[4,224,512]{2,1,0:T(8,128)(2,1)}), bf16[4,224,512]{2,1,0:T(8,128)(2,1)S(1)}, u32[]{:S(2)}, u32[]{:S(2)}) async-start(bf16[4,224,512]{2,1,0:T(8,128)(2,1)} %broadcast_in_dim.115), calls=%async_computation.10 | async-start | bytes 1835008 | tf_op jit(solution)/shard_map/all_to_all | solution.py:13
  188.6 0.7 fusion.41
  189.2 8.2 %all-to-all-done.10 = bf16[4,224,512]{2,1,0:T(8,128)(2,1)S(1)} async-done(((bf16[4,224,512]{2,1,0:T(8,128)(2,1)}), bf16[4,224,512]{2,1,0:T(8,128)(2,1)S(1)}, u32[]{:S(2)}, u32[]{:S(2)}) %all-to-all-start.10) | async-done | bytes 917536 | tf_op jit(solution)/shard_map/all_to_all | solution.py:13
  197.4 3.3 %all-to-all-start.8 = ((bf16[4,32,512]{2,1,0:T(8,128)(2,1)}), bf16[4,32,512]{2,1,0:T(8,128)(2,1)S(1)}, u32[]{:S(2)}, u32[]{:S(2)}) async-start(bf16[4,32,512]{2,1,0:T(8,128)(2,1)} %fusion.41), calls=%async_computation.8 | async-start | bytes 262144 | tf_op jit(solution)/shard_map/all_to_all | solution.py:13
  200.7 2.6 %convolution_convert_fusion.1 = bf16[896,512]{1,0:T(8,128)(2,1)} fusion(bf16[512,512]{1,0:T(8,128)(2,1)} %copy-done.18, bf16[896,512]{1,0:T(8,128)(2,1)S(1)} %bitcast.148, f32[512]{0:T(512)S(1)} %fusion.11), kind=kOutput, calls=%fused_computation.11 | convolution fusion | flops 471597056 | bytes 2361344 | tf_op jit(solution)/shard_map/dot_general | solution.py:22
  203.3 2.2 all-to-all-done.8
  205.5 3.6 %all-to-all-start.11 = ((bf16[4,224,512]{2,1,0:T(8,128)(2,1)}), bf16[4,224,512]{2,1,0:T(8,128)(2,1)S(1)}, u32[]{:S(2)}, u32[]{:S(2)}) async-start(bf16[4,224,512]{2,1,0:T(8,128)(2,1)} %bitcast.34), calls=%async_computation.11 | async-start | bytes 1835008 | tf_op jit(solution)/shard_map/all_to_all | solution.py:13
  209.2 3.2 %convolution_convert_fusion = bf16[896,512]{1,0:T(8,128)(2,1)} fusion(bf16[896,512]{1,0:T(8,128)(2,1)S(1)} %bitcast.147, bf16[768,512]{1,0:T(8,128)(2,1)} %bitcast.38, s32[512]{0:T(512)S(1)} %bitcast.175), kind=kOutput, calls=%fused_computation.10 | convolution fusion | flops 873529344 | bytes 2623488 | tf_op jit(solution)/shard_map/dot_general | solution.py:22
  212.4 0.2 convolution_reduce_fusion
  212.6 5.5 %all-to-all-done.11 = bf16[4,224,512]{2,1,0:T(8,128)(2,1)S(1)} async-done(((bf16[4,224,512]{2,1,0:T(8,128)(2,1)}), bf16[4,224,512]{2,1,0:T(8,128)(2,1)S(1)}, u32[]{:S(2)}, u32[]{:S(2)}) %all-to-all-start.11) | async-done | bytes 917536 | tf_op jit(solution)/shard_map/all_to_all | solution.py:13
  218.2 3.5 %all-to-all-start.13 = ((bf16[4,224,512]{2,1,0:T(8,128)(2,1)}), bf16[4,224,512]{2,1,0:T(8,128)(2,1)S(1)}, u32[]{:S(2)}, u32[]{:S(2)}) async-start(bf16[4,224,512]{2,1,0:T(8,128)(2,1)} %bitcast.39), calls=%async_computation.13 | async-start | bytes 1835008 | tf_op jit(solution)/shard_map/all_to_all | solution.py:13
  221.8 0.7 pad_maximum_fusion.2
  222.5 8.8 %all-to-all-done.13 = bf16[4,224,512]{2,1,0:T(8,128)(2,1)S(1)} async-done(((bf16[4,224,512]{2,1,0:T(8,128)(2,1)}), bf16[4,224,512]{2,1,0:T(8,128)(2,1)S(1)}, u32[]{:S(2)}, u32[]{:S(2)}) %all-to-all-start.13) | async-done | bytes 917536 | tf_op jit(solution)/shard_map/all_to_all | solution.py:13
  231.3 14.0 %all-to-all-start.9 = ((bf16[16,32,128]{2,1,0:T(8,128)(2,1)}), bf16[16,32,128]{2,1,0:T(8,128)(2,1)}, u32[]{:S(2)}, u32[]{:S(2)}) async-start(bf16[16,32,128]{2,1,0:T(8,128)(2,1)} %pad_maximum_fusion.2), calls=%async_computation.9 | async-start | bytes 262144 | tf_op jit(solution)/shard_map/all_to_all | solution.py:13
  245.3 0.9 fusion.39
  246.2 0.7 copy.47
  246.9 1.6 broadcast_in_dim_reshape.7
  248.5 0.7 copy.49
  249.2 1.6 broadcast_in_dim_reshape.8
  250.8 3.7 %all-to-all-done.9 = bf16[16,32,128]{2,1,0:T(8,128)(2,1)} async-done(((bf16[16,32,128]{2,1,0:T(8,128)(2,1)}), bf16[16,32,128]{2,1,0:T(8,128)(2,1)}, u32[]{:S(2)}, u32[]{:S(2)}) %all-to-all-start.9) | async-done | bytes 131104 | tf_op jit(solution)/shard_map/all_to_all | solution.py:13
  254.6 0.8 convert_reduce_fusion.2
  255.4 0.6 subtract_multiply_fusion
  256.0 2.0 fusion.10
  (81 shorter events, 1.5 us)
Async XLA Ops:
  0.6 2.7 %copy-start = (bf16[256,128]{1,0:T(8,128)(2,1)S(1)}, bf16[256,128]{1,0:T(8,128)(2,1)}, u32[]{:S(2)}) copy-start(bf16[256,128]{1,0:T(8,128)(2,1)} %param.9) | copy-start | bytes 196612
  1.6 15.7 %copy-start.13 = (f32[1,256]{1,0:T(1,128)S(1)}, f32[1,256]{1,0:T(1,128)}, u32[]{:S(2)}) copy-start(f32[1,256]{1,0:T(1,128)} %param.10) | copy-start | bytes 3076
  3.0 14.3 %copy-start.11 = (s32[16,32]{1,0:T(8,128)}, s32[16,32]{1,0:T(8,128)S(1)}, u32[]{:S(2)}) copy-start(s32[16,32]{1,0:T(8,128)S(1)} %get-tuple-element.12) | copy-start | bytes 6148
  5.4 22.0 %all-to-all-start = ((bf16[16,48,128]{2,1,0:T(8,128)(2,1)}), bf16[16,48,128]{2,1,0:T(8,128)(2,1)S(1)}, u32[]{:S(2)}, u32[]{:S(2)}) async-start(bf16[16,48,128]{2,1,0:T(8,128)(2,1)} %pad_maximum_fusion.1), calls=%async_computation | async-start | bytes 393216 | tf_op jit(solution)/shard_map/all_to_all | solution.py:13
  17.3 21.1 %copy-start.16 = (s32[128]{0:T(128)}, s32[128]{0:T(128)S(1)}, u32[]{:S(2)}) copy-start(s32[128]{0:T(128)S(1)} %pad.24) | copy-start | bytes 1540
  39.4 7.0 %copy-start.1 = (bf16[1,224,2048]{2,1,0:T(8,128)(2,1)S(1)}, bf16[1,224,2048]{2,1,0:T(8,128)(2,1)}, u32[]{:S(2)}) copy-start(bf16[1,224,2048]{2,1,0:T(8,128)(2,1)} %param.14) | copy-start | bytes 2752516
  39.4 31.9 %all-to-all-start.2 = ((bf16[8,104,512]{2,1,0:T(8,128)(2,1)}), bf16[8,104,512]{2,1,0:T(8,128)(2,1)S(1)}, u32[]{:S(2)}, u32[]{:S(2)}) async-start(bf16[8,104,512]{2,1,0:T(8,128)(2,1)} %broadcast_in_dim.109), calls=%async_computation.2 | async-start | bytes 1703936 | tf_op jit(solution)/shard_map/all_to_all | solution.py:13
  71.3 3.6 %copy-start.9 = (bf16[8,104,512]{2,1,0:T(8,128)(2,1)}, bf16[8,104,512]{2,1,0:T(8,128)(2,1)S(1)}, u32[]{:S(2)}) copy-start(bf16[8,104,512]{2,1,0:T(8,128)(2,1)S(1)} %all-to-all-done.2) | copy-start | bytes 2555908
  71.3 16.8 %all-to-all-start.3 = ((bf16[4,224,512]{2,1,0:T(8,128)(2,1)}), bf16[4,224,512]{2,1,0:T(8,128)(2,1)S(1)}, u32[]{:S(2)}, u32[]{:S(2)}) async-start(bf16[4,224,512]{2,1,0:T(8,128)(2,1)} %copy.43), calls=%async_computation.3 | async-start | bytes 1835008 | tf_op jit(solution)/shard_map/all_to_all | solution.py:13
  74.8 66.4 %copy-start.14 = (s32[1,512]{1,0:T(1,128)}, s32[1,512]{1,0:T(1,128)S(1)}, u32[]{:S(2)}) copy-start(s32[1,512]{1,0:T(1,128)S(1)} %get-tuple-element.7) | copy-start | bytes 6148
  75.6 14.5 %copy-start.18 = (bf16[512,512]{1,0:T(8,128)(2,1)}, bf16[512,512]{1,0:T(8,128)(2,1)S(1)}, u32[]{:S(2)}) copy-start(bf16[512,512]{1,0:T(8,128)(2,1)S(1)} %fusion.9) | copy-start | bytes 1572868
  90.1 3.7 %copy-start.2 = (bf16[1,224,2048]{2,1,0:T(8,128)(2,1)S(1)}, bf16[1,224,2048]{2,1,0:T(8,128)(2,1)}, u32[]{:S(2)}) copy-start(bf16[1,224,2048]{2,1,0:T(8,128)(2,1)} %param.15) | copy-start | bytes 2752516
  90.1 16.1 %all-to-all-start.4 = ((bf16[4,224,512]{2,1,0:T(8,128)(2,1)}), bf16[4,224,512]{2,1,0:T(8,128)(2,1)S(1)}, u32[]{:S(2)}, u32[]{:S(2)}) async-start(bf16[4,224,512]{2,1,0:T(8,128)(2,1)} %bitcast.17), calls=%async_computation.4 | async-start | bytes 1835008 | tf_op jit(solution)/shard_map/all_to_all | solution.py:13
  106.2 14.8 %all-to-all-start.6 = ((bf16[4,224,512]{2,1,0:T(8,128)(2,1)}), bf16[4,224,512]{2,1,0:T(8,128)(2,1)S(1)}, u32[]{:S(2)}, u32[]{:S(2)}) async-start(bf16[4,224,512]{2,1,0:T(8,128)(2,1)} %bitcast.140), calls=%async_computation.6 | async-start | bytes 1835008 | tf_op jit(solution)/shard_map/all_to_all | solution.py:13
  109.7 1.1 copy-start.5
  109.7 1.1 copy-start.6
  120.9 1.2 copy-start.3
  122.0 3.7 %copy-start.10 = (bf16[4,24,4,128]{3,1,2,0:T(8,128)(2,1)S(1)}, bf16[4,24,4,128]{3,1,2,0:T(8,128)(2,1)}, u32[]{:S(2)}) copy-start(bf16[4,24,4,128]{3,1,2,0:T(8,128)(2,1)} %get-tuple-element.17) | copy-start | bytes 294916
  122.2 13.6 %all-to-all-start.5 = ((bf16[4,224,512]{2,1,0:T(8,128)(2,1)}), bf16[4,224,512]{2,1,0:T(8,128)(2,1)S(1)}, u32[]{:S(2)}, u32[]{:S(2)}) async-start(bf16[4,224,512]{2,1,0:T(8,128)(2,1)} %broadcast_in_dim.111), calls=%async_computation.5 | async-start | bytes 1835008 | tf_op jit(solution)/shard_map/all_to_all | solution.py:13
  136.7 4.5 %copy-start.4 = (bf16[4,224,512]{2,1,0:T(8,128)(2,1)S(1)}, bf16[4,224,512]{2,1,0:T(8,128)(2,1)}, u32[]{:S(2)}) copy-start(bf16[4,224,512]{2,1,0:T(8,128)(2,1)} %copy-done.3) | copy-start | bytes 2752516
  136.7 24.6 %all-to-all-start.12 = ((bf16[8,96,512]{2,1,0:T(8,128)(2,1)}), bf16[8,96,512]{2,1,0:T(8,128)(2,1)}, u32[]{:S(2)}, u32[]{:S(2)}) async-start(bf16[8,96,512]{2,1,0:T(8,128)(2,1)} %broadcast_in_dim.117), calls=%async_computation.12 | async-start | bytes 1572864 | tf_op jit(solution)/shard_map/all_to_all | solution.py:13
  161.4 22.5 %copy-start.8 = (bf16[224,512]{1,0:T(8,128)(2,1)S(1)}, bf16[224,512]{1,0:T(8,128)(2,1)}, u32[]{:S(2)}) copy-start(bf16[224,512]{1,0:T(8,128)(2,1)} %get-tuple-element.16) | copy-start | bytes 688132
  184.9 12.5 %all-to-all-start.10 = ((bf16[4,224,512]{2,1,0:T(8,128)(2,1)}), bf16[4,224,512]{2,1,0:T(8,128)(2,1)S(1)}, u32[]{:S(2)}, u32[]{:S(2)}) async-start(bf16[4,224,512]{2,1,0:T(8,128)(2,1)} %broadcast_in_dim.115), calls=%async_computation.10 | async-start | bytes 1835008 | tf_op jit(solution)/shard_map/all_to_all | solution.py:13
  197.4 8.1 %all-to-all-start.8 = ((bf16[4,32,512]{2,1,0:T(8,128)(2,1)}), bf16[4,32,512]{2,1,0:T(8,128)(2,1)S(1)}, u32[]{:S(2)}, u32[]{:S(2)}) async-start(bf16[4,32,512]{2,1,0:T(8,128)(2,1)} %fusion.41), calls=%async_computation.8 | async-start | bytes 262144 | tf_op jit(solution)/shard_map/all_to_all | solution.py:13
  205.5 3.6 %copy-start.15 = (s32[1,512]{1,0:T(1,128)S(1)}, s32[1,512]{1,0:T(1,128)}, u32[]{:S(2)}) copy-start(s32[1,512]{1,0:T(1,128)} %copy-done.14) | copy-start | bytes 6148
  205.5 12.7 %all-to-all-start.11 = ((bf16[4,224,512]{2,1,0:T(8,128)(2,1)}), bf16[4,224,512]{2,1,0:T(8,128)(2,1)S(1)}, u32[]{:S(2)}, u32[]{:S(2)}) async-start(bf16[4,224,512]{2,1,0:T(8,128)(2,1)} %bitcast.34), calls=%async_computation.11 | async-start | bytes 1835008 | tf_op jit(solution)/shard_map/all_to_all | solution.py:13
  209.2 3.2 %copy-start.17 = (s32[128]{0:T(128)S(1)}, s32[128]{0:T(128)}, u32[]{:S(2)}) copy-start(s32[128]{0:T(128)} %copy-done.16) | copy-start | bytes 1540
  218.2 13.1 %all-to-all-start.13 = ((bf16[4,224,512]{2,1,0:T(8,128)(2,1)}), bf16[4,224,512]{2,1,0:T(8,128)(2,1)S(1)}, u32[]{:S(2)}, u32[]{:S(2)}) async-start(bf16[4,224,512]{2,1,0:T(8,128)(2,1)} %bitcast.39), calls=%async_computation.13 | async-start | bytes 1835008 | tf_op jit(solution)/shard_map/all_to_all | solution.py:13
  221.7 23.6 %copy-start.7 = (bf16[1,512,224]{1,2,0:T(8,128)(2,1)S(1)}, bf16[1,512,224]{1,2,0:T(8,128)(2,1)}, u32[]{:S(2)}) copy-start(bf16[1,512,224]{1,2,0:T(8,128)(2,1)} %param.13) | copy-start | bytes 688132
  231.3 23.2 %all-to-all-start.9 = ((bf16[16,32,128]{2,1,0:T(8,128)(2,1)}), bf16[16,32,128]{2,1,0:T(8,128)(2,1)}, u32[]{:S(2)}, u32[]{:S(2)}) async-start(bf16[16,32,128]{2,1,0:T(8,128)(2,1)} %pad_maximum_fusion.2), calls=%async_computation.9 | async-start | bytes 262144 | tf_op jit(solution)/shard_map/all_to_all | solution.py:13
  249.2 6.8 %copy-start.12 = (s32[16,32]{1,0:T(8,128)S(1)}, s32[16,32]{1,0:T(8,128)}, u32[]{:S(2)}) copy-start(s32[16,32]{1,0:T(8,128)} %copy-done.11) | copy-start | bytes 6148

commit v2 on v1

--- a/solution.py
+++ b/solution.py
@@ -4,6 +4,7 @@
 from jax.sharding import Mesh
 from jax.sharding import PartitionSpec as P
 
+
 X, Y, E = "dp_0", "dp_1", "expert"
 BF, F32 = jnp.bfloat16, jnp.float32
 PAD = 8
@@ -34,15 +35,23 @@
     return lax.broadcasted_iota(jnp.int32, (n, m), 1)
 
 
-def features_to_x(w, nx):
-    units, width = w.shape
-    parts = w.reshape(units, nx, width // nx).transpose(1, 0, 2)
-    return exchange(parts, X).reshape(nx * units, width // nx)
-
-
-def features_home(g, nx):
-    parts = exchange(g.reshape(nx, g.shape[0] // nx, g.shape[1]), X)
-    return parts.transpose(1, 0, 2).reshape(parts.shape[1], -1)
+def shift(x, by):
+    size = lax.axis_size(X)
+    return lax.ppermute(x, X, [(i, (i + by) % size) for i in range(size)])
+
+
+def quarter_at(w, index, nx):
+    return lax.dynamic_slice_in_dim(w, index * (w.shape[1] // nx), w.shape[1] // nx, axis=1)
+
+
+def in_turn(parts, xi):
+    size = len(parts)
+    stacked = jnp.stack(parts)
+    picked = [
+        lax.dynamic_index_in_dim(stacked, (q + size - xi) % size, 0, keepdims=False)
+        for q in range(size)
+    ]
+    return jnp.concatenate(picked, axis=1)
 
 
 def local(grad_out, saved_inputs, router_probs, chosen, gate_pre, up_pre, w_down, w_up):
@@ -77,8 +86,11 @@
     sent = jnp.concatenate([sent_grad[:, :cap], sent_input[:, :cap]], axis=1)
     rows = exchange(sent, E).reshape(nx, quarter, 2 * cap, width_dev)
 
-    down_part = features_to_x(w_down[0], nx)
-    up_part = features_to_x(w_up[0], nx)
+    down_mine = [quarter_at(w_down[0], (xi + k) % nx, nx) for k in range(nx)]
+    up_mine = [quarter_at(w_up[0], (xi + k) % nx, nx) for k in range(nx)]
+    down_part = jnp.concatenate(
+        [down_mine[0]] + [shift(down_mine[k], k) for k in range(1, nx)], axis=0
+    )
 
     own_rows = lax.dynamic_index_in_dim(local_rows, ei, 0, keepdims=False)
     own_rows = jnp.pad(own_rows, (0, lane - cap - PAD), constant_values=-1)
@@ -88,12 +100,26 @@
         jnp.pad(gate_row, ((0, PAD - 1), (0, 0)))[None, None], (nx, quarter, PAD, lane)
     )
     rows = exchange(jnp.concatenate([rows, gate_tile], axis=2), X)
+    gate_value = gate_pre[0].T.astype(F32)
+    up_value = up_pre[0].T.astype(F32)
+    sig = jax.nn.sigmoid(gate_value)
+    active = gate_value * sig
+    hidden = active * up_value
+    hidden_own = hidden.astype(BF)
+    up_mine, hidden_own, rows, down_part = lax.optimization_barrier(
+        (up_mine, hidden_own, rows, down_part)
+    )
+    pairs = [
+        shift(jnp.concatenate([up_mine[k], hidden_own], axis=0), k) for k in range(1, nx)
+    ]
+    up_part = jnp.concatenate([up_mine[0]] + [p[:units] for p in pairs], axis=0)
+    hidden_all = jnp.concatenate([hidden_own] + [p[units:] for p in pairs], axis=0)
+
     grads = rows[:, :, :cap].transpose(0, 2, 1, 3).reshape(nx * cap, part)
     inputs = rows[:, :, cap : 2 * cap].transpose(0, 2, 1, 3).reshape(nx * cap, part)
     gates = jnp.pad(rows[:, 0, 2 * cap], ((0, PAD - nx), (0, part - lane)))
     block = nx * cap + PAD
     grads_all = to_all(jnp.concatenate([grads, gates], axis=0), Y)
-    inputs_all = to_all(inputs, Y)
 
     chosen_row = lax.dynamic_index_in_dim(chosen, ei, 0, keepdims=True)
     owner = chosen_row // tok_dev
@@ -109,25 +135,24 @@
     owner_hit = rows_of(shards, slots) == owner_y * nx + owner_x
     within_hit = onehot(rows_of(lane, slots) == within)
 
-    gate_value = gate_pre[0].T.astype(F32)
-    up_value = up_pre[0].T.astype(F32)
-    sig = jax.nn.sigmoid(gate_value)
-    active = gate_value * sig
-    hidden = active * up_value
-    hidden_all = to_all(hidden.astype(BF), X).reshape(nx * units, slots)
-
+    grads_all, up_part, hidden_all = lax.optimization_barrier((grads_all, up_part, hidden_all))
     grads_slots = dot(place_block, grads_all.reshape(ny * block, part), 0, 0).astype(BF)
     gates_all = grads_all[:, nx * cap : nx * cap + nx, :lane].reshape(shards, lane)
     gate_slot = jnp.sum(
         jnp.where(owner_hit, dot(gates_all, within_hit, 1, 0), 0.0), axis=0, keepdims=True
     )
     raw_part = dot(down_part, grads_slots, 1, 1).astype(BF).reshape(nx, units, slots)
-    raw_grad = jnp.sum(exchange(raw_part, X).astype(F32), axis=0)
+    inputs, raw_part = lax.optimization_barrier((inputs, raw_part))
+    inputs_all = to_all(inputs, Y)
+    raw_came = [shift(raw_part[k], -k) for k in range(1, nx)]
+    raw_grad = raw_part[0].astype(F32)
+    for came in raw_came:
+        raw_grad = raw_grad + came.astype(F32)
     dots = jnp.sum(hidden * raw_grad, axis=0, keepdims=True)
     hid_grad = gate_slot * raw_grad
     up_grad = (hid_grad * active).astype(BF)
     gate_grad = (hid_grad * up_value * sig * (1.0 + gate_value * (1.0 - sig))).astype(BF)
-    up_all = to_all(up_grad, X).reshape(nx * units, slots)
+    up_all = jnp.concatenate([up_grad] + [shift(up_grad, k) for k in range(1, nx)], axis=0)
 
     dx = dot(up_all, up_part, 0, 0).astype(BF)
     dx_rows = dot(place_rows, dx, 1, 0).astype(BF).reshape(ny, nx * cap, part)
@@ -162,8 +187,12 @@
     grad_down = dot(hidden_gated, grads_slots, 1, 0).astype(BF)
     inputs_slots = dot(place_rows, inputs_all.reshape(-1, part), 0, 0).astype(BF)
     grad_up = dot(up_all, inputs_slots, 1, 0).astype(BF)
-    grad_down = features_home(grad_down, nx)
-    grad_up = features_home(grad_up, nx)
+    both = jnp.concatenate(
+        [grad_down.reshape(nx, units, part), grad_up.reshape(nx, units, part)], axis=1
+    )
+    home = [both[0]] + [shift(both[k], -k) for k in range(1, nx)]
+    grad_down = in_turn([h[:units] for h in home], xi)
+    grad_up = in_turn([h[units:] for h in home], xi)
     return grad_tokens, grad_logits, grad_down[None], grad_up[None], gate_grad.T[None]
 
 

time: 259 us -> 203 us (0.78)
  waiting for transfers between devices: 122 us -> 73.8 us
  blocking collectives: 32.7 us -> 0 us
  starting transfers between devices: 65.2 us -> 91.7 us
  local copies, waits for them, and re-layouts: 15.6 us -> 7.5 us
  other arithmetic: 8.94 us -> 15.5 us
    all_to_all x12 -> x7, waiting for transfers between devices: 122 us -> 12.6 us  [exchange(): return lax.all_to_all(x, axis, 0, 0, tiled=True)]
    ppermute x0 -> x15, waiting for transfers between devices: none -> 61.2 us  [shift(): return lax.ppermute(x, X, [(i, (i + by) % size) for i in range(size)])]
    ppermute x0 -> x15, starting transfers between devices: none -> 43.2 us  [shift(): return lax.ppermute(x, X, [(i, (i + by) % size) for i in range(size)])]
    all_to_all x2 -> x0, blocking collectives: 32.7 us -> none  [exchange(): return lax.all_to_all(x, axis, 0, 0, tiled=True)]
    all_to_all x12 -> x7, starting transfers between devices: 65.2 us -> 48.5 us  [exchange(): return lax.all_to_all(x, axis, 0, 0, tiled=True)]
    another operation x5 -> x3, local copies, waits for them, and re-layouts: 5.63 us -> 1.14 us  [in_turn(): stacked = jnp.stack(parts)]
  transfers between devices with their start and end apart: 12 -> 22, of which waited for: 12 -> 13; matrix products, arithmetic and copies ran while one was open for 9% -> 8% of each run, Pallas kernels for 0% -> 0%
where the time goes in v2:
time: 203 us; the launch traced here: 201 us
  starting transfers between devices  91.7 us (45%)
  waiting for transfers between devices  73.8 us (36%)
  other arithmetic  15.5 us (8%)
  matrix products  11.6 us (6%)
  local copies, waits for them, and re-layouts  7.5 us (4%)
    ppermute x15, waiting for transfers between devices, shift(): return lax.ppermute(x, X, [(i, (i + by) % size) for i in range(size)])  61.2 us
    all_to_all x7, starting transfers between devices, exchange(): return lax.all_to_all(x, axis, 0, 0, tiled=True)  48.5 us
    ppermute x15, starting transfers between devices, shift(): return lax.ppermute(x, X, [(i, (i + by) % size) for i in range(size)])  43.2 us
    all_to_all x7, waiting for transfers between devices, exchange(): return lax.all_to_all(x, axis, 0, 0, tiled=True)  12.6 us
    dot_general x12, matrix products, dot(): lax.dot_general(a, b, (((ca,), (cb,)), ((), ())), preferred_element_type=...  11.6 us
  transfers between devices with their start and end apart: 22, of which 13 were waited for; matrix products, arithmetic and copies ran while one was open for 8% of the time, Pallas kernels for 0%

profile of v2, /device:TPU:1, one launch (start us, length us, event | category | flops | bytes accessed | tf_op | source)
XLA Modules:
  0.0 201.3 jit_solution(9628883081696479109)
XLA Ops:
  0.7 0.9 convert_reduce_fusion.2
  1.6 1.2 select_reduce_fusion
  3.3 0.3 convolution_convert_fusion.4
  3.6 1.1 convolution_convert_fusion.5
  4.7 0.7 pad_maximum_fusion.11
  5.4 11.8 %all-to-all-start = ((bf16[16,48,128]{2,1,0:T(8,128)(2,1)}), bf16[16,48,128]{2,1,0:T(8,128)(2,1)S(1)}, u32[]{:S(2)}, u32[]{:S(2)}) async-start(bf16[16,48,128]{2,1,0:T(8,128)(2,1)} %pad_maximum_fusion.11), calls=%async_computation | async-start | bytes 393216 | tf_op jit(solution)/shard_map/all_to_all | solution.py:14
  17.3 0.9 dynamic-slice_bitcast_fusion.11
  18.1 4.4 %collective-permute-start.2 = (bf16[224,512]{1,0:T(8,128)(2,1)}, bf16[224,512]{1,0:T(8,128)(2,1)S(1)}, u32[]{:S(2)}, u32[]{:S(2)}) collective-permute-start(bf16[224,512]{1,0:T(8,128)(2,1)} %get-tuple-element.57), channel_id=1, source_target_pairs={{0,384},{128,0},{256,128},{384,256},{1,385},{129,1},{257,129},{385... | collective-permute-start | bytes 688136 | tf_op jit(solution)/shard_map/ppermute | solution.py:40
  22.5 2.4 %collective-permute-start.1 = (bf16[224,512]{1,0:T(8,128)(2,1)}, bf16[224,512]{1,0:T(8,128)(2,1)S(1)}, u32[]{:S(2)}, u32[]{:S(2)}) collective-permute-start(bf16[224,512]{1,0:T(8,128)(2,1)} %get-tuple-element.58), channel_id=1, source_target_pairs={{0,256},{128,384},{256,0},{384,128},{1,257},{129,385},{257,1},{385... | collective-permute-start | bytes 688136 | tf_op jit(solution)/shard_map/ppermute | solution.py:40
  25.0 2.5 %collective-permute-start = (bf16[224,512]{1,0:T(8,128)(2,1)}, bf16[224,512]{1,0:T(8,128)(2,1)}, u32[]{:S(2)}, u32[]{:S(2)}) collective-permute-start(bf16[224,512]{1,0:T(8,128)(2,1)} %get-tuple-element.56), channel_id=1, source_target_pairs={{0,128},{128,256},{256,384},{384,0},{1,129},{129,257},{257,385},{3... | collective-permute-start | bytes 688136 | tf_op jit(solution)/shard_map/ppermute | solution.py:40
  27.5 0.7 compare_select_fusion.1
  28.6 0.8 copy-done.5
  29.7 0.7 pad_maximum_fusion.10
  30.4 3.4 %all-to-all-start.1 = ((bf16[4,4,56,128]{3,2,1,0:T(8,128)(2,1)}), bf16[4,4,56,128]{3,2,1,0:T(8,128)(2,1)S(1)}, u32[]{:S(2)}, u32[]{:S(2)}) async-start(bf16[4,4,56,128]{3,2,1,0:T(8,128)(2,1)} %pad_maximum_fusion.10), calls=%async_computation.1 | async-start | bytes 458752 | tf_op jit(solution)/shard_map/all_to_all | solution.py:14
  34.0 4.7 %collective-permute-done = bf16[224,512]{1,0:T(8,128)(2,1)} collective-permute-done((bf16[224,512]{1,0:T(8,128)(2,1)}, bf16[224,512]{1,0:T(8,128)(2,1)}, u32[]{:S(2)}, u32[]{:S(2)}) %collective-permute-start) | collective-permute-done | bytes 229408 | tf_op jit(solution)/shard_map/ppermute | solution.py:40
  38.7 1.9 pad_maximum_fusion
  40.7 1.0 broadcast_in_dim.102
  41.7 6.8 %all-to-all-start.2 = ((bf16[8,104,512]{2,1,0:T(8,128)(2,1)}), bf16[8,104,512]{2,1,0:T(8,128)(2,1)}, u32[]{:S(2)}, u32[]{:S(2)}) async-start(bf16[8,104,512]{2,1,0:T(8,128)(2,1)} %broadcast_in_dim.102), calls=%async_computation.2 | async-start | bytes 1703936 | tf_op jit(solution)/shard_map/all_to_all | solution.py:14
  48.6 1.9 collective-permute-start.5
  50.7 2.5 %collective-permute-start.4 = (bf16[448,512]{1,0:T(8,128)(2,1)S(1)}, bf16[448,512]{1,0:T(8,128)(2,1)S(1)}, u32[]{:S(2)}, u32[]{:S(2)}) collective-permute-start(bf16[448,512]{1,0:T(8,128)(2,1)S(1)} %get-tuple-element.76), channel_id=1, source_target_pairs={{0,256},{128,384},{256,0},{384,128},{1,257},{129,385},{257,1},{385... | collective-permute-start | bytes 1376264 | tf_op jit(solution)/shard_map/ppermute | solution.py:40
  53.2 2.8 %collective-permute-start.3 = (bf16[448,512]{1,0:T(8,128)(2,1)S(1)}, bf16[448,512]{1,0:T(8,128)(2,1)S(1)}, u32[]{:S(2)}, u32[]{:S(2)}) collective-permute-start(bf16[448,512]{1,0:T(8,128)(2,1)S(1)} %get-tuple-element.75), channel_id=1, source_target_pairs={{0,128},{128,256},{256,384},{384,0},{1,129},{129,257},{257,385},{3... | collective-permute-start | bytes 1376264 | tf_op jit(solution)/shard_map/ppermute | solution.py:40
  56.1 5.4 %collective-permute-done.5 = bf16[448,512]{1,0:T(8,128)(2,1)S(1)} collective-permute-done((bf16[448,512]{1,0:T(8,128)(2,1)S(1)}, bf16[448,512]{1,0:T(8,128)(2,1)S(1)}, u32[]{:S(2)}, u32[]{:S(2)}) %collective-permute-start.5) | collective-permute-done | bytes 458784 | tf_op jit(solution)/shard_map/ppermute | solution.py:40
  61.5 2.4 %collective-permute-done.4 = bf16[448,512]{1,0:T(8,128)(2,1)S(1)} collective-permute-done((bf16[448,512]{1,0:T(8,128)(2,1)S(1)}, bf16[448,512]{1,0:T(8,128)(2,1)S(1)}, u32[]{:S(2)}, u32[]{:S(2)}) %collective-permute-start.4) | collective-permute-done | bytes 458784 | tf_op jit(solution)/shard_map/ppermute | solution.py:40
  63.9 12.4 %collective-permute-done.3 = bf16[448,512]{1,0:T(8,128)(2,1)S(1)} collective-permute-done((bf16[448,512]{1,0:T(8,128)(2,1)S(1)}, bf16[448,512]{1,0:T(8,128)(2,1)S(1)}, u32[]{:S(2)}, u32[]{:S(2)}) %collective-permute-start.3) | collective-permute-done | bytes 458784 | tf_op jit(solution)/shard_map/ppermute | solution.py:40
  76.5 2.0 fusion.6
  78.5 0.7 convolution_convert_fusion.2
  79.3 1.0 broadcast_in_dim.107
  80.3 6.6 %all-to-all-start.6 = ((bf16[8,96,512]{2,1,0:T(8,128)(2,1)}), bf16[8,96,512]{2,1,0:T(8,128)(2,1)}, u32[]{:S(2)}, u32[]{:S(2)}) async-start(bf16[8,96,512]{2,1,0:T(8,128)(2,1)} %broadcast_in_dim.107), calls=%async_computation.6 | async-start | bytes 1572864 | tf_op jit(solution)/shard_map/all_to_all | solution.py:14
  87.1 0.8 slice.133
  87.9 1.9 collective-permute-start.8
  89.8 2.5 %collective-permute-start.7 = (bf16[224,512]{1,0:T(8,128)(2,1)S(1)}, bf16[224,512]{1,0:T(8,128)(2,1)S(1)}, u32[]{:S(2)}, u32[]{:S(2)}) collective-permute-start(bf16[224,512]{1,0:T(8,128)(2,1)S(1)} %get-tuple-element.54), channel_id=1, source_target_pairs={{0,256},{128,384},{256,0},{384,128},{1,257},{129,385},{257,1},{385... | collective-permute-start | bytes 688136 | tf_op jit(solution)/shard_map/ppermute | solution.py:40
  92.4 4.0 %collective-permute-start.6 = (bf16[224,512]{1,0:T(8,128)(2,1)S(1)}, bf16[224,512]{1,0:T(8,128)(2,1)S(1)}, u32[]{:S(2)}, u32[]{:S(2)}) collective-permute-start(bf16[224,512]{1,0:T(8,128)(2,1)S(1)} %get-tuple-element.52), channel_id=1, source_target_pairs={{0,384},{128,0},{256,128},{384,256},{1,385},{129,1},{257,129},{385... | collective-permute-start | bytes 688136 | tf_op jit(solution)/shard_map/ppermute | solution.py:40
  96.5 0.6 convolution_convert_fusion.1
  97.2 5.2 %collective-permute-done.8 = bf16[224,512]{1,0:T(8,128)(2,1)S(1)} collective-permute-done((bf16[224,512]{1,0:T(8,128)(2,1)S(1)}, bf16[224,512]{1,0:T(8,128)(2,1)S(1)}, u32[]{:S(2)}, u32[]{:S(2)}) %collective-permute-start.8) | collective-permute-done | bytes 229408 | tf_op jit(solution)/shard_map/ppermute | solution.py:40
  102.4 2.5 %collective-permute-done.6 = bf16[224,512]{1,0:T(8,128)(2,1)S(1)} collective-permute-done((bf16[224,512]{1,0:T(8,128)(2,1)S(1)}, bf16[224,512]{1,0:T(8,128)(2,1)S(1)}, u32[]{:S(2)}, u32[]{:S(2)}) %collective-permute-start.6) | collective-permute-done | bytes 229408 | tf_op jit(solution)/shard_map/ppermute | solution.py:40
  104.9 2.0 %fusion.37 = (bf16[1,512,224]{1,2,0:T(8,128)(2,1)}, bf16[512]{0:T(512)(128)(2,1)S(1)}, bf16[224,512]{1,0:T(8,128)(2,1)S(1)}) fusion(bf16[1,512,224]{1,2,0:T(8,128)(2,1)S(1)} %copy-done.5, bf16[1,512,224]{1,2,0:T(8,128)(2,1)S(1)} %copy-done.6, f32[512]{0:T(512)S(1)} %fusion.8, bf16[224,512]{1,0:T(8,128)(2,1)S(1)} %collective-permute-done.8, ...), kind=kLoop, calls=%fused_computation.104 | loop fusion | flops 2981376 | bytes 1838080 | tf_op jit(solution)/shard_map/broadcast_in_dim | solution.py:196
  106.9 5.4 %collective-permute-start.11 = (bf16[224,512]{1,0:T(8,128)(2,1)S(1)}, bf16[224,512]{1,0:T(8,128)(2,1)S(1)}, u32[]{:S(2)}, u32[]{:S(2)}) collective-permute-start(bf16[224,512]{1,0:T(8,128)(2,1)S(1)} %get-tuple-element.40), channel_id=1, source_target_pairs={{0,384},{128,0},{256,128},{384,256},{1,385},{129,1},{257,129},{385... | collective-permute-start | bytes 688136 | tf_op jit(solution)/shard_map/ppermute | solution.py:40
  112.4 1.9 collective-permute-start.10
  114.3 2.5 %collective-permute-start.9 = (bf16[224,512]{1,0:T(8,128)(2,1)S(1)}, bf16[224,512]{1,0:T(8,128)(2,1)S(1)}, u32[]{:S(2)}, u32[]{:S(2)}) collective-permute-start(bf16[224,512]{1,0:T(8,128)(2,1)S(1)} %get-tuple-element.40), channel_id=1, source_target_pairs={{0,128},{128,256},{256,384},{384,0},{1,129},{129,257},{257,385},{3... | collective-permute-start | bytes 688136 | tf_op jit(solution)/shard_map/ppermute | solution.py:40
  117.0 4.7 %collective-permute-done.11 = bf16[224,512]{1,0:T(8,128)(2,1)S(1)} collective-permute-done((bf16[224,512]{1,0:T(8,128)(2,1)S(1)}, bf16[224,512]{1,0:T(8,128)(2,1)S(1)}, u32[]{:S(2)}, u32[]{:S(2)}) %collective-permute-start.11) | collective-permute-done | bytes 229408 | tf_op jit(solution)/shard_map/ppermute | solution.py:40
  121.7 0.7 collective-permute-done.10
  122.4 5.8 %collective-permute-done.9 = bf16[224,512]{1,0:T(8,128)(2,1)S(1)} collective-permute-done((bf16[224,512]{1,0:T(8,128)(2,1)S(1)}, bf16[224,512]{1,0:T(8,128)(2,1)S(1)}, u32[]{:S(2)}, u32[]{:S(2)}) %collective-permute-start.9) | collective-permute-done | bytes 229408 | tf_op jit(solution)/shard_map/ppermute | solution.py:40
  128.2 0.7 copy-done.11
  128.9 2.5 %convolution_convert_fusion = bf16[896,512]{1,0:T(8,128)(2,1)S(1)} fusion(bf16[768,512]{1,0:T(8,128)(2,1)} %bitcast.43, s32[512]{0:T(512)S(1)} %bitcast.242, bf16[224,512]{1,0:T(8,128)(2,1)S(1)} %collective-permute-done.11, bf16[224,512]{1,0:T(8,128)(2,1)} %collective-permute-done.10, bf16[224,512]{1,0:T(8,128)(2,1)} %copy-done.11, ...), kind=kOutput, calls=%fused_computation.8 | convolution fusion | flops 877199360 | bytes 2623488 | tf_op jit(solution)/shard_map/dot_general | solution.py:23
  131.4 1.0 maximum_bitcast_fusion.3
  132.5 1.9 collective-permute-start.14
  134.4 2.5 %fusion.4 = bf16[768,512]{1,0:T(8,128)(2,1)S(1)} fusion(bf16[896,512]{1,0:T(8,128)(2,1)S(1)} %get-tuple-element.26, s32[512]{0:T(512)S(1)} %bitcast.243, bf16[224,512]{1,0:T(8,128)(2,1)} %copy-done.10, bf16[224,512]{1,0:T(8,128)(2,1)} %collective-permute-done.10, bf16[224,512]{1,0:T(8,128)(2,1)} %copy-done.11, bf16[224,512]{1,0:T(8,128)(2,1)} %copy-done.8), kind=kOutput, calls=%fused_computation.11 | convolution fusion | flops 877133824 | bytes 2623488 | tf_op jit(solution)/shard_map/dot_general | solution.py:23
  136.9 1.0 fusion.12
  137.9 6.4 %all-to-all-start.3 = ((bf16[8,104,512]{2,1,0:T(8,128)(2,1)}), bf16[8,104,512]{2,1,0:T(8,128)(2,1)S(1)}, u32[]{:S(2)}, u32[]{:S(2)}) async-start(bf16[8,104,512]{2,1,0:T(8,128)(2,1)} %fusion.12), calls=%async_computation.3 | async-start | bytes 1703936 | tf_op jit(solution)/shard_map/all_to_all | solution.py:14
  144.3 2.4 %collective-permute-start.13 = (bf16[448,512]{1,0:T(8,128)(2,1)S(1)}, bf16[448,512]{1,0:T(8,128)(2,1)S(1)}, u32[]{:S(2)}, u32[]{:S(2)}) collective-permute-start(bf16[448,512]{1,0:T(8,128)(2,1)S(1)} %copy-done.7), channel_id=1, source_target_pairs={{0,256},{128,384},{256,0},{384,128},{1,257},{129,385},{257,1},{385... | collective-permute-start | bytes 1376264 | tf_op jit(solution)/shard_map/ppermute | solution.py:40
  146.7 4.1 %collective-permute-start.12 = (bf16[448,512]{1,0:T(8,128)(2,1)S(1)}, bf16[448,512]{1,0:T(8,128)(2,1)S(1)}, u32[]{:S(2)}, u32[]{:S(2)}) collective-permute-start(bf16[448,512]{1,0:T(8,128)(2,1)S(1)} %get-tuple-element.41), channel_id=1, source_target_pairs={{0,384},{128,0},{256,128},{384,256},{1,385},{129,1},{257,129},{385... | collective-permute-start | bytes 1376264 | tf_op jit(solution)/shard_map/ppermute | solution.py:40
  150.8 1.1 slice_bitcast_fusion
  151.9 7.1 %collective-permute-done.13 = bf16[448,512]{1,0:T(8,128)(2,1)S(1)} collective-permute-done((bf16[448,512]{1,0:T(8,128)(2,1)S(1)}, bf16[448,512]{1,0:T(8,128)(2,1)S(1)}, u32[]{:S(2)}, u32[]{:S(2)}) %collective-permute-start.13) | collective-permute-done | bytes 458784 | tf_op jit(solution)/shard_map/ppermute | solution.py:40
  159.0 10.2 %collective-permute-done.12 = bf16[448,512]{1,0:T(8,128)(2,1)S(1)} collective-permute-done((bf16[448,512]{1,0:T(8,128)(2,1)S(1)}, bf16[448,512]{1,0:T(8,128)(2,1)S(1)}, u32[]{:S(2)}, u32[]{:S(2)}) %collective-permute-start.12) | collective-permute-done | bytes 458784 | tf_op jit(solution)/shard_map/ppermute | solution.py:40
  169.6 1.0 maximum_bitcast_fusion
  170.8 0.7 fusion.39
  171.4 4.7 %all-to-all-start.4 = ((bf16[4,32,512]{2,1,0:T(8,128)(2,1)}), bf16[4,32,512]{2,1,0:T(8,128)(2,1)S(1)}, u32[]{:S(2)}, u32[]{:S(2)}) async-start(bf16[4,32,512]{2,1,0:T(8,128)(2,1)} %fusion.39), calls=%async_computation.4 | async-start | bytes 262144 | tf_op jit(solution)/shard_map/all_to_all | solution.py:14
  176.2 4.8 %all-to-all-done.4 = bf16[4,32,512]{2,1,0:T(8,128)(2,1)S(1)} async-done(((bf16[4,32,512]{2,1,0:T(8,128)(2,1)}), bf16[4,32,512]{2,1,0:T(8,128)(2,1)S(1)}, u32[]{:S(2)}, u32[]{:S(2)}) %all-to-all-start.4) | async-done | bytes 131104 | tf_op jit(solution)/shard_map/all_to_all | solution.py:14
  181.3 0.7 pad_maximum_fusion.15
  182.0 8.8 %all-to-all-start.5 = ((bf16[16,32,128]{2,1,0:T(8,128)(2,1)}), bf16[16,32,128]{2,1,0:T(8,128)(2,1)S(1)}, u32[]{:S(2)}, u32[]{:S(2)}) async-start(bf16[16,32,128]{2,1,0:T(8,128)(2,1)} %pad_maximum_fusion.15), calls=%async_computation.5 | async-start | bytes 262144 | tf_op jit(solution)/shard_map/all_to_all | solution.py:14
  190.7 1.0 maximum_bitcast_fusion.1
  191.8 7.8 %all-to-all-done.5 = bf16[16,32,128]{2,1,0:T(8,128)(2,1)S(1)} async-done(((bf16[16,32,128]{2,1,0:T(8,128)(2,1)}), bf16[16,32,128]{2,1,0:T(8,128)(2,1)S(1)}, u32[]{:S(2)}, u32[]{:S(2)}) %all-to-all-start.5) | async-done | bytes 131104 | tf_op jit(solution)/shard_map/all_to_all | solution.py:14
  199.7 0.6 subtract_multiply_fusion
  200.2 1.1 fusion.7
  (98 shorter events, 3.4 us)
Async XLA Ops:
  0.6 2.6 %copy-start = (bf16[256,128]{1,0:T(8,128)(2,1)S(1)}, bf16[256,128]{1,0:T(8,128)(2,1)}, u32[]{:S(2)}) copy-start(bf16[256,128]{1,0:T(8,128)(2,1)} %param.9) | copy-start | bytes 196612
  3.3 14.0 %copy-start.2 = (bf16[1,224,2048]{2,1,0:T(8,128)(2,1)S(1)}, bf16[1,224,2048]{2,1,0:T(8,128)(2,1)}, u32[]{:S(2)}) copy-start(bf16[1,224,2048]{2,1,0:T(8,128)(2,1)} %param.14) | copy-start | bytes 2752516
  5.4 24.3 %all-to-all-start = ((bf16[16,48,128]{2,1,0:T(8,128)(2,1)}), bf16[16,48,128]{2,1,0:T(8,128)(2,1)S(1)}, u32[]{:S(2)}, u32[]{:S(2)}) async-start(bf16[16,48,128]{2,1,0:T(8,128)(2,1)} %pad_maximum_fusion.11), calls=%async_computation | async-start | bytes 393216 | tf_op jit(solution)/shard_map/all_to_all | solution.py:14
  17.2 11.0 %copy-start.9 = (f32[1,256]{1,0:T(1,128)S(1)}, f32[1,256]{1,0:T(1,128)}, u32[]{:S(2)}) copy-start(f32[1,256]{1,0:T(1,128)} %param.10) | copy-start | bytes 3076
  17.3 11.2 %copy-start.3 = (bf16[1,224,2048]{2,1,0:T(8,128)(2,1)S(1)}, bf16[1,224,2048]{2,1,0:T(8,128)(2,1)}, u32[]{:S(2)}) copy-start(bf16[1,224,2048]{2,1,0:T(8,128)(2,1)} %param.15) | copy-start | bytes 2752516
  18.1 15.8 %collective-permute-start.2 = (bf16[224,512]{1,0:T(8,128)(2,1)}, bf16[224,512]{1,0:T(8,128)(2,1)S(1)}, u32[]{:S(2)}, u32[]{:S(2)}) collective-permute-start(bf16[224,512]{1,0:T(8,128)(2,1)} %get-tuple-element.57), channel_id=1, source_target_pairs={{0,384},{128,0},{256,128},{384,256},{1,385},{129,1},{257,129},{385... | collective-permute-start | bytes 688136 | tf_op jit(solution)/shard_map/ppermute | solution.py:40
  22.5 11.4 %collective-permute-start.1 = (bf16[224,512]{1,0:T(8,128)(2,1)}, bf16[224,512]{1,0:T(8,128)(2,1)S(1)}, u32[]{:S(2)}, u32[]{:S(2)}) collective-permute-start(bf16[224,512]{1,0:T(8,128)(2,1)} %get-tuple-element.58), channel_id=1, source_target_pairs={{0,256},{128,384},{256,0},{384,128},{1,257},{129,385},{257,1},{385... | collective-permute-start | bytes 688136 | tf_op jit(solution)/shard_map/ppermute | solution.py:40
  25.0 13.7 %collective-permute-start = (bf16[224,512]{1,0:T(8,128)(2,1)}, bf16[224,512]{1,0:T(8,128)(2,1)}, u32[]{:S(2)}, u32[]{:S(2)}) collective-permute-start(bf16[224,512]{1,0:T(8,128)(2,1)} %get-tuple-element.56), channel_id=1, source_target_pairs={{0,128},{128,256},{256,384},{384,0},{1,129},{129,257},{257,385},{3... | collective-permute-start | bytes 688136 | tf_op jit(solution)/shard_map/ppermute | solution.py:40
  28.5 1.0 copy-start.5
  28.5 1.0 copy-start.6
  30.4 10.2 %all-to-all-start.1 = ((bf16[4,4,56,128]{3,2,1,0:T(8,128)(2,1)}), bf16[4,4,56,128]{3,2,1,0:T(8,128)(2,1)S(1)}, u32[]{:S(2)}, u32[]{:S(2)}) async-start(bf16[4,4,56,128]{3,2,1,0:T(8,128)(2,1)} %pad_maximum_fusion.10), calls=%async_computation.1 | async-start | bytes 458752 | tf_op jit(solution)/shard_map/all_to_all | solution.py:14
  41.7 34.8 %all-to-all-start.2 = ((bf16[8,104,512]{2,1,0:T(8,128)(2,1)}), bf16[8,104,512]{2,1,0:T(8,128)(2,1)}, u32[]{:S(2)}, u32[]{:S(2)}) async-start(bf16[8,104,512]{2,1,0:T(8,128)(2,1)} %broadcast_in_dim.102), calls=%async_computation.2 | async-start | bytes 1703936 | tf_op jit(solution)/shard_map/all_to_all | solution.py:14
  48.6 12.8 %collective-permute-start.5 = (bf16[448,512]{1,0:T(8,128)(2,1)S(1)}, bf16[448,512]{1,0:T(8,128)(2,1)S(1)}, u32[]{:S(2)}, u32[]{:S(2)}) collective-permute-start(bf16[448,512]{1,0:T(8,128)(2,1)S(1)} %get-tuple-element.77), channel_id=1, source_target_pairs={{0,384},{128,0},{256,128},{384,256},{1,385},{129,1},{257,129},{385... | collective-permute-start | bytes 1376264 | tf_op jit(solution)/shard_map/ppermute | solution.py:40
  50.7 13.2 %collective-permute-start.4 = (bf16[448,512]{1,0:T(8,128)(2,1)S(1)}, bf16[448,512]{1,0:T(8,128)(2,1)S(1)}, u32[]{:S(2)}, u32[]{:S(2)}) collective-permute-start(bf16[448,512]{1,0:T(8,128)(2,1)S(1)} %get-tuple-element.76), channel_id=1, source_target_pairs={{0,256},{128,384},{256,0},{384,128},{1,257},{129,385},{257,1},{385... | collective-permute-start | bytes 1376264 | tf_op jit(solution)/shard_map/ppermute | solution.py:40
  53.2 23.1 %collective-permute-start.3 = (bf16[448,512]{1,0:T(8,128)(2,1)S(1)}, bf16[448,512]{1,0:T(8,128)(2,1)S(1)}, u32[]{:S(2)}, u32[]{:S(2)}) collective-permute-start(bf16[448,512]{1,0:T(8,128)(2,1)S(1)} %get-tuple-element.75), channel_id=1, source_target_pairs={{0,128},{128,256},{256,384},{384,0},{1,129},{129,257},{257,385},{3... | collective-permute-start | bytes 1376264 | tf_op jit(solution)/shard_map/ppermute | solution.py:40
  76.5 2.0 copy-start.1
  78.5 0.8 copy-start.12
  79.3 8.5 %copy-start.4 = (bf16[896,512]{1,0:T(8,128)(2,1)}, bf16[896,512]{1,0:T(8,128)(2,1)S(1)}, u32[]{:S(2)}) copy-start(bf16[896,512]{1,0:T(8,128)(2,1)S(1)} %convolution_convert_fusion.2) | copy-start | bytes 2752516
  80.3 47.9 %all-to-all-start.6 = ((bf16[8,96,512]{2,1,0:T(8,128)(2,1)}), bf16[8,96,512]{2,1,0:T(8,128)(2,1)}, u32[]{:S(2)}, u32[]{:S(2)}) async-start(bf16[8,96,512]{2,1,0:T(8,128)(2,1)} %broadcast_in_dim.107), calls=%async_computation.6 | async-start | bytes 1572864 | tf_op jit(solution)/shard_map/all_to_all | solution.py:14
  87.1 9.5 %copy-start.13 = (bf16[512,512]{1,0:T(8,128)(2,1)S(1)}, bf16[512,512]{1,0:T(8,128)(2,1)}, u32[]{:S(2)}) copy-start(bf16[512,512]{1,0:T(8,128)(2,1)} %copy-done.12) | copy-start | bytes 1572868
  87.9 14.5 %collective-permute-start.8 = (bf16[224,512]{1,0:T(8,128)(2,1)S(1)}, bf16[224,512]{1,0:T(8,128)(2,1)S(1)}, u32[]{:S(2)}, u32[]{:S(2)}) collective-permute-start(bf16[224,512]{1,0:T(8,128)(2,1)S(1)} %get-tuple-element.53), channel_id=1, source_target_pairs={{0,128},{128,256},{256,384},{384,0},{1,129},{129,257},{257,385},{3... | collective-permute-start | bytes 688136 | tf_op jit(solution)/shard_map/ppermute | solution.py:40
  89.8 12.6 %collective-permute-start.7 = (bf16[224,512]{1,0:T(8,128)(2,1)S(1)}, bf16[224,512]{1,0:T(8,128)(2,1)S(1)}, u32[]{:S(2)}, u32[]{:S(2)}) collective-permute-start(bf16[224,512]{1,0:T(8,128)(2,1)S(1)} %get-tuple-element.54), channel_id=1, source_target_pairs={{0,256},{128,384},{256,0},{384,128},{1,257},{129,385},{257,1},{385... | collective-permute-start | bytes 688136 | tf_op jit(solution)/shard_map/ppermute | solution.py:40
  92.4 12.6 %collective-permute-start.6 = (bf16[224,512]{1,0:T(8,128)(2,1)S(1)}, bf16[224,512]{1,0:T(8,128)(2,1)S(1)}, u32[]{:S(2)}, u32[]{:S(2)}) collective-permute-start(bf16[224,512]{1,0:T(8,128)(2,1)S(1)} %get-tuple-element.52), channel_id=1, source_target_pairs={{0,384},{128,0},{256,128},{384,256},{1,385},{129,1},{257,129},{385... | collective-permute-start | bytes 688136 | tf_op jit(solution)/shard_map/ppermute | solution.py:40
  106.9 24.5 %copy-start.8 = (bf16[224,512]{1,0:T(8,128)(2,1)}, bf16[224,512]{1,0:T(8,128)(2,1)S(1)}, u32[]{:S(2)}) copy-start(bf16[224,512]{1,0:T(8,128)(2,1)S(1)} %get-tuple-element.40) | copy-start | bytes 688132
  106.9 14.7 %collective-permute-start.11 = (bf16[224,512]{1,0:T(8,128)(2,1)S(1)}, bf16[224,512]{1,0:T(8,128)(2,1)S(1)}, u32[]{:S(2)}, u32[]{:S(2)}) collective-permute-start(bf16[224,512]{1,0:T(8,128)(2,1)S(1)} %get-tuple-element.40), channel_id=1, source_target_pairs={{0,384},{128,0},{256,128},{384,256},{1,385},{129,1},{257,129},{385... | collective-permute-start | bytes 688136 | tf_op jit(solution)/shard_map/ppermute | solution.py:40
  112.4 10.0 %collective-permute-start.10 = (bf16[224,512]{1,0:T(8,128)(2,1)S(1)}, bf16[224,512]{1,0:T(8,128)(2,1)}, u32[]{:S(2)}, u32[]{:S(2)}) collective-permute-start(bf16[224,512]{1,0:T(8,128)(2,1)S(1)} %get-tuple-element.40), channel_id=1, source_target_pairs={{0,256},{128,384},{256,0},{384,128},{1,257},{129,385},{257,1},{385... | collective-permute-start | bytes 688136 | tf_op jit(solution)/shard_map/ppermute | solution.py:40
  114.3 13.9 %collective-permute-start.9 = (bf16[224,512]{1,0:T(8,128)(2,1)S(1)}, bf16[224,512]{1,0:T(8,128)(2,1)S(1)}, u32[]{:S(2)}, u32[]{:S(2)}) collective-permute-start(bf16[224,512]{1,0:T(8,128)(2,1)S(1)} %get-tuple-element.40), channel_id=1, source_target_pairs={{0,128},{128,256},{256,384},{384,0},{1,129},{129,257},{257,385},{3... | collective-permute-start | bytes 688136 | tf_op jit(solution)/shard_map/ppermute | solution.py:40
  121.7 9.7 %copy-start.10 = (bf16[224,512]{1,0:T(8,128)(2,1)}, bf16[224,512]{1,0:T(8,128)(2,1)S(1)}, u32[]{:S(2)}) copy-start(bf16[224,512]{1,0:T(8,128)(2,1)S(1)} %collective-permute-done.11) | copy-start | bytes 688132
  128.2 0.7 copy-start.11
  132.5 18.4 %collective-permute-start.14 = (bf16[448,512]{1,0:T(8,128)(2,1)}, bf16[448,512]{1,0:T(8,128)(2,1)}, u32[]{:S(2)}, u32[]{:S(2)}) collective-permute-start(bf16[448,512]{1,0:T(8,128)(2,1)} %get-tuple-element.43), channel_id=1, source_target_pairs={{0,128},{128,256},{256,384},{384,0},{1,129},{129,257},{257,385},{3... | collective-permute-start | bytes 1376264 | tf_op jit(solution)/shard_map/ppermute | solution.py:40
  137.9 6.4 %copy-start.7 = (bf16[448,512]{1,0:T(8,128)(2,1)S(1)}, bf16[448,512]{1,0:T(8,128)(2,1)}, u32[]{:S(2)}) copy-start(bf16[448,512]{1,0:T(8,128)(2,1)} %get-tuple-element.42) | copy-start | bytes 1376260
  137.9 32.7 %all-to-all-start.3 = ((bf16[8,104,512]{2,1,0:T(8,128)(2,1)}), bf16[8,104,512]{2,1,0:T(8,128)(2,1)S(1)}, u32[]{:S(2)}, u32[]{:S(2)}) async-start(bf16[8,104,512]{2,1,0:T(8,128)(2,1)} %fusion.12), calls=%async_computation.3 | async-start | bytes 1703936 | tf_op jit(solution)/shard_map/all_to_all | solution.py:14
  144.3 14.7 %collective-permute-start.13 = (bf16[448,512]{1,0:T(8,128)(2,1)S(1)}, bf16[448,512]{1,0:T(8,128)(2,1)S(1)}, u32[]{:S(2)}, u32[]{:S(2)}) collective-permute-start(bf16[448,512]{1,0:T(8,128)(2,1)S(1)} %copy-done.7), channel_id=1, source_target_pairs={{0,256},{128,384},{256,0},{384,128},{1,257},{129,385},{257,1},{385... | collective-permute-start | bytes 1376264 | tf_op jit(solution)/shard_map/ppermute | solution.py:40
  146.7 22.5 %collective-permute-start.12 = (bf16[448,512]{1,0:T(8,128)(2,1)S(1)}, bf16[448,512]{1,0:T(8,128)(2,1)S(1)}, u32[]{:S(2)}, u32[]{:S(2)}) collective-permute-start(bf16[448,512]{1,0:T(8,128)(2,1)S(1)} %get-tuple-element.41), channel_id=1, source_target_pairs={{0,384},{128,0},{256,128},{384,256},{1,385},{129,1},{257,129},{385... | collective-permute-start | bytes 1376264 | tf_op jit(solution)/shard_map/ppermute | solution.py:40
  171.4 9.5 %all-to-all-start.4 = ((bf16[4,32,512]{2,1,0:T(8,128)(2,1)}), bf16[4,32,512]{2,1,0:T(8,128)(2,1)S(1)}, u32[]{:S(2)}, u32[]{:S(2)}) async-start(bf16[4,32,512]{2,1,0:T(8,128)(2,1)} %fusion.39), calls=%async_computation.4 | async-start | bytes 262144 | tf_op jit(solution)/shard_map/all_to_all | solution.py:14
  182.0 17.7 %all-to-all-start.5 = ((bf16[16,32,128]{2,1,0:T(8,128)(2,1)}), bf16[16,32,128]{2,1,0:T(8,128)(2,1)S(1)}, u32[]{:S(2)}, u32[]{:S(2)}) async-start(bf16[16,32,128]{2,1,0:T(8,128)(2,1)} %pad_maximum_fusion.15), calls=%async_computation.5 | async-start | bytes 262144 | tf_op jit(solution)/shard_map/all_to_all | solution.py:14

commit v3 on v2

--- a/solution.py
+++ b/solution.py
@@ -38,6 +38,21 @@
 def shift(x, by):
     size = lax.axis_size(X)
     return lax.ppermute(x, X, [(i, (i + by) % size) for i in range(size)])
+
+
+def over_x(blocks, sign):
+    came = [blocks[0]]
+    for k in range(1, len(blocks)):
+        came.append(shift(blocks[k], sign * k))
+    return came
+
+
+def back_in_x(blocks, xi):
+    size = blocks.shape[0]
+    return [
+        lax.dynamic_index_in_dim(blocks, (xi + size - k) % size, 0, keepdims=False)
+        for k in range(size)
+    ]
 
 
 def quarter_at(w, index, nx):
@@ -84,13 +99,12 @@
     sent_grad = dot(flat_pick, grad_out, 1, 0).astype(BF).reshape(ne, cap + PAD, width_dev)
     sent_input = dot(flat_pick, saved_inputs, 1, 0).astype(BF).reshape(ne, cap + PAD, width_dev)
     sent = jnp.concatenate([sent_grad[:, :cap], sent_input[:, :cap]], axis=1)
-    rows = exchange(sent, E).reshape(nx, quarter, 2 * cap, width_dev)
-
-    down_mine = [quarter_at(w_down[0], (xi + k) % nx, nx) for k in range(nx)]
-    up_mine = [quarter_at(w_up[0], (xi + k) % nx, nx) for k in range(nx)]
-    down_part = jnp.concatenate(
-        [down_mine[0]] + [shift(down_mine[k], k) for k in range(1, nx)], axis=0
-    )
+    rows = exchange(sent, E)
+    rows = rows.reshape(nx, quarter, 2 * cap, width_dev)
+
+    down_part = jnp.concatenate([quarter_at(w_down[0], (xi + nx - k) % nx, nx) for k in range(nx)], axis=1)
+    up_part = [quarter_at(w_up[0], (xi + k) % nx, nx) for k in range(nx)]
+    up_part = jnp.concatenate(over_x(up_part, 1), axis=0)
 
     own_rows = lax.dynamic_index_in_dim(local_rows, ei, 0, keepdims=False)
     own_rows = jnp.pad(own_rows, (0, lane - cap - PAD), constant_values=-1)
@@ -105,21 +119,13 @@
     sig = jax.nn.sigmoid(gate_value)
     active = gate_value * sig
     hidden = active * up_value
-    hidden_own = hidden.astype(BF)
-    up_mine, hidden_own, rows, down_part = lax.optimization_barrier(
-        (up_mine, hidden_own, rows, down_part)
-    )
-    pairs = [
-        shift(jnp.concatenate([up_mine[k], hidden_own], axis=0), k) for k in range(1, nx)
-    ]
-    up_part = jnp.concatenate([up_mine[0]] + [p[:units] for p in pairs], axis=0)
-    hidden_all = jnp.concatenate([hidden_own] + [p[units:] for p in pairs], axis=0)
 
     grads = rows[:, :, :cap].transpose(0, 2, 1, 3).reshape(nx * cap, part)
     inputs = rows[:, :, cap : 2 * cap].transpose(0, 2, 1, 3).reshape(nx * cap, part)
     gates = jnp.pad(rows[:, 0, 2 * cap], ((0, PAD - nx), (0, part - lane)))
     block = nx * cap + PAD
     grads_all = to_all(jnp.concatenate([grads, gates], axis=0), Y)
+    inputs_all = to_all(inputs, Y)
 
     chosen_row = lax.dynamic_index_in_dim(chosen, ei, 0, keepdims=True)
     owner = chosen_row // tok_dev
@@ -135,31 +141,34 @@
     owner_hit = rows_of(shards, slots) == owner_y * nx + owner_x
     within_hit = onehot(rows_of(lane, slots) == within)
 
-    grads_all, up_part, hidden_all = lax.optimization_barrier((grads_all, up_part, hidden_all))
     grads_slots = dot(place_block, grads_all.reshape(ny * block, part), 0, 0).astype(BF)
     gates_all = grads_all[:, nx * cap : nx * cap + nx, :lane].reshape(shards, lane)
     gate_slot = jnp.sum(
         jnp.where(owner_hit, dot(gates_all, within_hit, 1, 0), 0.0), axis=0, keepdims=True
     )
-    raw_part = dot(down_part, grads_slots, 1, 1).astype(BF).reshape(nx, units, slots)
-    inputs, raw_part = lax.optimization_barrier((inputs, raw_part))
-    inputs_all = to_all(inputs, Y)
-    raw_came = [shift(raw_part[k], -k) for k in range(1, nx)]
-    raw_grad = raw_part[0].astype(F32)
-    for came in raw_came:
-        raw_grad = raw_grad + came.astype(F32)
+    grads_slots = jnp.concatenate(over_x([grads_slots] * nx, 1), axis=1)
+    raw_grad = dot(down_part, grads_slots, 1, 1)
     dots = jnp.sum(hidden * raw_grad, axis=0, keepdims=True)
     hid_grad = gate_slot * raw_grad
     up_grad = (hid_grad * active).astype(BF)
     gate_grad = (hid_grad * up_value * sig * (1.0 + gate_value * (1.0 - sig))).astype(BF)
-    up_all = jnp.concatenate([up_grad] + [shift(up_grad, k) for k in range(1, nx)], axis=0)
-
+    up_all = lax.all_gather(up_grad, X)
+    up_all = jnp.concatenate(back_in_x(up_all, xi), axis=0)
+
+    hidden_gated = (hidden.astype(BF).astype(F32) * gate_slot).astype(BF)
+    grad_down = dot(hidden_gated, grads_slots, 1, 0).astype(BF)
+    grad_down = jnp.concatenate(
+        [quarter_at(grad_down, (xi + nx - q) % nx, nx) for q in range(nx)], axis=1
+    )
     dx = dot(up_all, up_part, 0, 0).astype(BF)
     dx_rows = dot(place_rows, dx, 1, 0).astype(BF).reshape(ny, nx * cap, part)
     dots_own = jnp.where(owner_hit, dots, 0.0).astype(BF)
     dots_rows = dot(dots_own, within_hit, 1, 1).astype(BF).reshape(ny, nx, lane)
     dots_rows = jnp.pad(dots_rows, ((0, 0), (0, PAD - nx), (0, part - lane)))
     dx_back = exchange(jnp.concatenate([dx_rows, dots_rows], axis=1), Y)
+    inputs_slots = dot(place_rows, inputs_all.reshape(-1, part), 0, 0).astype(BF)
+    grad_up = dot(up_all, inputs_slots, 1, 0).astype(BF).reshape(nx, units, part)
+    up_home = over_x(grad_up, -1)
     dx_sum = jnp.sum(dx_back.astype(F32), axis=0).astype(BF)
     dots_sum = dx_sum[nx * cap : nx * cap + nx].reshape(nx, 1, part)
     dx_sum = jnp.concatenate(
@@ -178,21 +187,13 @@
     spread = exchange(
         jnp.concatenate([to_experts, jnp.broadcast_to(tail[None], (ne, PAD, lane))], axis=1), E
     )
+    up_home, spread = lax.optimization_barrier((up_home, spread))
+    grad_up = in_turn(up_home, xi)
     grad_tokens = dot(flat_pick, spread.reshape(-1, width_dev), 0, 0).astype(BF)
     pieces = jnp.sum(spread[:, cap : cap + 2 * tok_dev // lane].astype(F32), axis=0)
     router_sum = jnp.sum(pieces.reshape(2, 1, tok_dev), axis=0)
     grad_logits = router_probs * (gate_tokens - router_sum)
 
-    hidden_gated = (hidden_all.astype(F32) * gate_slot).astype(BF)
-    grad_down = dot(hidden_gated, grads_slots, 1, 0).astype(BF)
-    inputs_slots = dot(place_rows, inputs_all.reshape(-1, part), 0, 0).astype(BF)
-    grad_up = dot(up_all, inputs_slots, 1, 0).astype(BF)
-    both = jnp.concatenate(
-        [grad_down.reshape(nx, units, part), grad_up.reshape(nx, units, part)], axis=1
-    )
-    home = [both[0]] + [shift(both[k], -k) for k in range(1, nx)]
-    grad_down = in_turn([h[:units] for h in home], xi)
-    grad_up = in_turn([h[units:] for h in home], xi)
     return grad_tokens, grad_logits, grad_down[None], grad_up[None], gate_grad.T[None]
 
 

time: 203 us -> 184 us (0.906)
  starting transfers between devices: 91.7 us -> 65.6 us
  blocking collectives: 0 us -> 25.8 us
  waiting for transfers between devices: 73.8 us -> 59.5 us
  other arithmetic: 15.5 us -> 10.6 us
  matrix products: 11.6 us -> 14.2 us
    ppermute x15 -> x9, waiting for transfers between devices: 61.2 us -> 5.08 us  [shift(): return lax.ppermute(x, X, [(i, (i + by) % size) for i in range(size)])]
    all_to_all x7 -> x6, waiting for transfers between devices: 12.6 us -> 54.4 us  [exchange(): return lax.all_to_all(x, axis, 0, 0, tiled=True)]
    all_gather x0 -> x1, blocking collectives: none -> 15.7 us  [local(): up_all = lax.all_gather(up_grad, X)]
    ppermute x15 -> x9, starting transfers between devices: 43.2 us -> 27.8 us  [shift(): return lax.ppermute(x, X, [(i, (i + by) % size) for i in range(size)])]
    all_to_all x7 -> x6, starting transfers between devices: 48.5 us -> 37.8 us  [exchange(): return lax.all_to_all(x, axis, 0, 0, tiled=True)]
    all_to_all x0 -> x1, blocking collectives: none -> 10.2 us  [exchange(): return lax.all_to_all(x, axis, 0, 0, tiled=True)]
    dot_general x12, matrix products: 11.6 us -> 14.2 us  [dot(): lax.dot_general(a, b, (((ca,), (cb,)), ((), ())), preferred_element_type=...]
    concatenate x4 -> x1, other arithmetic: 2.16 us -> 0.01 us  [the longest x1 1.92 us: local(): jnp.concatenate([down_mine[0]] + [shift(down_mine[k], k) for k in range(1...]
  transfers between devices with their start and end apart: 22 -> 15, of which waited for: 13 -> 7; matrix products, arithmetic and copies ran while one was open for 8% -> 10% of each run, Pallas kernels for 0% -> 0%
where the time goes in v3:
time: 184 us; the launch traced here: 183 us
  starting transfers between devices  65.6 us (36%)
  waiting for transfers between devices  59.5 us (32%)
  blocking collectives  25.8 us (14%)
  matrix products  14.2 us (8%)
  other arithmetic  10.6 us (6%)
  local copies, waits for them, and re-layouts  6.2 us (3%)
    all_to_all x6, waiting for transfers between devices, exchange(): return lax.all_to_all(x, axis, 0, 0, tiled=True)  54.4 us
    all_to_all x6, starting transfers between devices, exchange(): return lax.all_to_all(x, axis, 0, 0, tiled=True)  37.8 us
    ppermute x9, starting transfers between devices, shift(): return lax.ppermute(x, X, [(i, (i + by) % size) for i in range(size)])  27.8 us
    all_gather x1, blocking collectives, local(): up_all = lax.all_gather(up_grad, X)  15.7 us
    dot_general x12, matrix products, dot(): lax.dot_general(a, b, (((ca,), (cb,)), ((), ())), preferred_element_type=...  14.2 us
    all_to_all x1, blocking collectives, exchange(): return lax.all_to_all(x, axis, 0, 0, tiled=True)  10.2 us
    ppermute x9, waiting for transfers between devices, shift(): return lax.ppermute(x, X, [(i, (i + by) % size) for i in range(size)])  5.08 us
  transfers between devices with their start and end apart: 15, of which 7 were waited for; matrix products, arithmetic and copies ran while one was open for 10% of the time, Pallas kernels for 0%

profile of v3, /device:TPU:1, one launch (start us, length us, event | category | flops | bytes accessed | tf_op | source)
XLA Modules:
  0.0 183.2 jit_solution(11677049363271185796)
XLA Ops:
  0.7 0.9 convert_reduce_fusion.2
  1.5 0.1 iota_add_fusion
  1.6 1.2 select_reduce_fusion
  2.9 0.1 broadcast_compare_fusion
  2.9 0.1 and_select_fusion.3
  3.0 0.1 sub.87
  3.1 0.1 lt.175
  3.2 0.1 and.93
  3.3 0.3 convolution_convert_fusion.4
  3.6 1.1 convolution_convert_fusion.3
  4.7 0.7 pad_maximum_fusion.6
  5.4 11.8 %all-to-all-start = ((bf16[16,48,128]{2,1,0:T(8,128)(2,1)}), bf16[16,48,128]{2,1,0:T(8,128)(2,1)S(1)}, u32[]{:S(2)}, u32[]{:S(2)}) async-start(bf16[16,48,128]{2,1,0:T(8,128)(2,1)} %pad_maximum_fusion.6), calls=%async_computation | async-start | bytes 393216 | tf_op jit(solution)/shard_map/all_to_all | solution.py:14
  17.3 0.2 fusion.10
  17.5 10.0 %all-to-all-done = bf16[16,48,128]{2,1,0:T(8,128)(2,1)S(1)} async-done(((bf16[16,48,128]{2,1,0:T(8,128)(2,1)}), bf16[16,48,128]{2,1,0:T(8,128)(2,1)S(1)}, u32[]{:S(2)}, u32[]{:S(2)}) %all-to-all-start) | async-done | bytes 196640 | tf_op jit(solution)/shard_map/all_to_all | solution.py:14
  27.5 10.2 %all_to_all.35 = bf16[4,4,56,128]{3,2,1,0:T(8,128)(2,1)S(1)} all-to-all(bf16[4,4,56,128]{3,2,1,0:T(8,128)(2,1)S(1)} %pad_maximum_fusion.5), channel_id=1, replica_groups=mesh['dp_0'=4,'dp_1'=8,'expert'=16] {'dp_0'}, dimensions={0} | all-to-all | bytes 458752 | tf_op jit(solution)/shard_map/all_to_all | solution.py:14
  37.8 1.0 broadcast_in_dim.101
  38.7 6.8 %all-to-all-start.2 = ((bf16[8,104,512]{2,1,0:T(8,128)(2,1)}), bf16[8,104,512]{2,1,0:T(8,128)(2,1)S(1)}, u32[]{:S(2)}, u32[]{:S(2)}) async-start(bf16[8,104,512]{2,1,0:T(8,128)(2,1)} %broadcast_in_dim.101), calls=%async_computation.2 | async-start | bytes 1703936 | tf_op jit(solution)/shard_map/all_to_all | solution.py:14
  45.6 0.7 compare_select_fusion.1
  46.3 0.1 convert_reduce_fusion
  46.4 0.1 select_reduce_fusion.1
  46.5 24.0 %all-to-all-done.2 = bf16[8,104,512]{2,1,0:T(8,128)(2,1)S(1)} async-done(((bf16[8,104,512]{2,1,0:T(8,128)(2,1)}), bf16[8,104,512]{2,1,0:T(8,128)(2,1)S(1)}, u32[]{:S(2)}, u32[]{:S(2)}) %all-to-all-start.2) | async-done | bytes 852000 | tf_op jit(solution)/shard_map/all_to_all | solution.py:14
  70.5 1.6 fusion.6
  72.1 2.3 %collective-permute-start = (bf16[512,512]{0,1:T(8,128)(2,1)}, bf16[512,512]{0,1:T(8,128)(2,1)}, u32[]{:S(2)}, u32[]{:S(2)}) collective-permute-start(bf16[512,512]{0,1:T(8,128)(2,1)} %fusion.6), channel_id=1, source_target_pairs={{0,128},{128,256},{256,384},{384,0},{1,129},{129,257},{257,385},{3... | collective-permute-start | bytes 1572872 | tf_op jit(solution)/shard_map/ppermute | solution.py:40
  74.5 3.7 %collective-permute-start.1 = (bf16[512,512]{0,1:T(8,128)(2,1)}, bf16[512,512]{0,1:T(8,128)(2,1)}, u32[]{:S(2)}, u32[]{:S(2)}) collective-permute-start(bf16[512,512]{0,1:T(8,128)(2,1)} %fusion.6), channel_id=1, source_target_pairs={{0,256},{128,384},{256,0},{384,128},{1,257},{129,385},{257,1},{385... | collective-permute-start | bytes 1572872 | tf_op jit(solution)/shard_map/ppermute | solution.py:40
  78.2 2.5 %collective-permute-start.2 = (bf16[512,512]{0,1:T(8,128)(2,1)}, bf16[512,512]{0,1:T(8,128)(2,1)}, u32[]{:S(2)}, u32[]{:S(2)}) collective-permute-start(bf16[512,512]{0,1:T(8,128)(2,1)} %fusion.6), channel_id=1, source_target_pairs={{0,384},{128,0},{256,128},{384,256},{1,385},{129,1},{257,129},{385... | collective-permute-start | bytes 1572872 | tf_op jit(solution)/shard_map/ppermute | solution.py:40
  80.7 1.0 dynamic-slice_bitcast_fusion.7
  81.7 2.7 %collective-permute-start.6 = (bf16[224,512]{1,0:T(8,128)(2,1)}, bf16[224,512]{1,0:T(8,128)(2,1)}, u32[]{:S(2)}, u32[]{:S(2)}) collective-permute-start(bf16[224,512]{1,0:T(8,128)(2,1)} %get-tuple-element.33), channel_id=1, source_target_pairs={{0,128},{128,256},{256,384},{384,0},{1,129},{129,257},{257,385},{3... | collective-permute-start | bytes 688136 | tf_op jit(solution)/shard_map/ppermute | solution.py:40
  84.4 3.4 %collective-permute-start.7 = (bf16[224,512]{1,0:T(8,128)(2,1)}, bf16[224,512]{1,0:T(8,128)(2,1)}, u32[]{:S(2)}, u32[]{:S(2)}) collective-permute-start(bf16[224,512]{1,0:T(8,128)(2,1)} %get-tuple-element.35), channel_id=1, source_target_pairs={{0,256},{128,384},{256,0},{384,128},{1,257},{129,385},{257,1},{385... | collective-permute-start | bytes 688136 | tf_op jit(solution)/shard_map/ppermute | solution.py:40
  87.9 0.9 dynamic-slice_bitcast_fusion.15
  88.9 0.9 broadcast_in_dim.106
  89.9 3.7 %all-to-all-start.3 = ((bf16[8,96,512]{2,1,0:T(8,128)(2,1)}), bf16[8,96,512]{2,1,0:T(8,128)(2,1)S(1)}, u32[]{:S(2)}, u32[]{:S(2)}) async-start(bf16[8,96,512]{2,1,0:T(8,128)(2,1)} %broadcast_in_dim.106), calls=%async_computation.3 | async-start | bytes 1572864 | tf_op jit(solution)/shard_map/all_to_all | solution.py:14
  93.6 0.2 fusion.8
  93.8 4.0 %collective-permute-start.8 = (bf16[224,512]{1,0:T(8,128)(2,1)}, bf16[224,512]{1,0:T(8,128)(2,1)S(1)}, u32[]{:S(2)}, u32[]{:S(2)}) collective-permute-start(bf16[224,512]{1,0:T(8,128)(2,1)} %get-tuple-element.34), channel_id=1, source_target_pairs={{0,384},{128,0},{256,128},{384,256},{1,385},{129,1},{257,129},{385... | collective-permute-start | bytes 688136 | tf_op jit(solution)/shard_map/ppermute | solution.py:40
  97.8 1.6 collective-permute-done.1
  99.3 3.5 %collective-permute-done.2 = bf16[512,512]{0,1:T(8,128)(2,1)} collective-permute-done((bf16[512,512]{0,1:T(8,128)(2,1)}, bf16[512,512]{0,1:T(8,128)(2,1)}, u32[]{:S(2)}, u32[]{:S(2)}) %collective-permute-start.2) | collective-permute-done | bytes 524320 | tf_op jit(solution)/shard_map/ppermute | solution.py:40
  102.8 2.4 %multiply_reduce_fusion = (bf16[512]{0:T(512)(128)(2,1)S(1)}, bf16[224,512]{1,0:T(8,128)(2,1)S(1)}, f32[224,512]{1,0:T(8,128)S(1)}) fusion(bf16[1,512,224]{1,2,0:T(8,128)(2,1)S(1)} %copy-done.3, bf16[1,512,224]{1,2,0:T(8,128)(2,1)S(1)} %copy-done.6, f32[512]{0:T(512)S(1)} %fusion.8, bf16[512,512]{0,1:T(8,128)(2,1)} %collective-permute-done.2, ...), kind=kOutput, calls=%fused_computation.71 | convolution fusion | flops 483196416 | bytes 4164608 | tf_op jit(solution)/shard_map/dot_general | solution.py:23
  105.2 15.7 %all-gather = bf16[896,512]{1,0:T(8,128)(2,1)S(1)} all-gather(bf16[224,512]{1,0:T(8,128)(2,1)S(1)} %get-tuple-element.49), channel_id=2, replica_groups=mesh['dp_0'=4,'dp_1'=8,'expert'=16] {'dp_0'}, dimensions={0}, use_global_device_ids=true | all-gather | bytes 1146880 | tf_op jit(solution)/shard_map/all_gather | solution.py:155
  121.0 0.2 convolution_convert_fusion.5
  121.2 0.7 copy-done.17
  121.9 2.4 %fusion.4 = bf16[768,512]{1,0:T(8,128)(2,1)S(1)} fusion(bf16[224,512]{1,0:T(8,128)(2,1)} %copy-done.17, bf16[224,512]{1,0:T(8,128)(2,1)} %collective-permute-done.7, bf16[224,512]{1,0:T(8,128)(2,1)} %collective-permute-done.6, bf16[224,512]{1,0:T(8,128)(2,1)S(1)} %copy-done.12, s32[512]{0:T(512)S(1)} %bitcast.191, ...), kind=kOutput, calls=%fused_computation.10 | convolution fusion | flops 880803840 | bytes 2623488 | tf_op jit(solution)/shard_map/dot_general | solution.py:23
  124.3 1.0 fusion.33
  125.3 3.6 %all-to-all-start.4 = ((bf16[8,104,512]{2,1,0:T(8,128)(2,1)}), bf16[8,104,512]{2,1,0:T(8,128)(2,1)S(1)}, u32[]{:S(2)}, u32[]{:S(2)}) async-start(bf16[8,104,512]{2,1,0:T(8,128)(2,1)} %fusion.33), calls=%async_computation.4 | async-start | bytes 1703936 | tf_op jit(solution)/shard_map/all_to_all | solution.py:14
  128.9 2.3 %convolution_convert_fusion.1 = bf16[896,512]{1,0:T(8,128)(2,1)S(1)} fusion(bf16[768,512]{1,0:T(8,128)(2,1)S(1)} %bitcast.170, s32[512]{0:T(512)S(1)} %bitcast.192, bf16[224,512]{1,0:T(8,128)(2,1)} %copy-done.9, bf16[224,512]{1,0:T(8,128)(2,1)} %copy-done.10, bf16[224,512]{1,0:T(8,128)(2,1)} %copy-done.11, bf16[224,512]{1,0:T(8,128)(2,1)S(1)} %get-tuple-element.40), kind=kOutput, calls=%fused_computation.9 | convolution fusion | flops 877199360 | bytes 2623488 | tf_op jit(solution)/shard_map/dot_general | solution.py:23
  131.2 0.9 fusion.82
  132.1 4.7 %collective-permute-start.3 = (bf16[224,512]{1,0:T(8,128)(2,1)}, bf16[224,512]{1,0:T(8,128)(2,1)S(1)}, u32[]{:S(2)}, u32[]{:S(2)}) collective-permute-start(bf16[224,512]{1,0:T(8,128)(2,1)} %get-tuple-element.38), channel_id=1, source_target_pairs={{0,384},{128,0},{256,128},{384,256},{1,385},{129,1},{257,129},{385... | collective-permute-start | bytes 688136 | tf_op jit(solution)/shard_map/ppermute | solution.py:40
  136.8 2.5 %collective-permute-start.4 = (bf16[224,512]{1,0:T(8,128)(2,1)}, bf16[224,512]{1,0:T(8,128)(2,1)S(1)}, u32[]{:S(2)}, u32[]{:S(2)}) collective-permute-start(bf16[224,512]{1,0:T(8,128)(2,1)} %get-tuple-element.37), channel_id=1, source_target_pairs={{0,256},{128,384},{256,0},{384,128},{1,257},{129,385},{257,1},{385... | collective-permute-start | bytes 688136 | tf_op jit(solution)/shard_map/ppermute | solution.py:40
  139.4 1.9 %collective-permute-start.5 = (bf16[224,512]{1,0:T(8,128)(2,1)}, bf16[224,512]{1,0:T(8,128)(2,1)}, u32[]{:S(2)}, u32[]{:S(2)}) collective-permute-start(bf16[224,512]{1,0:T(8,128)(2,1)} %get-tuple-element.36), channel_id=1, source_target_pairs={{0,128},{128,256},{256,384},{384,0},{1,129},{129,257},{257,385},{3... | collective-permute-start | bytes 688136 | tf_op jit(solution)/shard_map/ppermute | solution.py:40
  141.3 2.3 %convolution_convert_fusion = bf16[224,2048]{1,0:T(8,128)(2,1)S(1)} fusion(bf16[512,512]{0,1:T(8,128)(2,1)} %collective-permute-done.2, bf16[512,512]{0,1:T(8,128)(2,1)} %collective-permute-done.1, bf16[512,512]{0,1:T(8,128)(2,1)} %collective-permute-done, bf16[512,512]{0,1:T(8,128)(2,1)} %fusion.6, bf16[1,512,224]{1,2,0:T(8,128)(2,1)S(1)} %copy-done.4, ...), kind=kOutput, calls=%fused_computation | convolution fusion | flops 479870976 | bytes 3475456 | tf_op jit(solution)/shard_map/dot_general | solution.py:23
  143.7 7.5 %all-to-all-done.4 = bf16[8,104,512]{2,1,0:T(8,128)(2,1)S(1)} async-done(((bf16[8,104,512]{2,1,0:T(8,128)(2,1)}), bf16[8,104,512]{2,1,0:T(8,128)(2,1)S(1)}, u32[]{:S(2)}, u32[]{:S(2)}) %all-to-all-start.4) | async-done | bytes 852000 | tf_op jit(solution)/shard_map/all_to_all | solution.py:14
  151.2 0.1 reduce_sum.114
  151.3 0.7 fusion.60
  152.0 6.5 %all-to-all-start.5 = ((bf16[4,32,512]{2,1,0:T(8,128)(2,1)}), bf16[4,32,512]{2,1,0:T(8,128)(2,1)S(1)}, u32[]{:S(2)}, u32[]{:S(2)}) async-start(bf16[4,32,512]{2,1,0:T(8,128)(2,1)} %fusion.60), calls=%async_computation.5 | async-start | bytes 262144 | tf_op jit(solution)/shard_map/all_to_all | solution.py:14
  158.6 0.1 constant_dynamic-slice_fusion.3
  158.7 4.7 %all-to-all-done.5 = bf16[4,32,512]{2,1,0:T(8,128)(2,1)S(1)} async-done(((bf16[4,32,512]{2,1,0:T(8,128)(2,1)}), bf16[4,32,512]{2,1,0:T(8,128)(2,1)S(1)}, u32[]{:S(2)}, u32[]{:S(2)}) %all-to-all-start.5) | async-done | bytes 131104 | tf_op jit(solution)/shard_map/all_to_all | solution.py:14
  163.4 0.2 convolution_reduce_fusion
  163.7 0.7 pad_maximum_fusion.10
  164.4 5.3 %all-to-all-start.6 = ((bf16[16,32,128]{2,1,0:T(8,128)(2,1)}), bf16[16,32,128]{2,1,0:T(8,128)(2,1)S(1)}, u32[]{:S(2)}, u32[]{:S(2)}) async-start(bf16[16,32,128]{2,1,0:T(8,128)(2,1)} %pad_maximum_fusion.10), calls=%async_computation.6 | async-start | bytes 262144 | tf_op jit(solution)/shard_map/all_to_all | solution.py:14
  169.8 0.9 fusion.58
  170.7 8.3 %all-to-all-done.6 = bf16[16,32,128]{2,1,0:T(8,128)(2,1)S(1)} async-done(((bf16[16,32,128]{2,1,0:T(8,128)(2,1)}), bf16[16,32,128]{2,1,0:T(8,128)(2,1)S(1)}, u32[]{:S(2)}, u32[]{:S(2)}) %all-to-all-start.6) | async-done | bytes 131104 | tf_op jit(solution)/shard_map/all_to_all | solution.py:14
  179.0 1.1 fusion.7
  180.1 0.6 subtract_multiply_fusion
  180.6 1.1 pad_maximum_fusion.2
  181.7 0.1 dynamic-slice_bitcast_fusion.3
  181.8 1.5 maximum_bitcast_fusion
  (80 shorter events, 0.6 us)
Async XLA Ops:
  0.6 2.7 %copy-start = (bf16[256,128]{1,0:T(8,128)(2,1)S(1)}, bf16[256,128]{1,0:T(8,128)(2,1)}, u32[]{:S(2)}) copy-start(bf16[256,128]{1,0:T(8,128)(2,1)} %param.8) | copy-start | bytes 196612
  1.6 15.7 %copy-start.16 = (f32[1,256]{1,0:T(1,128)S(1)}, f32[1,256]{1,0:T(1,128)}, u32[]{:S(2)}) copy-start(f32[1,256]{1,0:T(1,128)} %param.10) | copy-start | bytes 3076
  5.4 22.0 %all-to-all-start = ((bf16[16,48,128]{2,1,0:T(8,128)(2,1)}), bf16[16,48,128]{2,1,0:T(8,128)(2,1)S(1)}, u32[]{:S(2)}, u32[]{:S(2)}) async-start(bf16[16,48,128]{2,1,0:T(8,128)(2,1)} %pad_maximum_fusion.6), calls=%async_computation | async-start | bytes 393216 | tf_op jit(solution)/shard_map/all_to_all | solution.py:14
  38.7 31.8 %all-to-all-start.2 = ((bf16[8,104,512]{2,1,0:T(8,128)(2,1)}), bf16[8,104,512]{2,1,0:T(8,128)(2,1)S(1)}, u32[]{:S(2)}, u32[]{:S(2)}) async-start(bf16[8,104,512]{2,1,0:T(8,128)(2,1)} %broadcast_in_dim.101), calls=%async_computation.2 | async-start | bytes 1703936 | tf_op jit(solution)/shard_map/all_to_all | solution.py:14
  70.5 10.2 %copy-start.1 = (bf16[1,224,2048]{2,1,0:T(8,128)(2,1)S(1)}, bf16[1,224,2048]{2,1,0:T(8,128)(2,1)}, u32[]{:S(2)}) copy-start(bf16[1,224,2048]{2,1,0:T(8,128)(2,1)} %param.15) | copy-start | bytes 2752516
  72.1 15.8 %copy-start.2 = (bf16[1,224,2048]{2,1,0:T(8,128)(2,1)S(1)}, bf16[1,224,2048]{2,1,0:T(8,128)(2,1)}, u32[]{:S(2)}) copy-start(bf16[1,224,2048]{2,1,0:T(8,128)(2,1)} %param.14) | copy-start | bytes 2752516
  72.1 21.6 %collective-permute-start = (bf16[512,512]{0,1:T(8,128)(2,1)}, bf16[512,512]{0,1:T(8,128)(2,1)}, u32[]{:S(2)}, u32[]{:S(2)}) collective-permute-start(bf16[512,512]{0,1:T(8,128)(2,1)} %fusion.6), channel_id=1, source_target_pairs={{0,128},{128,256},{256,384},{384,0},{1,129},{129,257},{257,385},{3... | collective-permute-start | bytes 1572872 | tf_op jit(solution)/shard_map/ppermute | solution.py:40
  74.5 24.9 %collective-permute-start.1 = (bf16[512,512]{0,1:T(8,128)(2,1)}, bf16[512,512]{0,1:T(8,128)(2,1)}, u32[]{:S(2)}, u32[]{:S(2)}) collective-permute-start(bf16[512,512]{0,1:T(8,128)(2,1)} %fusion.6), channel_id=1, source_target_pairs={{0,256},{128,384},{256,0},{384,128},{1,257},{129,385},{257,1},{385... | collective-permute-start | bytes 1572872 | tf_op jit(solution)/shard_map/ppermute | solution.py:40
  78.2 24.7 %collective-permute-start.2 = (bf16[512,512]{0,1:T(8,128)(2,1)}, bf16[512,512]{0,1:T(8,128)(2,1)}, u32[]{:S(2)}, u32[]{:S(2)}) collective-permute-start(bf16[512,512]{0,1:T(8,128)(2,1)} %fusion.6), channel_id=1, source_target_pairs={{0,384},{128,0},{256,128},{384,256},{1,385},{129,1},{257,129},{385... | collective-permute-start | bytes 1572872 | tf_op jit(solution)/shard_map/ppermute | solution.py:40
  81.7 39.5 %collective-permute-start.6 = (bf16[224,512]{1,0:T(8,128)(2,1)}, bf16[224,512]{1,0:T(8,128)(2,1)}, u32[]{:S(2)}, u32[]{:S(2)}) collective-permute-start(bf16[224,512]{1,0:T(8,128)(2,1)} %get-tuple-element.33), channel_id=1, source_target_pairs={{0,128},{128,256},{256,384},{384,0},{1,129},{129,257},{257,385},{3... | collective-permute-start | bytes 688136 | tf_op jit(solution)/shard_map/ppermute | solution.py:40
  84.4 36.7 %collective-permute-start.7 = (bf16[224,512]{1,0:T(8,128)(2,1)}, bf16[224,512]{1,0:T(8,128)(2,1)}, u32[]{:S(2)}, u32[]{:S(2)}) collective-permute-start(bf16[224,512]{1,0:T(8,128)(2,1)} %get-tuple-element.35), channel_id=1, source_target_pairs={{0,256},{128,384},{256,0},{384,128},{1,257},{129,385},{257,1},{385... | collective-permute-start | bytes 688136 | tf_op jit(solution)/shard_map/ppermute | solution.py:40
  89.9 13.0 %copy-start.3 = (bf16[1,512,224]{1,2,0:T(8,128)(2,1)S(1)}, bf16[1,512,224]{1,2,0:T(8,128)(2,1)}, u32[]{:S(2)}) copy-start(bf16[1,512,224]{1,2,0:T(8,128)(2,1)} %param.13) | copy-start | bytes 688132
  89.9 13.0 %copy-start.6 = (bf16[1,512,224]{1,2,0:T(8,128)(2,1)S(1)}, bf16[1,512,224]{1,2,0:T(8,128)(2,1)}, u32[]{:S(2)}) copy-start(bf16[1,512,224]{1,2,0:T(8,128)(2,1)} %param.12) | copy-start | bytes 688132
  89.9 13.0 %copy-start.13 = (bf16[224,512]{1,0:T(8,128)(2,1)S(1)}, bf16[224,512]{1,0:T(8,128)(2,1)}, u32[]{:S(2)}) copy-start(bf16[224,512]{1,0:T(8,128)(2,1)} %get-tuple-element.44) | copy-start | bytes 688132
  89.9 13.0 %copy-start.14 = (bf16[224,512]{1,0:T(8,128)(2,1)S(1)}, bf16[224,512]{1,0:T(8,128)(2,1)}, u32[]{:S(2)}) copy-start(bf16[224,512]{1,0:T(8,128)(2,1)} %get-tuple-element.45) | copy-start | bytes 688132
  89.9 13.0 %copy-start.15 = (bf16[224,512]{1,0:T(8,128)(2,1)S(1)}, bf16[224,512]{1,0:T(8,128)(2,1)}, u32[]{:S(2)}) copy-start(bf16[224,512]{1,0:T(8,128)(2,1)} %get-tuple-element.46) | copy-start | bytes 688132
  89.9 35.4 %all-to-all-start.3 = ((bf16[8,96,512]{2,1,0:T(8,128)(2,1)}), bf16[8,96,512]{2,1,0:T(8,128)(2,1)S(1)}, u32[]{:S(2)}, u32[]{:S(2)}) async-start(bf16[8,96,512]{2,1,0:T(8,128)(2,1)} %broadcast_in_dim.106), calls=%async_computation.3 | async-start | bytes 1572864 | tf_op jit(solution)/shard_map/all_to_all | solution.py:14
  93.8 27.4 %collective-permute-start.8 = (bf16[224,512]{1,0:T(8,128)(2,1)}, bf16[224,512]{1,0:T(8,128)(2,1)S(1)}, u32[]{:S(2)}, u32[]{:S(2)}) collective-permute-start(bf16[224,512]{1,0:T(8,128)(2,1)} %get-tuple-element.34), channel_id=1, source_target_pairs={{0,384},{128,0},{256,128},{384,256},{1,385},{129,1},{257,129},{385... | collective-permute-start | bytes 688136 | tf_op jit(solution)/shard_map/ppermute | solution.py:40
  120.9 1.0 copy-start.12
  120.9 3.3 %copy-start.9 = (bf16[224,512]{1,0:T(8,128)(2,1)}, bf16[224,512]{1,0:T(8,128)(2,1)S(1)}, u32[]{:S(2)}) copy-start(bf16[224,512]{1,0:T(8,128)(2,1)S(1)} %get-tuple-element.41) | copy-start | bytes 688132
  121.0 3.3 %copy-start.10 = (bf16[224,512]{1,0:T(8,128)(2,1)}, bf16[224,512]{1,0:T(8,128)(2,1)S(1)}, u32[]{:S(2)}) copy-start(bf16[224,512]{1,0:T(8,128)(2,1)S(1)} %get-tuple-element.42) | copy-start | bytes 688132
  121.0 3.3 %copy-start.11 = (bf16[224,512]{1,0:T(8,128)(2,1)}, bf16[224,512]{1,0:T(8,128)(2,1)S(1)}, u32[]{:S(2)}) copy-start(bf16[224,512]{1,0:T(8,128)(2,1)S(1)} %get-tuple-element.43) | copy-start | bytes 688132
  121.2 0.7 copy-start.17
  125.3 25.9 %all-to-all-start.4 = ((bf16[8,104,512]{2,1,0:T(8,128)(2,1)}), bf16[8,104,512]{2,1,0:T(8,128)(2,1)S(1)}, u32[]{:S(2)}, u32[]{:S(2)}) async-start(bf16[8,104,512]{2,1,0:T(8,128)(2,1)} %fusion.33), calls=%async_computation.4 | async-start | bytes 1703936 | tf_op jit(solution)/shard_map/all_to_all | solution.py:14
  131.2 10.1 %copy-start.4 = (bf16[1,512,224]{1,2,0:T(8,128)(2,1)S(1)}, bf16[1,512,224]{1,2,0:T(8,128)(2,1)}, u32[]{:S(2)}) copy-start(bf16[1,512,224]{1,2,0:T(8,128)(2,1)} %param.13) | copy-start | bytes 688132
  131.2 10.1 %copy-start.7 = (bf16[1,512,224]{1,2,0:T(8,128)(2,1)S(1)}, bf16[1,512,224]{1,2,0:T(8,128)(2,1)}, u32[]{:S(2)}) copy-start(bf16[1,512,224]{1,2,0:T(8,128)(2,1)} %param.12) | copy-start | bytes 688132
  132.1 38.5 %collective-permute-start.3 = (bf16[224,512]{1,0:T(8,128)(2,1)}, bf16[224,512]{1,0:T(8,128)(2,1)S(1)}, u32[]{:S(2)}, u32[]{:S(2)}) collective-permute-start(bf16[224,512]{1,0:T(8,128)(2,1)} %get-tuple-element.38), channel_id=1, source_target_pairs={{0,384},{128,0},{256,128},{384,256},{1,385},{129,1},{257,129},{385... | collective-permute-start | bytes 688136 | tf_op jit(solution)/shard_map/ppermute | solution.py:40
  136.8 33.8 %collective-permute-start.4 = (bf16[224,512]{1,0:T(8,128)(2,1)}, bf16[224,512]{1,0:T(8,128)(2,1)S(1)}, u32[]{:S(2)}, u32[]{:S(2)}) collective-permute-start(bf16[224,512]{1,0:T(8,128)(2,1)} %get-tuple-element.37), channel_id=1, source_target_pairs={{0,256},{128,384},{256,0},{384,128},{1,257},{129,385},{257,1},{385... | collective-permute-start | bytes 688136 | tf_op jit(solution)/shard_map/ppermute | solution.py:40
  139.4 31.3 %collective-permute-start.5 = (bf16[224,512]{1,0:T(8,128)(2,1)}, bf16[224,512]{1,0:T(8,128)(2,1)}, u32[]{:S(2)}, u32[]{:S(2)}) collective-permute-start(bf16[224,512]{1,0:T(8,128)(2,1)} %get-tuple-element.36), channel_id=1, source_target_pairs={{0,128},{128,256},{256,384},{384,0},{1,129},{129,257},{257,385},{3... | collective-permute-start | bytes 688136 | tf_op jit(solution)/shard_map/ppermute | solution.py:40
  152.0 11.4 %all-to-all-start.5 = ((bf16[4,32,512]{2,1,0:T(8,128)(2,1)}), bf16[4,32,512]{2,1,0:T(8,128)(2,1)S(1)}, u32[]{:S(2)}, u32[]{:S(2)}) async-start(bf16[4,32,512]{2,1,0:T(8,128)(2,1)} %fusion.60), calls=%async_computation.5 | async-start | bytes 262144 | tf_op jit(solution)/shard_map/all_to_all | solution.py:14
  158.6 11.1 %copy-start.5 = (bf16[1,512,224]{1,2,0:T(8,128)(2,1)S(1)}, bf16[1,512,224]{1,2,0:T(8,128)(2,1)}, u32[]{:S(2)}) copy-start(bf16[1,512,224]{1,2,0:T(8,128)(2,1)} %param.13) | copy-start | bytes 688132
  158.7 11.1 %copy-start.8 = (bf16[1,512,224]{1,2,0:T(8,128)(2,1)S(1)}, bf16[1,512,224]{1,2,0:T(8,128)(2,1)}, u32[]{:S(2)}) copy-start(bf16[1,512,224]{1,2,0:T(8,128)(2,1)} %param.12) | copy-start | bytes 688132
  164.4 14.5 %all-to-all-start.6 = ((bf16[16,32,128]{2,1,0:T(8,128)(2,1)}), bf16[16,32,128]{2,1,0:T(8,128)(2,1)S(1)}, u32[]{:S(2)}, u32[]{:S(2)}) async-start(bf16[16,32,128]{2,1,0:T(8,128)(2,1)} %pad_maximum_fusion.10), calls=%async_computation.6 | async-start | bytes 262144 | tf_op jit(solution)/shard_map/all_to_all | solution.py:14

commit v4 on v3

--- a/solution.py
+++ b/solution.py
@@ -14,11 +14,6 @@
     return lax.all_to_all(x, axis, 0, 0, tiled=True)
 
 
-def to_all(x, axis):
-    size = lax.axis_size(axis)
-    return exchange(jnp.broadcast_to(x[None], (size, *x.shape)), axis)
-
-
 def dot(a, b, ca, cb):
     return lax.dot_general(a, b, (((ca,), (cb,)), ((), ())), preferred_element_type=F32)
 
@@ -45,6 +40,18 @@
     for k in range(1, len(blocks)):
         came.append(shift(blocks[k], sign * k))
     return came
+
+
+def to_quarters(x, ny):
+    size = x.shape[0] * ny
+    sent = jnp.broadcast_to(x[:, None], (x.shape[0], ny, *x.shape[1:]))
+    return exchange(sent.reshape(size, *x.shape[1:]), (X, Y))
+
+
+def joined(x, pieces):
+    size, rows, lane = x.shape
+    x = x.reshape(size, pieces, rows // pieces, lane).transpose(0, 2, 1, 3)
+    return x.reshape(size * rows // pieces, pieces * lane)
 
 
 def back_in_x(blocks, xi):
@@ -80,7 +87,7 @@
     units = gate_pre.shape[2]
     quarter = ne // nx
     part = quarter * width_dev
-    lane = 128
+    lane = width_dev
 
     firsts = jnp.sum((chosen < shard * tok_dev).astype(jnp.int32), axis=1)
     ends = jnp.sum((chosen < (shard + 1) * tok_dev).astype(jnp.int32), axis=1)
@@ -95,12 +102,10 @@
     token_iota = jnp.arange(tok_dev, dtype=jnp.int32)
     picker = onehot(local_rows[:, :, None] == token_iota[None, None, :])
 
-    flat_pick = picker.reshape(ne * (cap + PAD), tok_dev)
-    sent_grad = dot(flat_pick, grad_out, 1, 0).astype(BF).reshape(ne, cap + PAD, width_dev)
-    sent_input = dot(flat_pick, saved_inputs, 1, 0).astype(BF).reshape(ne, cap + PAD, width_dev)
-    sent = jnp.concatenate([sent_grad[:, :cap], sent_input[:, :cap]], axis=1)
-    rows = exchange(sent, E)
-    rows = rows.reshape(nx, quarter, 2 * cap, width_dev)
+    sent_pick = picker[:, :cap].reshape(ne * cap, tok_dev)
+    both = jnp.concatenate([grad_out, saved_inputs], axis=1)
+    sent = dot(sent_pick, both, 1, 0).astype(BF).reshape(ne, cap, 2 * width_dev)
+    rows = exchange(sent, E).reshape(nx, quarter, cap, 2 * width_dev)
 
     down_part = jnp.concatenate([quarter_at(w_down[0], (xi + nx - k) % nx, nx) for k in range(nx)], axis=1)
     up_part = [quarter_at(w_up[0], (xi + k) % nx, nx) for k in range(nx)]
@@ -111,21 +116,19 @@
     own_hit = onehot(own_rows[:, None] == token_iota[None, :])
     gate_row = dot(router_probs.astype(BF), own_hit, 1, 1).astype(BF)
     gate_tile = jnp.broadcast_to(
-        jnp.pad(gate_row, ((0, PAD - 1), (0, 0)))[None, None], (nx, quarter, PAD, lane)
-    )
-    rows = exchange(jnp.concatenate([rows, gate_tile], axis=2), X)
+        jnp.pad(gate_row, ((0, PAD - 1), (0, 0)))[None], (nx, PAD, lane)
+    )
+    grads = jnp.concatenate([rows[..., :lane].reshape(nx, quarter * cap, lane), gate_tile], axis=1)
+    inputs = rows[..., lane:].reshape(nx, quarter * cap, lane)
+
     gate_value = gate_pre[0].T.astype(F32)
     up_value = up_pre[0].T.astype(F32)
     sig = jax.nn.sigmoid(gate_value)
     active = gate_value * sig
     hidden = active * up_value
 
-    grads = rows[:, :, :cap].transpose(0, 2, 1, 3).reshape(nx * cap, part)
-    inputs = rows[:, :, cap : 2 * cap].transpose(0, 2, 1, 3).reshape(nx * cap, part)
-    gates = jnp.pad(rows[:, 0, 2 * cap], ((0, PAD - nx), (0, part - lane)))
-    block = nx * cap + PAD
-    grads_all = to_all(jnp.concatenate([grads, gates], axis=0), Y)
-    inputs_all = to_all(inputs, Y)
+    grads_all = to_quarters(grads, ny)
+    inputs_all = to_quarters(inputs, ny)
 
     chosen_row = lax.dynamic_index_in_dim(chosen, ei, 0, keepdims=True)
     owner = chosen_row // tok_dev
@@ -134,15 +137,12 @@
     within = lanes_of(1, slots) - jnp.sum(
         jnp.where(owner == shard_col, before, 0), axis=0, keepdims=True
     )
-    owner_x, owner_y = owner // ny, owner % ny
-    spot = owner_x * cap + within
-    place_block = onehot(rows_of(ny * block, slots) == owner_y * block + spot)
-    place_rows = onehot(rows_of(ny * nx * cap, slots) == owner_y * (nx * cap) + spot)
-    owner_hit = rows_of(shards, slots) == owner_y * nx + owner_x
+    place = onehot(rows_of(shards * cap, slots) == owner * cap + within)
+    owner_hit = owner == shard_col
     within_hit = onehot(rows_of(lane, slots) == within)
 
-    grads_slots = dot(place_block, grads_all.reshape(ny * block, part), 0, 0).astype(BF)
-    gates_all = grads_all[:, nx * cap : nx * cap + nx, :lane].reshape(shards, lane)
+    grads_slots = dot(place, joined(grads_all[:, : quarter * cap], quarter), 0, 0).astype(BF)
+    gates_all = grads_all[:, quarter * cap]
     gate_slot = jnp.sum(
         jnp.where(owner_hit, dot(gates_all, within_hit, 1, 0), 0.0), axis=0, keepdims=True
     )
@@ -161,35 +161,36 @@
         [quarter_at(grad_down, (xi + nx - q) % nx, nx) for q in range(nx)], axis=1
     )
     dx = dot(up_all, up_part, 0, 0).astype(BF)
-    dx_rows = dot(place_rows, dx, 1, 0).astype(BF).reshape(ny, nx * cap, part)
+    dx_rows = dot(place, dx, 1, 0).astype(BF).reshape(shards, cap, quarter, lane)
+    dx_rows = dx_rows.transpose(0, 2, 1, 3).reshape(shards, quarter * cap, lane)
     dots_own = jnp.where(owner_hit, dots, 0.0).astype(BF)
-    dots_rows = dot(dots_own, within_hit, 1, 1).astype(BF).reshape(ny, nx, lane)
-    dots_rows = jnp.pad(dots_rows, ((0, 0), (0, PAD - nx), (0, part - lane)))
-    dx_back = exchange(jnp.concatenate([dx_rows, dots_rows], axis=1), Y)
-    inputs_slots = dot(place_rows, inputs_all.reshape(-1, part), 0, 0).astype(BF)
+    dots_rows = dot(dots_own, within_hit, 1, 1).astype(BF)
+    dots_rows = jnp.pad(dots_rows[:, None], ((0, 0), (0, PAD - 1), (0, 0)))
+    dx_back = exchange(jnp.concatenate([dx_rows, dots_rows], axis=1), (X, Y))
+    inputs_slots = dot(place, joined(inputs_all, quarter), 0, 0).astype(BF)
     grad_up = dot(up_all, inputs_slots, 1, 0).astype(BF).reshape(nx, units, part)
     up_home = over_x(grad_up, -1)
-    dx_sum = jnp.sum(dx_back.astype(F32), axis=0).astype(BF)
-    dots_sum = dx_sum[nx * cap : nx * cap + nx].reshape(nx, 1, part)
-    dx_sum = jnp.concatenate(
-        [dx_sum[: nx * cap].reshape(nx, cap, part), jnp.pad(dots_sum, ((0, 0), (0, PAD - 1), (0, 0)))],
-        axis=1,
-    )
-    dx_own = exchange(dx_sum, X)
-    gate_tokens = jnp.sum(dot(dx_own[:, cap, :lane], own_hit, 1, 0), axis=0, keepdims=True)
+    dx_sum = jnp.sum(dx_back.reshape(nx, ny, -1, lane).astype(F32), axis=1)
+    dots_sum = jnp.sum(dx_sum[:, quarter * cap], axis=0, keepdims=True)
+    gate_tokens = lax.dot_general(
+        dots_sum,
+        own_hit.astype(F32),
+        (((1,), (0,)), ((), ())),
+        precision=lax.Precision.HIGHEST,
+        preferred_element_type=F32,
+    )
     product = router_probs * gate_tokens
     high = lax.reduce_precision(product, 8, 7)
     low = product - high
     tail = jnp.concatenate([high, low], axis=0).astype(BF).reshape(-1, lane)
     tail = jnp.pad(tail, ((0, PAD - tail.shape[0]), (0, 0)))
-    to_experts = dx_own[:, :cap].reshape(nx, cap, quarter, width_dev).transpose(0, 2, 1, 3)
-    to_experts = to_experts.reshape(ne, cap, width_dev)
+    to_experts = dx_sum[:, : quarter * cap].astype(BF).reshape(ne, cap, width_dev)
     spread = exchange(
         jnp.concatenate([to_experts, jnp.broadcast_to(tail[None], (ne, PAD, lane))], axis=1), E
     )
     up_home, spread = lax.optimization_barrier((up_home, spread))
     grad_up = in_turn(up_home, xi)
-    grad_tokens = dot(flat_pick, spread.reshape(-1, width_dev), 0, 0).astype(BF)
+    grad_tokens = dot(picker.reshape(-1, tok_dev), spread.reshape(-1, width_dev), 0, 0).astype(BF)
     pieces = jnp.sum(spread[:, cap : cap + 2 * tok_dev // lane].astype(F32), axis=0)
     router_sum = jnp.sum(pieces.reshape(2, 1, tok_dev), axis=0)
     grad_logits = router_probs * (gate_tokens - router_sum)

time: 184 us -> 176 us (0.957)
  waiting for transfers between devices: 59.5 us -> 50.6 us
  starting transfers between devices: 65.6 us -> 73.2 us
  blocking collectives: 25.8 us -> 18.9 us
    all_to_all x1 -> x0, blocking collectives: 10.2 us -> none  [exchange(): return lax.all_to_all(x, axis, 0, 0, tiled=True)]
    all_to_all x6 -> x5, waiting for transfers between devices: 54.4 us -> 44.3 us  [exchange(): return lax.all_to_all(x, axis, 0, 0, tiled=True)]
    all_to_all x6 -> x5, starting transfers between devices: 37.8 us -> 44.8 us  [exchange(): return lax.all_to_all(x, axis, 0, 0, tiled=True)]
    all_gather x1, blocking collectives: 15.7 us -> 18.9 us  [local(): up_all = lax.all_gather(up_grad, X)]
    dot_general x12 -> x10, matrix products: 14.2 us -> 14.4 us  [dot(): lax.dot_general(a, b, (((ca,), (cb,)), ((), ())), preferred_element_type=...]
  transfers between devices with their start and end apart: 15 -> 14, of which waited for: 7 -> 5; matrix products, arithmetic and copies ran while one was open for 10% -> 11% of each run, Pallas kernels for 0% -> 0%
where the time goes in v4:
time: 176 us; the launch traced here: 174 us
  starting transfers between devices  73.2 us (42%)
  waiting for transfers between devices  50.6 us (29%)
  blocking collectives  18.9 us (11%)
  matrix products  14.6 us (8%)
  other arithmetic  9.02 us (5%)
  local copies, waits for them, and re-layouts  6.89 us (4%)
    all_to_all x5, starting transfers between devices, exchange(): return lax.all_to_all(x, axis, 0, 0, tiled=True)  44.8 us
    all_to_all x5, waiting for transfers between devices, exchange(): return lax.all_to_all(x, axis, 0, 0, tiled=True)  44.3 us
    ppermute x9, starting transfers between devices, shift(): return lax.ppermute(x, X, [(i, (i + by) % size) for i in range(size)])  28.4 us
    all_gather x1, blocking collectives, local(): up_all = lax.all_gather(up_grad, X)  18.9 us
    dot_general x10, matrix products, dot(): lax.dot_general(a, b, (((ca,), (cb,)), ((), ())), preferred_element_type=...  14.4 us
    ppermute x9, waiting for transfers between devices, shift(): return lax.ppermute(x, X, [(i, (i + by) % size) for i in range(size)])  6.3 us
  transfers between devices with their start and end apart: 14, of which 5 were waited for; matrix products, arithmetic and copies ran while one was open for 11% of the time, Pallas kernels for 0%

profile of v4, /device:TPU:1, one launch (start us, length us, event | category | flops | bytes accessed | tf_op | source)
XLA Modules:
  0.0 174.4 jit_solution(15918969479598103469)
XLA Ops:
  0.7 0.9 convert_reduce_fusion.3
  1.5 0.1 iota_add_fusion
  1.6 1.2 select_reduce_fusion
  2.8 0.1 subtract_select_fusion
  2.9 0.1 iota_compare_fusion.14
  3.1 1.8 %convolution_convert_fusion.3 = bf16[384,256]{1,0:T(8,128)(2,1)} fusion(pred[384,256]{1,0:T(8,128)(4,1)S(1)} %bitcast.180, bf16[256,128]{1,0:T(8,128)(2,1)} %param.9, bf16[256,128]{1,0:T(8,128)(2,1)} %param.8), kind=kOutput, calls=%fused_computation.14 | convolution fusion | flops 50692096 | bytes 425984 | tf_op jit(solution)/shard_map/dot_general | solution.py:18
  4.9 11.8 %all-to-all-start = ((bf16[16,24,256]{2,1,0:T(8,128)(2,1)}), bf16[16,24,256]{2,1,0:T(8,128)(2,1)S(1)}, u32[]{:S(2)}, u32[]{:S(2)}) async-start(bf16[16,24,256]{2,1,0:T(8,128)(2,1)} %bitcast.2), calls=%async_computation | async-start | bytes 393216 | tf_op jit(solution)/shard_map/all_to_all | solution.py:14
  16.7 0.2 fusion.11
  16.9 10.0 %all-to-all-done = bf16[16,24,256]{2,1,0:T(8,128)(2,1)S(1)} async-done(((bf16[16,24,256]{2,1,0:T(8,128)(2,1)}), bf16[16,24,256]{2,1,0:T(8,128)(2,1)S(1)}, u32[]{:S(2)}, u32[]{:S(2)}) %all-to-all-start) | async-done | bytes 196640 | tf_op jit(solution)/shard_map/all_to_all | solution.py:14
  27.0 1.0 broadcast_in_dim.99
  28.0 9.7 %all-to-all-start.1 = ((bf16[32,104,128]{2,1,0:T(8,128)(2,1)}), bf16[32,104,128]{2,1,0:T(8,128)(2,1)S(1)}, u32[]{:S(2)}, u32[]{:S(2)}) async-start(bf16[32,104,128]{2,1,0:T(8,128)(2,1)} %bitcast.8), calls=%async_computation.1 | async-start | bytes 1703936 | tf_op jit(solution)/shard_map/all_to_all | solution.py:14
  37.7 0.7 and_select_fusion
  38.5 0.1 convert_reduce_fusion.1
  38.6 0.1 select_reduce_fusion.1
  38.7 0.7 subtract_add_fusion
  39.4 20.8 %all-to-all-done.1 = bf16[32,104,128]{2,1,0:T(8,128)(2,1)S(1)} async-done(((bf16[32,104,128]{2,1,0:T(8,128)(2,1)}), bf16[32,104,128]{2,1,0:T(8,128)(2,1)S(1)}, u32[]{:S(2)}, u32[]{:S(2)}) %all-to-all-start.1) | async-done | bytes 852000 | tf_op jit(solution)/shard_map/all_to_all | solution.py:14
  60.2 0.1 slice.56
  60.2 0.3 copy.29
  60.6 1.4 fusion.5
  62.0 2.0 %collective-permute-start = (bf16[512,512]{0,1:T(8,128)(2,1)}, bf16[512,512]{0,1:T(8,128)(2,1)}, u32[]{:S(2)}, u32[]{:S(2)}) collective-permute-start(bf16[512,512]{0,1:T(8,128)(2,1)} %fusion.5), channel_id=1, source_target_pairs={{0,128},{128,256},{256,384},{384,0},{1,129},{129,257},{257,385},{3... | collective-permute-start | bytes 1572872 | tf_op jit(solution)/shard_map/ppermute | solution.py:35
  64.0 3.9 %collective-permute-start.1 = (bf16[512,512]{0,1:T(8,128)(2,1)}, bf16[512,512]{0,1:T(8,128)(2,1)}, u32[]{:S(2)}, u32[]{:S(2)}) collective-permute-start(bf16[512,512]{0,1:T(8,128)(2,1)} %fusion.5), channel_id=1, source_target_pairs={{0,256},{128,384},{256,0},{384,128},{1,257},{129,385},{257,1},{385... | collective-permute-start | bytes 1572872 | tf_op jit(solution)/shard_map/ppermute | solution.py:35
  67.9 2.9 %collective-permute-start.2 = (bf16[512,512]{0,1:T(8,128)(2,1)}, bf16[512,512]{0,1:T(8,128)(2,1)}, u32[]{:S(2)}, u32[]{:S(2)}) collective-permute-start(bf16[512,512]{0,1:T(8,128)(2,1)} %fusion.5), channel_id=1, source_target_pairs={{0,384},{128,0},{256,128},{384,256},{1,385},{129,1},{257,129},{385... | collective-permute-start | bytes 1572872 | tf_op jit(solution)/shard_map/ppermute | solution.py:35
  70.9 0.9 dynamic-slice_bitcast_fusion.7
  71.7 2.4 %collective-permute-start.6 = (bf16[224,512]{1,0:T(8,128)(2,1)}, bf16[224,512]{1,0:T(8,128)(2,1)}, u32[]{:S(2)}, u32[]{:S(2)}) collective-permute-start(bf16[224,512]{1,0:T(8,128)(2,1)} %get-tuple-element.26), channel_id=1, source_target_pairs={{0,128},{128,256},{256,384},{384,0},{1,129},{129,257},{257,385},{3... | collective-permute-start | bytes 688136 | tf_op jit(solution)/shard_map/ppermute | solution.py:35
  74.1 3.5 %collective-permute-start.7 = (bf16[224,512]{1,0:T(8,128)(2,1)S(1)}, bf16[224,512]{1,0:T(8,128)(2,1)}, u32[]{:S(2)}, u32[]{:S(2)}) collective-permute-start(bf16[224,512]{1,0:T(8,128)(2,1)S(1)} %get-tuple-element.28), channel_id=1, source_target_pairs={{0,256},{128,384},{256,0},{384,128},{1,257},{129,385},{257,1},{385... | collective-permute-start | bytes 688136 | tf_op jit(solution)/shard_map/ppermute | solution.py:35
  77.7 0.9 dynamic-slice_bitcast_fusion.15
  78.5 1.0 broadcast_in_dim.104
  79.5 7.4 %all-to-all-start.2 = ((bf16[32,96,128]{2,1,0:T(8,128)(2,1)}), bf16[32,96,128]{2,1,0:T(8,128)(2,1)S(1)}, u32[]{:S(2)}, u32[]{:S(2)}) async-start(bf16[32,96,128]{2,1,0:T(8,128)(2,1)} %bitcast.27), calls=%async_computation.2 | async-start | bytes 1572864 | tf_op jit(solution)/shard_map/all_to_all | solution.py:14
  86.9 0.2 fusion.8
  87.1 4.4 %collective-permute-start.8 = (bf16[224,512]{1,0:T(8,128)(2,1)S(1)}, bf16[224,512]{1,0:T(8,128)(2,1)S(1)}, u32[]{:S(2)}, u32[]{:S(2)}) collective-permute-start(bf16[224,512]{1,0:T(8,128)(2,1)S(1)} %get-tuple-element.27), channel_id=1, source_target_pairs={{0,384},{128,0},{256,128},{384,256},{1,385},{129,1},{257,129},{385... | collective-permute-start | bytes 688136 | tf_op jit(solution)/shard_map/ppermute | solution.py:35
  91.6 6.3 %collective-permute-done.2 = bf16[512,512]{0,1:T(8,128)(2,1)} collective-permute-done((bf16[512,512]{0,1:T(8,128)(2,1)}, bf16[512,512]{0,1:T(8,128)(2,1)}, u32[]{:S(2)}, u32[]{:S(2)}) %collective-permute-start.2) | collective-permute-done | bytes 524320 | tf_op jit(solution)/shard_map/ppermute | solution.py:35
  97.8 2.5 %multiply_reduce_fusion = (bf16[512]{0:T(512)(128)(2,1)S(1)}, bf16[224,512]{1,0:T(8,128)(2,1)S(1)}, f32[224,512]{1,0:T(8,128)S(1)}) fusion(bf16[1,512,224]{1,2,0:T(8,128)(2,1)S(1)} %copy-done.2, bf16[1,512,224]{1,2,0:T(8,128)(2,1)S(1)} %copy-done.5, f32[512]{0:T(512)S(1)} %fusion.8, bf16[512,512]{0,1:T(8,128)(2,1)} %collective-permute-done.2, ...), kind=kOutput, calls=%fused_computation.73 | convolution fusion | flops 483196416 | bytes 4164608 | tf_op jit(solution)/shard_map/dot_general | solution.py:18
  100.3 18.9 %all-gather = bf16[896,512]{1,0:T(8,128)(2,1)S(1)} all-gather(bf16[224,512]{1,0:T(8,128)(2,1)S(1)} %get-tuple-element.42), channel_id=2, replica_groups=mesh['dp_0'=4,'dp_1'=8,'expert'=16] {'dp_0'}, dimensions={0}, use_global_device_ids=true | all-gather | bytes 1146880 | tf_op jit(solution)/shard_map/all_gather | solution.py:155
  119.2 0.8 dynamic-slice_bitcast_fusion.11
  120.1 0.2 copy-done.8
  120.2 2.5 %fusion.4 = bf16[768,512]{1,0:T(8,128)(2,1)S(1)} fusion(bf16[224,512]{1,0:T(8,128)(2,1)S(1)} %collective-permute-done.8, bf16[224,512]{1,0:T(8,128)(2,1)} %collective-permute-done.7, bf16[224,512]{1,0:T(8,128)(2,1)} %collective-permute-done.6, bf16[224,512]{1,0:T(8,128)(2,1)S(1)} %copy-done.8, s32[512]{0:T(512)S(1)} %bitcast.188, ...), kind=kOutput, calls=%fused_computation.10 | convolution fusion | flops 880803840 | bytes 2623488 | tf_op jit(solution)/shard_map/dot_general | solution.py:18
  122.7 0.2 reshape.205
  122.9 0.1 copy.31
  123.0 0.2 fusion.9
  123.2 1.0 fusion.34
  124.2 7.9 %all-to-all-start.3 = ((bf16[32,104,128]{2,1,0:T(8,128)(2,1)}), bf16[32,104,128]{2,1,0:T(8,128)(2,1)S(1)}, u32[]{:S(2)}, u32[]{:S(2)}) async-start(bf16[32,104,128]{2,1,0:T(8,128)(2,1)} %fusion.34), calls=%async_computation.3 | async-start | bytes 1703936 | tf_op jit(solution)/shard_map/all_to_all | solution.py:14
  132.2 0.3 copy.30
  132.5 2.2 %convolution_convert_fusion.1 = bf16[896,512]{1,0:T(8,128)(2,1)S(1)} fusion(bf16[96,8,4,128]{3,2,1,0:T(4,128)(2,1)S(1)} %bitcast.171, s32[512]{0:T(512)S(1)} %bitcast.189, bf16[224,512]{1,0:T(8,128)(2,1)S(1)} %get-tuple-element.34, bf16[224,512]{1,0:T(8,128)(2,1)} %get-tuple-element.35, bf16[224,512]{1,0:T(8,128)(2,1)} %get-tuple-element.36, ...), kind=kOutput, calls=%fused_computation.9 | convolution fusion | flops 877199360 | bytes 2623488 | tf_op jit(solution)/shard_map/dot_general | solution.py:18
  134.7 0.0 copy-start.3
  134.7 0.0 copy-start.6
  134.7 0.8 fusion.86
  135.6 4.4 %collective-permute-start.3 = (bf16[224,512]{1,0:T(8,128)(2,1)}, bf16[224,512]{1,0:T(8,128)(2,1)S(1)}, u32[]{:S(2)}, u32[]{:S(2)}) collective-permute-start(bf16[224,512]{1,0:T(8,128)(2,1)} %get-tuple-element.31), channel_id=1, source_target_pairs={{0,384},{128,0},{256,128},{384,256},{1,385},{129,1},{257,129},{385... | collective-permute-start | bytes 688136 | tf_op jit(solution)/shard_map/ppermute | solution.py:35
  140.0 2.5 %collective-permute-start.4 = (bf16[224,512]{1,0:T(8,128)(2,1)}, bf16[224,512]{1,0:T(8,128)(2,1)S(1)}, u32[]{:S(2)}, u32[]{:S(2)}) collective-permute-start(bf16[224,512]{1,0:T(8,128)(2,1)} %get-tuple-element.30), channel_id=1, source_target_pairs={{0,256},{128,384},{256,0},{384,128},{1,257},{129,385},{257,1},{385... | collective-permute-start | bytes 688136 | tf_op jit(solution)/shard_map/ppermute | solution.py:35
  142.4 2.5 %collective-permute-start.5 = (bf16[224,512]{1,0:T(8,128)(2,1)S(1)}, bf16[224,512]{1,0:T(8,128)(2,1)S(1)}, u32[]{:S(2)}, u32[]{:S(2)}) collective-permute-start(bf16[224,512]{1,0:T(8,128)(2,1)S(1)} %get-tuple-element.29), channel_id=1, source_target_pairs={{0,128},{128,256},{256,384},{384,0},{1,129},{129,257},{257,385},{3... | collective-permute-start | bytes 688136 | tf_op jit(solution)/shard_map/ppermute | solution.py:35
  144.9 2.3 %convolution_convert_fusion = bf16[224,2048]{1,0:T(8,128)(2,1)S(1)} fusion(bf16[512,512]{0,1:T(8,128)(2,1)} %collective-permute-done.2, bf16[512,512]{0,1:T(8,128)(2,1)} %collective-permute-done.1, bf16[512,512]{0,1:T(8,128)(2,1)} %collective-permute-done, bf16[512,512]{0,1:T(8,128)(2,1)} %fusion.5, bf16[1,512,224]{1,2,0:T(8,128)(2,1)S(1)} %copy-done.3, ...), kind=kOutput, calls=%fused_computation | convolution fusion | flops 479870976 | bytes 3475456 | tf_op jit(solution)/shard_map/dot_general | solution.py:18
  147.3 0.1 constant_dynamic-slice_fusion.3
  147.4 5.4 %all-to-all-done.3 = bf16[32,104,128]{2,1,0:T(8,128)(2,1)S(1)} async-done(((bf16[32,104,128]{2,1,0:T(8,128)(2,1)}), bf16[32,104,128]{2,1,0:T(8,128)(2,1)S(1)}, u32[]{:S(2)}, u32[]{:S(2)}) %all-to-all-start.3) | async-done | bytes 852000 | tf_op jit(solution)/shard_map/all_to_all | solution.py:14
  152.8 0.1 convert_reduce_fusion
  152.9 0.0 copy-start.4
  152.9 0.2 reduce-precision_convert_fusion
  153.2 0.7 pad_maximum_fusion.8
  153.9 8.0 %all-to-all-start.4 = ((bf16[16,32,128]{2,1,0:T(8,128)(2,1)}), bf16[16,32,128]{2,1,0:T(8,128)(2,1)S(1)}, u32[]{:S(2)}, u32[]{:S(2)}) async-start(bf16[16,32,128]{2,1,0:T(8,128)(2,1)} %pad_maximum_fusion.8), calls=%async_computation.4 | async-start | bytes 262144 | tf_op jit(solution)/shard_map/all_to_all | solution.py:14
  161.9 0.9 fusion.61
  162.8 8.3 %all-to-all-done.4 = bf16[16,32,128]{2,1,0:T(8,128)(2,1)S(1)} async-done(((bf16[16,32,128]{2,1,0:T(8,128)(2,1)}), bf16[16,32,128]{2,1,0:T(8,128)(2,1)S(1)}, u32[]{:S(2)}, u32[]{:S(2)}) %all-to-all-start.4) | async-done | bytes 131104 | tf_op jit(solution)/shard_map/all_to_all | solution.py:14
  171.1 1.1 fusion.7
  172.2 0.6 mul.107
  172.8 0.1 pad_maximum_fusion.2
  172.9 0.1 dynamic-slice_bitcast_fusion.3
  173.0 1.5 maximum_bitcast_fusion
  (46 shorter events, 0.3 us)
Async XLA Ops:
  0.6 16.1 %copy-start.9 = (f32[1,256]{1,0:T(1,128)S(1)}, f32[1,256]{1,0:T(1,128)}, u32[]{:S(2)}) copy-start(f32[1,256]{1,0:T(1,128)} %param.10) | copy-start | bytes 3076
  4.9 22.0 %all-to-all-start = ((bf16[16,24,256]{2,1,0:T(8,128)(2,1)}), bf16[16,24,256]{2,1,0:T(8,128)(2,1)S(1)}, u32[]{:S(2)}, u32[]{:S(2)}) async-start(bf16[16,24,256]{2,1,0:T(8,128)(2,1)} %bitcast.2), calls=%async_computation | async-start | bytes 393216 | tf_op jit(solution)/shard_map/all_to_all | solution.py:14
  28.0 32.2 %all-to-all-start.1 = ((bf16[32,104,128]{2,1,0:T(8,128)(2,1)}), bf16[32,104,128]{2,1,0:T(8,128)(2,1)S(1)}, u32[]{:S(2)}, u32[]{:S(2)}) async-start(bf16[32,104,128]{2,1,0:T(8,128)(2,1)} %bitcast.8), calls=%async_computation.1 | async-start | bytes 1703936 | tf_op jit(solution)/shard_map/all_to_all | solution.py:14
  60.5 10.3 %copy-start = (bf16[1,224,2048]{2,1,0:T(8,128)(2,1)S(1)}, bf16[1,224,2048]{2,1,0:T(8,128)(2,1)}, u32[]{:S(2)}) copy-start(bf16[1,224,2048]{2,1,0:T(8,128)(2,1)} %param.15) | copy-start | bytes 2752516
  62.0 15.7 %copy-start.1 = (bf16[1,224,2048]{2,1,0:T(8,128)(2,1)S(1)}, bf16[1,224,2048]{2,1,0:T(8,128)(2,1)}, u32[]{:S(2)}) copy-start(bf16[1,224,2048]{2,1,0:T(8,128)(2,1)} %param.14) | copy-start | bytes 2752516
  62.0 25.1 %collective-permute-start = (bf16[512,512]{0,1:T(8,128)(2,1)}, bf16[512,512]{0,1:T(8,128)(2,1)}, u32[]{:S(2)}, u32[]{:S(2)}) collective-permute-start(bf16[512,512]{0,1:T(8,128)(2,1)} %fusion.5), channel_id=1, source_target_pairs={{0,128},{128,256},{256,384},{384,0},{1,129},{129,257},{257,385},{3... | collective-permute-start | bytes 1572872 | tf_op jit(solution)/shard_map/ppermute | solution.py:35
  64.0 27.5 %collective-permute-start.1 = (bf16[512,512]{0,1:T(8,128)(2,1)}, bf16[512,512]{0,1:T(8,128)(2,1)}, u32[]{:S(2)}, u32[]{:S(2)}) collective-permute-start(bf16[512,512]{0,1:T(8,128)(2,1)} %fusion.5), channel_id=1, source_target_pairs={{0,256},{128,384},{256,0},{384,128},{1,257},{129,385},{257,1},{385... | collective-permute-start | bytes 1572872 | tf_op jit(solution)/shard_map/ppermute | solution.py:35
  67.9 29.9 %collective-permute-start.2 = (bf16[512,512]{0,1:T(8,128)(2,1)}, bf16[512,512]{0,1:T(8,128)(2,1)}, u32[]{:S(2)}, u32[]{:S(2)}) collective-permute-start(bf16[512,512]{0,1:T(8,128)(2,1)} %fusion.5), channel_id=1, source_target_pairs={{0,384},{128,0},{256,128},{384,256},{1,385},{129,1},{257,129},{385... | collective-permute-start | bytes 1572872 | tf_op jit(solution)/shard_map/ppermute | solution.py:35
  71.7 48.3 %collective-permute-start.6 = (bf16[224,512]{1,0:T(8,128)(2,1)}, bf16[224,512]{1,0:T(8,128)(2,1)}, u32[]{:S(2)}, u32[]{:S(2)}) collective-permute-start(bf16[224,512]{1,0:T(8,128)(2,1)} %get-tuple-element.26), channel_id=1, source_target_pairs={{0,128},{128,256},{256,384},{384,0},{1,129},{129,257},{257,385},{3... | collective-permute-start | bytes 688136 | tf_op jit(solution)/shard_map/ppermute | solution.py:35
  74.1 46.0 %collective-permute-start.7 = (bf16[224,512]{1,0:T(8,128)(2,1)S(1)}, bf16[224,512]{1,0:T(8,128)(2,1)}, u32[]{:S(2)}, u32[]{:S(2)}) collective-permute-start(bf16[224,512]{1,0:T(8,128)(2,1)S(1)} %get-tuple-element.28), channel_id=1, source_target_pairs={{0,256},{128,384},{256,0},{384,128},{1,257},{129,385},{257,1},{385... | collective-permute-start | bytes 688136 | tf_op jit(solution)/shard_map/ppermute | solution.py:35
  79.5 18.3 %copy-start.2 = (bf16[1,512,224]{1,2,0:T(8,128)(2,1)S(1)}, bf16[1,512,224]{1,2,0:T(8,128)(2,1)}, u32[]{:S(2)}) copy-start(bf16[1,512,224]{1,2,0:T(8,128)(2,1)} %param.13) | copy-start | bytes 688132
  79.5 18.3 %copy-start.5 = (bf16[1,512,224]{1,2,0:T(8,128)(2,1)S(1)}, bf16[1,512,224]{1,2,0:T(8,128)(2,1)}, u32[]{:S(2)}) copy-start(bf16[1,512,224]{1,2,0:T(8,128)(2,1)} %param.12) | copy-start | bytes 688132
  79.5 44.6 %all-to-all-start.2 = ((bf16[32,96,128]{2,1,0:T(8,128)(2,1)}), bf16[32,96,128]{2,1,0:T(8,128)(2,1)S(1)}, u32[]{:S(2)}, u32[]{:S(2)}) async-start(bf16[32,96,128]{2,1,0:T(8,128)(2,1)} %bitcast.27), calls=%async_computation.2 | async-start | bytes 1572864 | tf_op jit(solution)/shard_map/all_to_all | solution.py:14
  87.1 32.9 %collective-permute-start.8 = (bf16[224,512]{1,0:T(8,128)(2,1)S(1)}, bf16[224,512]{1,0:T(8,128)(2,1)S(1)}, u32[]{:S(2)}, u32[]{:S(2)}) collective-permute-start(bf16[224,512]{1,0:T(8,128)(2,1)S(1)} %get-tuple-element.27), channel_id=1, source_target_pairs={{0,384},{128,0},{256,128},{384,256},{1,385},{129,1},{257,129},{385... | collective-permute-start | bytes 688136 | tf_op jit(solution)/shard_map/ppermute | solution.py:35
  119.2 1.0 copy-start.8
  124.2 28.6 %all-to-all-start.3 = ((bf16[32,104,128]{2,1,0:T(8,128)(2,1)}), bf16[32,104,128]{2,1,0:T(8,128)(2,1)S(1)}, u32[]{:S(2)}, u32[]{:S(2)}) async-start(bf16[32,104,128]{2,1,0:T(8,128)(2,1)} %fusion.34), calls=%async_computation.3 | async-start | bytes 1703936 | tf_op jit(solution)/shard_map/all_to_all | solution.py:14
  134.7 10.2 %copy-start.3 = (bf16[1,512,224]{1,2,0:T(8,128)(2,1)S(1)}, bf16[1,512,224]{1,2,0:T(8,128)(2,1)}, u32[]{:S(2)}) copy-start(bf16[1,512,224]{1,2,0:T(8,128)(2,1)} %param.13) | copy-start | bytes 688132
  134.7 10.2 %copy-start.6 = (bf16[1,512,224]{1,2,0:T(8,128)(2,1)S(1)}, bf16[1,512,224]{1,2,0:T(8,128)(2,1)}, u32[]{:S(2)}) copy-start(bf16[1,512,224]{1,2,0:T(8,128)(2,1)} %param.12) | copy-start | bytes 688132
  135.6 27.2 %collective-permute-start.3 = (bf16[224,512]{1,0:T(8,128)(2,1)}, bf16[224,512]{1,0:T(8,128)(2,1)S(1)}, u32[]{:S(2)}, u32[]{:S(2)}) collective-permute-start(bf16[224,512]{1,0:T(8,128)(2,1)} %get-tuple-element.31), channel_id=1, source_target_pairs={{0,384},{128,0},{256,128},{384,256},{1,385},{129,1},{257,129},{385... | collective-permute-start | bytes 688136 | tf_op jit(solution)/shard_map/ppermute | solution.py:35
  140.0 22.8 %collective-permute-start.4 = (bf16[224,512]{1,0:T(8,128)(2,1)}, bf16[224,512]{1,0:T(8,128)(2,1)S(1)}, u32[]{:S(2)}, u32[]{:S(2)}) collective-permute-start(bf16[224,512]{1,0:T(8,128)(2,1)} %get-tuple-element.30), channel_id=1, source_target_pairs={{0,256},{128,384},{256,0},{384,128},{1,257},{129,385},{257,1},{385... | collective-permute-start | bytes 688136 | tf_op jit(solution)/shard_map/ppermute | solution.py:35
  142.4 20.4 %collective-permute-start.5 = (bf16[224,512]{1,0:T(8,128)(2,1)S(1)}, bf16[224,512]{1,0:T(8,128)(2,1)S(1)}, u32[]{:S(2)}, u32[]{:S(2)}) collective-permute-start(bf16[224,512]{1,0:T(8,128)(2,1)S(1)} %get-tuple-element.29), channel_id=1, source_target_pairs={{0,128},{128,256},{256,384},{384,0},{1,129},{129,257},{257,385},{3... | collective-permute-start | bytes 688136 | tf_op jit(solution)/shard_map/ppermute | solution.py:35
  152.9 9.0 %copy-start.4 = (bf16[1,512,224]{1,2,0:T(8,128)(2,1)S(1)}, bf16[1,512,224]{1,2,0:T(8,128)(2,1)}, u32[]{:S(2)}) copy-start(bf16[1,512,224]{1,2,0:T(8,128)(2,1)} %param.13) | copy-start | bytes 688132
  152.9 9.0 %copy-start.7 = (bf16[1,512,224]{1,2,0:T(8,128)(2,1)S(1)}, bf16[1,512,224]{1,2,0:T(8,128)(2,1)}, u32[]{:S(2)}) copy-start(bf16[1,512,224]{1,2,0:T(8,128)(2,1)} %param.12) | copy-start | bytes 688132
  153.9 17.2 %all-to-all-start.4 = ((bf16[16,32,128]{2,1,0:T(8,128)(2,1)}), bf16[16,32,128]{2,1,0:T(8,128)(2,1)S(1)}, u32[]{:S(2)}, u32[]{:S(2)}) async-start(bf16[16,32,128]{2,1,0:T(8,128)(2,1)} %pad_maximum_fusion.8), calls=%async_computation.4 | async-start | bytes 262144 | tf_op jit(solution)/shard_map/all_to_all | solution.py:14

commit v5 on v4

--- a/solution.py
+++ b/solution.py
@@ -12,6 +12,11 @@
 
 def exchange(x, axis):
     return lax.all_to_all(x, axis, 0, 0, tiled=True)
+
+
+def to_all(x, axis):
+    size = lax.axis_size(axis)
+    return exchange(jnp.broadcast_to(x[None], (size, *x.shape)), axis)
 
 
 def dot(a, b, ca, cb):
@@ -120,6 +125,10 @@
     )
     grads = jnp.concatenate([rows[..., :lane].reshape(nx, quarter * cap, lane), gate_tile], axis=1)
     inputs = rows[..., lane:].reshape(nx, quarter * cap, lane)
+    inputs = [
+        lax.dynamic_index_in_dim(inputs, (xi + k) % nx, 0, keepdims=False) for k in range(nx)
+    ]
+    inputs = jnp.concatenate(over_x(inputs, 1), axis=0)
 
     gate_value = gate_pre[0].T.astype(F32)
     up_value = up_pre[0].T.astype(F32)
@@ -128,7 +137,7 @@
     hidden = active * up_value
 
     grads_all = to_quarters(grads, ny)
-    inputs_all = to_quarters(inputs, ny)
+    inputs_all = to_all(inputs, Y).reshape(shards, quarter * cap, lane)
 
     chosen_row = lax.dynamic_index_in_dim(chosen, ei, 0, keepdims=True)
     owner = chosen_row // tok_dev
@@ -138,6 +147,10 @@
         jnp.where(owner == shard_col, before, 0), axis=0, keepdims=True
     )
     place = onehot(rows_of(shards * cap, slots) == owner * cap + within)
+    behind = (xi + nx - owner // ny) % nx
+    place_inputs = onehot(
+        rows_of(shards * cap, slots) == (owner % ny * nx + behind) * cap + within
+    )
     owner_hit = owner == shard_col
     within_hit = onehot(rows_of(lane, slots) == within)
 
@@ -167,7 +180,7 @@
     dots_rows = dot(dots_own, within_hit, 1, 1).astype(BF)
     dots_rows = jnp.pad(dots_rows[:, None], ((0, 0), (0, PAD - 1), (0, 0)))
     dx_back = exchange(jnp.concatenate([dx_rows, dots_rows], axis=1), (X, Y))
-    inputs_slots = dot(place, joined(inputs_all, quarter), 0, 0).astype(BF)
+    inputs_slots = dot(place_inputs, joined(inputs_all, quarter), 0, 0).astype(BF)
     grad_up = dot(up_all, inputs_slots, 1, 0).astype(BF).reshape(nx, units, part)
     up_home = over_x(grad_up, -1)
     dx_sum = jnp.sum(dx_back.reshape(nx, ny, -1, lane).astype(F32), axis=1)
@@ -188,7 +201,6 @@
     spread = exchange(
         jnp.concatenate([to_experts, jnp.broadcast_to(tail[None], (ne, PAD, lane))], axis=1), E
     )
-    up_home, spread = lax.optimization_barrier((up_home, spread))
     grad_up = in_turn(up_home, xi)
     grad_tokens = dot(picker.reshape(-1, tok_dev), spread.reshape(-1, width_dev), 0, 0).astype(BF)
     pieces = jnp.sum(spread[:, cap : cap + 2 * tok_dev // lane].astype(F32), axis=0)

time: 176 us -> 181 us (1.028)
  starting transfers between devices: 73.2 us -> 82.7 us
  blocking collectives: 18.9 us -> 12.7 us
  waiting for transfers between devices: 50.6 us -> 53 us
    ppermute x9 -> x12, starting transfers between devices: 28.4 us -> 38 us  [shift(): return lax.ppermute(x, X, [(i, (i + by) % size) for i in range(size)])]
    ppermute x9 -> x12, waiting for transfers between devices: 6.3 us -> 14.7 us  [shift(): return lax.ppermute(x, X, [(i, (i + by) % size) for i in range(size)])]
    all_gather x1, blocking collectives: 18.9 us -> 12.7 us  [local(): up_all = lax.all_gather(up_grad, X)]
    all_to_all x5, waiting for transfers between devices: 44.3 us -> 38.3 us  [exchange(): return lax.all_to_all(x, axis, 0, 0, tiled=True)]
  transfers between devices with their start and end apart: 14 -> 17, of which waited for: 5 -> 6; matrix products, arithmetic and copies ran while one was open for 11% -> 11% of each run, Pallas kernels for 0% -> 0%
where the time goes in v5:
time: 181 us; the launch traced here: 180 us
  starting transfers between devices  82.7 us (46%)
  waiting for transfers between devices  53 us (29%)
  matrix products  14.8 us (8%)
  blocking collectives  12.7 us (7%)
  other arithmetic  9.08 us (5%)
  local copies, waits for them, and re-layouts  6.23 us (3%)
    all_to_all x5, starting transfers between devices, exchange(): return lax.all_to_all(x, axis, 0, 0, tiled=True)  44.6 us
    all_to_all x5, waiting for transfers between devices, exchange(): return lax.all_to_all(x, axis, 0, 0, tiled=True)  38.3 us
    ppermute x12, starting transfers between devices, shift(): return lax.ppermute(x, X, [(i, (i + by) % size) for i in range(size)])  38 us
    ppermute x12, waiting for transfers between devices, shift(): return lax.ppermute(x, X, [(i, (i + by) % size) for i in range(size)])  14.7 us
    dot_general x10, matrix products, dot(): lax.dot_general(a, b, (((ca,), (cb,)), ((), ())), preferred_element_type=...  14.6 us
    all_gather x1, blocking collectives, local(): up_all = lax.all_gather(up_grad, X)  12.7 us
  transfers between devices with their start and end apart: 17, of which 6 were waited for; matrix products, arithmetic and copies ran while one was open for 11% of the time, Pallas kernels for 0%

profile of v5, /device:TPU:1, one launch (start us, length us, event | category | flops | bytes accessed | tf_op | source)
XLA Modules:
  0.0 179.8 jit_solution(704152354216870234)
XLA Ops:
  0.7 0.9 convert_reduce_fusion.3
  1.5 0.1 iota_add_fusion
  1.6 1.2 select_reduce_fusion
  2.8 0.1 subtract_select_fusion
  2.9 0.1 iota_compare_fusion.15
  3.1 1.8 convolution_convert_fusion.3
  4.9 11.8 %all-to-all-start = ((bf16[16,24,256]{2,1,0:T(8,128)(2,1)}), bf16[16,24,256]{2,1,0:T(8,128)(2,1)S(1)}, u32[]{:S(2)}, u32[]{:S(2)}) async-start(bf16[16,24,256]{2,1,0:T(8,128)(2,1)} %bitcast.4), calls=%async_computation | async-start | bytes 393216 | tf_op jit(solution)/shard_map/all_to_all | solution.py:14
  16.7 0.2 fusion.11
  16.9 10.0 %all-to-all-done = bf16[16,24,256]{2,1,0:T(8,128)(2,1)S(1)} async-done(((bf16[16,24,256]{2,1,0:T(8,128)(2,1)}), bf16[16,24,256]{2,1,0:T(8,128)(2,1)S(1)}, u32[]{:S(2)}, u32[]{:S(2)}) %all-to-all-start) | async-done | bytes 196640 | tf_op jit(solution)/shard_map/all_to_all | solution.py:14
  27.0 1.0 broadcast_in_dim.100
  28.0 9.7 %all-to-all-start.1 = ((bf16[32,104,128]{2,1,0:T(8,128)(2,1)}), bf16[32,104,128]{2,1,0:T(8,128)(2,1)S(1)}, u32[]{:S(2)}, u32[]{:S(2)}) async-start(bf16[32,104,128]{2,1,0:T(8,128)(2,1)} %bitcast.10), calls=%async_computation.1 | async-start | bytes 1703936 | tf_op jit(solution)/shard_map/all_to_all | solution.py:14
  37.7 0.7 and_select_fusion.3
  38.5 0.1 convert_reduce_fusion.1
  38.6 0.1 select_reduce_fusion.1
  38.7 0.8 multiply_add_fusion
  39.5 20.7 %all-to-all-done.1 = bf16[32,104,128]{2,1,0:T(8,128)(2,1)S(1)} async-done(((bf16[32,104,128]{2,1,0:T(8,128)(2,1)}), bf16[32,104,128]{2,1,0:T(8,128)(2,1)S(1)}, u32[]{:S(2)}, u32[]{:S(2)}) %all-to-all-start.1) | async-done | bytes 852000 | tf_op jit(solution)/shard_map/all_to_all | solution.py:14
  60.2 0.3 copy.29
  60.5 1.5 fusion.6
  62.0 1.9 %collective-permute-start = (bf16[512,512]{0,1:T(8,128)(2,1)}, bf16[512,512]{0,1:T(8,128)(2,1)}, u32[]{:S(2)}, u32[]{:S(2)}) collective-permute-start(bf16[512,512]{0,1:T(8,128)(2,1)} %fusion.6), channel_id=1, source_target_pairs={{0,128},{128,256},{256,384},{384,0},{1,129},{129,257},{257,385},{3... | collective-permute-start | bytes 1572872 | tf_op jit(solution)/shard_map/ppermute | solution.py:40
  63.9 3.9 %collective-permute-start.1 = (bf16[512,512]{0,1:T(8,128)(2,1)}, bf16[512,512]{0,1:T(8,128)(2,1)}, u32[]{:S(2)}, u32[]{:S(2)}) collective-permute-start(bf16[512,512]{0,1:T(8,128)(2,1)} %fusion.6), channel_id=1, source_target_pairs={{0,256},{128,384},{256,0},{384,128},{1,257},{129,385},{257,1},{385... | collective-permute-start | bytes 1572872 | tf_op jit(solution)/shard_map/ppermute | solution.py:40
  67.8 2.9 %collective-permute-start.2 = (bf16[512,512]{0,1:T(8,128)(2,1)}, bf16[512,512]{0,1:T(8,128)(2,1)}, u32[]{:S(2)}, u32[]{:S(2)}) collective-permute-start(bf16[512,512]{0,1:T(8,128)(2,1)} %fusion.6), channel_id=1, source_target_pairs={{0,384},{128,0},{256,128},{384,256},{1,385},{129,1},{257,129},{385... | collective-permute-start | bytes 1572872 | tf_op jit(solution)/shard_map/ppermute | solution.py:40
  70.8 2.5 %collective-permute-start.6 = (bf16[96,128]{1,0:T(8,128)(2,1)S(1)}, bf16[96,128]{1,0:T(8,128)(2,1)S(1)}, u32[]{:S(2)}, u32[]{:S(2)}) collective-permute-start(bf16[96,128]{1,0:T(8,128)(2,1)S(1)} %get-tuple-element.38), channel_id=1, source_target_pairs={{0,128},{128,256},{256,384},{384,0},{1,129},{129,257},{257,385},{3... | collective-permute-start | bytes 73736 | tf_op jit(solution)/shard_map/ppermute | solution.py:40
  73.3 0.8 dynamic-slice_bitcast_fusion.15
  74.1 3.5 %collective-permute-start.7 = (bf16[96,128]{1,0:T(8,128)(2,1)S(1)}, bf16[96,128]{1,0:T(8,128)(2,1)S(1)}, u32[]{:S(2)}, u32[]{:S(2)}) collective-permute-start(bf16[96,128]{1,0:T(8,128)(2,1)S(1)} %get-tuple-element.37), channel_id=1, source_target_pairs={{0,256},{128,384},{256,0},{384,128},{1,257},{129,385},{257,1},{385... | collective-permute-start | bytes 73736 | tf_op jit(solution)/shard_map/ppermute | solution.py:40
  77.6 7.4 %collective-permute-done.6 = bf16[96,128]{1,0:T(8,128)(2,1)S(1)} collective-permute-done((bf16[96,128]{1,0:T(8,128)(2,1)S(1)}, bf16[96,128]{1,0:T(8,128)(2,1)S(1)}, u32[]{:S(2)}, u32[]{:S(2)}) %collective-permute-start.6) | collective-permute-done | bytes 24608 | tf_op jit(solution)/shard_map/ppermute | solution.py:40
  84.9 5.1 %collective-permute-start.8 = (bf16[96,128]{1,0:T(8,128)(2,1)S(1)}, bf16[96,128]{1,0:T(8,128)(2,1)S(1)}, u32[]{:S(2)}, u32[]{:S(2)}) collective-permute-start(bf16[96,128]{1,0:T(8,128)(2,1)S(1)} %get-tuple-element.36), channel_id=1, source_target_pairs={{0,384},{128,0},{256,128},{384,256},{1,385},{129,1},{257,129},{385... | collective-permute-start | bytes 73736 | tf_op jit(solution)/shard_map/ppermute | solution.py:40
  90.0 1.0 dynamic-slice_bitcast_fusion.7
  91.0 1.9 %collective-permute-start.3 = (bf16[224,512]{1,0:T(8,128)(2,1)}, bf16[224,512]{1,0:T(8,128)(2,1)}, u32[]{:S(2)}, u32[]{:S(2)}) collective-permute-start(bf16[224,512]{1,0:T(8,128)(2,1)} %get-tuple-element.24), channel_id=1, source_target_pairs={{0,128},{128,256},{256,384},{384,0},{1,129},{129,257},{257,385},{3... | collective-permute-start | bytes 688136 | tf_op jit(solution)/shard_map/ppermute | solution.py:40
  92.9 4.5 %collective-permute-start.4 = (bf16[224,512]{1,0:T(8,128)(2,1)}, bf16[224,512]{1,0:T(8,128)(2,1)}, u32[]{:S(2)}, u32[]{:S(2)}) collective-permute-start(bf16[224,512]{1,0:T(8,128)(2,1)} %get-tuple-element.26), channel_id=1, source_target_pairs={{0,256},{128,384},{256,0},{384,128},{1,257},{129,385},{257,1},{385... | collective-permute-start | bytes 688136 | tf_op jit(solution)/shard_map/ppermute | solution.py:40
  97.5 1.0 broadcast_in_dim.106
  98.4 6.9 %all-to-all-start.4 = ((bf16[8,384,128]{2,1,0:T(8,128)(2,1)}), bf16[8,384,128]{2,1,0:T(8,128)(2,1)S(1)}, u32[]{:S(2)}, u32[]{:S(2)}) async-start(bf16[8,384,128]{2,1,0:T(8,128)(2,1)} %broadcast_in_dim.106), calls=%async_computation.4 | async-start | bytes 1572864 | tf_op jit(solution)/shard_map/all_to_all | solution.py:14
  105.4 0.2 fusion.8
  105.6 2.5 %collective-permute-start.5 = (bf16[224,512]{1,0:T(8,128)(2,1)}, bf16[224,512]{1,0:T(8,128)(2,1)S(1)}, u32[]{:S(2)}, u32[]{:S(2)}) collective-permute-start(bf16[224,512]{1,0:T(8,128)(2,1)} %get-tuple-element.25), channel_id=1, source_target_pairs={{0,384},{128,0},{256,128},{384,256},{1,385},{129,1},{257,129},{385... | collective-permute-start | bytes 688136 | tf_op jit(solution)/shard_map/ppermute | solution.py:40
  108.1 2.4 %multiply_convert_fusion.1 = (bf16[224,512]{1,0:T(8,128)(2,1)S(1)}, bf16[512]{0:T(512)(128)(2,1)S(1)}, f32[224,512]{1,0:T(8,128)S(1)}) fusion(f32[512]{0:T(512)S(1)} %fusion.8, bf16[1,512,224]{1,2,0:T(8,128)(2,1)S(1)} %copy-done.2, bf16[1,512,224]{1,2,0:T(8,128)(2,1)S(1)} %copy-done.3, bf16[512,512]{0,1:T(8,128)(2,1)} %collective-permute-done.2, ...), kind=kOutput, calls=%fused_computation.75 | convolution fusion | flops 483196416 | bytes 4164608 | tf_op jit(solution)/shard_map/dot_general | solution.py:23
  110.5 12.7 %all-gather = bf16[896,512]{1,0:T(8,128)(2,1)S(1)} all-gather(bf16[224,512]{1,0:T(8,128)(2,1)S(1)} %get-tuple-element.31), channel_id=2, replica_groups=mesh['dp_0'=4,'dp_1'=8,'expert'=16] {'dp_0'}, dimensions={0}, use_global_device_ids=true | all-gather | bytes 1146880 | tf_op jit(solution)/shard_map/all_gather | solution.py:168
  123.2 0.9 dynamic-slice_bitcast_fusion.11
  124.2 0.2 copy-done.4
  124.3 2.6 %fusion.4 = bf16[768,512]{1,0:T(8,128)(2,1)S(1)} fusion(bf16[224,512]{1,0:T(8,128)(2,1)S(1)} %collective-permute-done.5, bf16[224,512]{1,0:T(8,128)(2,1)} %collective-permute-done.4, bf16[224,512]{1,0:T(8,128)(2,1)} %collective-permute-done.3, bf16[224,512]{1,0:T(8,128)(2,1)S(1)} %copy-done.4, s32[512]{0:T(512)S(1)} %bitcast.197, ...), kind=kOutput, calls=%fused_computation.11 | convolution fusion | flops 880803840 | bytes 2623488 | tf_op jit(solution)/shard_map/dot_general | solution.py:23
  127.0 0.2 reshape.198
  127.2 0.1 copy.30
  127.3 0.2 fusion.9
  127.5 1.0 fusion.34
  128.4 7.5 %all-to-all-start.2 = ((bf16[32,104,128]{2,1,0:T(8,128)(2,1)}), bf16[32,104,128]{2,1,0:T(8,128)(2,1)S(1)}, u32[]{:S(2)}, u32[]{:S(2)}) async-start(bf16[32,104,128]{2,1,0:T(8,128)(2,1)} %fusion.34), calls=%async_computation.2 | async-start | bytes 1703936 | tf_op jit(solution)/shard_map/all_to_all | solution.py:14
  136.0 0.3 copy.32
  136.3 2.4 %convolution_convert_fusion.1 = bf16[896,512]{1,0:T(8,128)(2,1)S(1)} fusion(bf16[96,8,4,128]{3,2,1,0:T(4,128)(2,1)S(1)} %bitcast.179, s32[512]{0:T(512)S(1)} %bitcast.195, bf16[224,512]{1,0:T(8,128)(2,1)} %get-tuple-element.20, bf16[224,512]{1,0:T(8,128)(2,1)} %get-tuple-element.21, bf16[224,512]{1,0:T(8,128)(2,1)} %get-tuple-element.22, ...), kind=kOutput, calls=%fused_computation.10 | convolution fusion | flops 877199360 | bytes 2623488 | tf_op jit(solution)/shard_map/dot_general | solution.py:23
  138.8 0.1 slice_bitcast_fusion
  138.8 4.4 %collective-permute-start.9 = (bf16[224,512]{1,0:T(8,128)(2,1)S(1)}, bf16[224,512]{1,0:T(8,128)(2,1)S(1)}, u32[]{:S(2)}, u32[]{:S(2)}) collective-permute-start(bf16[224,512]{1,0:T(8,128)(2,1)S(1)} %get-tuple-element.14), channel_id=1, source_target_pairs={{0,384},{128,0},{256,128},{384,256},{1,385},{129,1},{257,129},{385... | collective-permute-start | bytes 688136 | tf_op jit(solution)/shard_map/ppermute | solution.py:40
  143.3 2.4 %collective-permute-start.10 = (bf16[224,512]{1,0:T(8,128)(2,1)S(1)}, bf16[224,512]{1,0:T(8,128)(2,1)S(1)}, u32[]{:S(2)}, u32[]{:S(2)}) collective-permute-start(bf16[224,512]{1,0:T(8,128)(2,1)S(1)} %get-tuple-element.13), channel_id=1, source_target_pairs={{0,256},{128,384},{256,0},{384,128},{1,257},{129,385},{257,1},{385... | collective-permute-start | bytes 688136 | tf_op jit(solution)/shard_map/ppermute | solution.py:40
  145.7 2.5 %collective-permute-start.11 = (bf16[224,512]{1,0:T(8,128)(2,1)S(1)}, bf16[224,512]{1,0:T(8,128)(2,1)S(1)}, u32[]{:S(2)}, u32[]{:S(2)}) collective-permute-start(bf16[224,512]{1,0:T(8,128)(2,1)S(1)} %get-tuple-element.12), channel_id=1, source_target_pairs={{0,128},{128,256},{256,384},{384,0},{1,129},{129,257},{257,385},{3... | collective-permute-start | bytes 688136 | tf_op jit(solution)/shard_map/ppermute | solution.py:40
  148.2 2.3 %convolution_convert_fusion = bf16[224,2048]{1,0:T(8,128)(2,1)S(1)} fusion(bf16[512,512]{0,1:T(8,128)(2,1)} %collective-permute-done.2, bf16[512,512]{0,1:T(8,128)(2,1)} %collective-permute-done.1, bf16[512,512]{0,1:T(8,128)(2,1)} %collective-permute-done, bf16[512,512]{0,1:T(8,128)(2,1)} %fusion.6, bf16[1,512,224]{1,2,0:T(8,128)(2,1)S(1)} %copy-done.3, ...), kind=kOutput, calls=%fused_computation | convolution fusion | flops 479870976 | bytes 3475456 | tf_op jit(solution)/shard_map/dot_general | solution.py:23
  150.5 0.1 constant_dynamic-slice_fusion.3
  150.6 0.9 fusion.61
  151.5 2.1 %collective-permute-done.10 = bf16[224,512]{1,0:T(8,128)(2,1)S(1)} collective-permute-done((bf16[224,512]{1,0:T(8,128)(2,1)S(1)}, bf16[224,512]{1,0:T(8,128)(2,1)S(1)}, u32[]{:S(2)}, u32[]{:S(2)}) %collective-permute-start.10) | collective-permute-done | bytes 229408 | tf_op jit(solution)/shard_map/ppermute | solution.py:40
  153.7 5.1 %collective-permute-done.11 = bf16[224,512]{1,0:T(8,128)(2,1)S(1)} collective-permute-done((bf16[224,512]{1,0:T(8,128)(2,1)S(1)}, bf16[224,512]{1,0:T(8,128)(2,1)S(1)}, u32[]{:S(2)}, u32[]{:S(2)}) %collective-permute-start.11) | collective-permute-done | bytes 229408 | tf_op jit(solution)/shard_map/ppermute | solution.py:40
  158.8 0.1 pad_maximum_fusion.2
  158.9 0.1 dynamic-slice_bitcast_fusion.3
  159.0 0.1 convert_reduce_fusion
  159.2 0.2 reduce-precision_convert_fusion
  159.5 0.7 pad_maximum_fusion.8
  160.1 8.7 %all-to-all-start.3 = ((bf16[16,32,128]{2,1,0:T(8,128)(2,1)}), bf16[16,32,128]{2,1,0:T(8,128)(2,1)S(1)}, u32[]{:S(2)}, u32[]{:S(2)}) async-start(bf16[16,32,128]{2,1,0:T(8,128)(2,1)} %pad_maximum_fusion.8), calls=%async_computation.3 | async-start | bytes 262144 | tf_op jit(solution)/shard_map/all_to_all | solution.py:14
  168.9 1.5 maximum_bitcast_fusion
  170.4 7.7 %all-to-all-done.3 = bf16[16,32,128]{2,1,0:T(8,128)(2,1)S(1)} async-done(((bf16[16,32,128]{2,1,0:T(8,128)(2,1)}), bf16[16,32,128]{2,1,0:T(8,128)(2,1)S(1)}, u32[]{:S(2)}, u32[]{:S(2)}) %all-to-all-start.3) | async-done | bytes 131104 | tf_op jit(solution)/shard_map/all_to_all | solution.py:14
  178.1 0.6 mul.112
  178.7 1.1 fusion.7
  (46 shorter events, 0.4 us)
Async XLA Ops:
  0.6 16.1 %copy-start.5 = (f32[1,256]{1,0:T(1,128)S(1)}, f32[1,256]{1,0:T(1,128)}, u32[]{:S(2)}) copy-start(f32[1,256]{1,0:T(1,128)} %param.10) | copy-start | bytes 3076
  4.9 22.0 %all-to-all-start = ((bf16[16,24,256]{2,1,0:T(8,128)(2,1)}), bf16[16,24,256]{2,1,0:T(8,128)(2,1)S(1)}, u32[]{:S(2)}, u32[]{:S(2)}) async-start(bf16[16,24,256]{2,1,0:T(8,128)(2,1)} %bitcast.4), calls=%async_computation | async-start | bytes 393216 | tf_op jit(solution)/shard_map/all_to_all | solution.py:14
  28.0 32.2 %all-to-all-start.1 = ((bf16[32,104,128]{2,1,0:T(8,128)(2,1)}), bf16[32,104,128]{2,1,0:T(8,128)(2,1)S(1)}, u32[]{:S(2)}, u32[]{:S(2)}) async-start(bf16[32,104,128]{2,1,0:T(8,128)(2,1)} %bitcast.10), calls=%async_computation.1 | async-start | bytes 1703936 | tf_op jit(solution)/shard_map/all_to_all | solution.py:14
  60.5 12.7 %copy-start = (bf16[1,224,2048]{2,1,0:T(8,128)(2,1)S(1)}, bf16[1,224,2048]{2,1,0:T(8,128)(2,1)}, u32[]{:S(2)}) copy-start(bf16[1,224,2048]{2,1,0:T(8,128)(2,1)} %param.14) | copy-start | bytes 2752516
  62.0 43.5 %collective-permute-start = (bf16[512,512]{0,1:T(8,128)(2,1)}, bf16[512,512]{0,1:T(8,128)(2,1)}, u32[]{:S(2)}, u32[]{:S(2)}) collective-permute-start(bf16[512,512]{0,1:T(8,128)(2,1)} %fusion.6), channel_id=1, source_target_pairs={{0,128},{128,256},{256,384},{384,0},{1,129},{129,257},{257,385},{3... | collective-permute-start | bytes 1572872 | tf_op jit(solution)/shard_map/ppermute | solution.py:40
  63.9 44.1 %collective-permute-start.1 = (bf16[512,512]{0,1:T(8,128)(2,1)}, bf16[512,512]{0,1:T(8,128)(2,1)}, u32[]{:S(2)}, u32[]{:S(2)}) collective-permute-start(bf16[512,512]{0,1:T(8,128)(2,1)} %fusion.6), channel_id=1, source_target_pairs={{0,256},{128,384},{256,0},{384,128},{1,257},{129,385},{257,1},{385... | collective-permute-start | bytes 1572872 | tf_op jit(solution)/shard_map/ppermute | solution.py:40
  67.8 40.3 %collective-permute-start.2 = (bf16[512,512]{0,1:T(8,128)(2,1)}, bf16[512,512]{0,1:T(8,128)(2,1)}, u32[]{:S(2)}, u32[]{:S(2)}) collective-permute-start(bf16[512,512]{0,1:T(8,128)(2,1)} %fusion.6), channel_id=1, source_target_pairs={{0,384},{128,0},{256,128},{384,256},{1,385},{129,1},{257,129},{385... | collective-permute-start | bytes 1572872 | tf_op jit(solution)/shard_map/ppermute | solution.py:40
  70.8 19.3 %copy-start.1 = (bf16[1,224,2048]{2,1,0:T(8,128)(2,1)S(1)}, bf16[1,224,2048]{2,1,0:T(8,128)(2,1)}, u32[]{:S(2)}) copy-start(bf16[1,224,2048]{2,1,0:T(8,128)(2,1)} %param.15) | copy-start | bytes 2752516
  70.8 14.2 %collective-permute-start.6 = (bf16[96,128]{1,0:T(8,128)(2,1)S(1)}, bf16[96,128]{1,0:T(8,128)(2,1)S(1)}, u32[]{:S(2)}, u32[]{:S(2)}) collective-permute-start(bf16[96,128]{1,0:T(8,128)(2,1)S(1)} %get-tuple-element.38), channel_id=1, source_target_pairs={{0,128},{128,256},{256,384},{384,0},{1,129},{129,257},{257,385},{3... | collective-permute-start | bytes 73736 | tf_op jit(solution)/shard_map/ppermute | solution.py:40
  74.1 16.9 %collective-permute-start.7 = (bf16[96,128]{1,0:T(8,128)(2,1)S(1)}, bf16[96,128]{1,0:T(8,128)(2,1)S(1)}, u32[]{:S(2)}, u32[]{:S(2)}) collective-permute-start(bf16[96,128]{1,0:T(8,128)(2,1)S(1)} %get-tuple-element.37), channel_id=1, source_target_pairs={{0,256},{128,384},{256,0},{384,128},{1,257},{129,385},{257,1},{385... | collective-permute-start | bytes 73736 | tf_op jit(solution)/shard_map/ppermute | solution.py:40
  84.9 8.0 %collective-permute-start.8 = (bf16[96,128]{1,0:T(8,128)(2,1)S(1)}, bf16[96,128]{1,0:T(8,128)(2,1)S(1)}, u32[]{:S(2)}, u32[]{:S(2)}) collective-permute-start(bf16[96,128]{1,0:T(8,128)(2,1)S(1)} %get-tuple-element.36), channel_id=1, source_target_pairs={{0,384},{128,0},{256,128},{384,256},{1,385},{129,1},{257,129},{385... | collective-permute-start | bytes 73736 | tf_op jit(solution)/shard_map/ppermute | solution.py:40
  91.0 33.1 %collective-permute-start.3 = (bf16[224,512]{1,0:T(8,128)(2,1)}, bf16[224,512]{1,0:T(8,128)(2,1)}, u32[]{:S(2)}, u32[]{:S(2)}) collective-permute-start(bf16[224,512]{1,0:T(8,128)(2,1)} %get-tuple-element.24), channel_id=1, source_target_pairs={{0,128},{128,256},{256,384},{384,0},{1,129},{129,257},{257,385},{3... | collective-permute-start | bytes 688136 | tf_op jit(solution)/shard_map/ppermute | solution.py:40
  92.9 31.2 %collective-permute-start.4 = (bf16[224,512]{1,0:T(8,128)(2,1)}, bf16[224,512]{1,0:T(8,128)(2,1)}, u32[]{:S(2)}, u32[]{:S(2)}) collective-permute-start(bf16[224,512]{1,0:T(8,128)(2,1)} %get-tuple-element.26), channel_id=1, source_target_pairs={{0,256},{128,384},{256,0},{384,128},{1,257},{129,385},{257,1},{385... | collective-permute-start | bytes 688136 | tf_op jit(solution)/shard_map/ppermute | solution.py:40
  98.4 9.6 %copy-start.2 = (bf16[1,512,224]{1,2,0:T(8,128)(2,1)S(1)}, bf16[1,512,224]{1,2,0:T(8,128)(2,1)}, u32[]{:S(2)}) copy-start(bf16[1,512,224]{1,2,0:T(8,128)(2,1)} %param.12) | copy-start | bytes 688132
  98.4 9.7 %copy-start.3 = (bf16[1,512,224]{1,2,0:T(8,128)(2,1)S(1)}, bf16[1,512,224]{1,2,0:T(8,128)(2,1)}, u32[]{:S(2)}) copy-start(bf16[1,512,224]{1,2,0:T(8,128)(2,1)} %param.13) | copy-start | bytes 688132
  98.4 30.0 %all-to-all-start.4 = ((bf16[8,384,128]{2,1,0:T(8,128)(2,1)}), bf16[8,384,128]{2,1,0:T(8,128)(2,1)S(1)}, u32[]{:S(2)}, u32[]{:S(2)}) async-start(bf16[8,384,128]{2,1,0:T(8,128)(2,1)} %broadcast_in_dim.106), calls=%async_computation.4 | async-start | bytes 1572864 | tf_op jit(solution)/shard_map/all_to_all | solution.py:14
  105.6 18.6 %collective-permute-start.5 = (bf16[224,512]{1,0:T(8,128)(2,1)}, bf16[224,512]{1,0:T(8,128)(2,1)S(1)}, u32[]{:S(2)}, u32[]{:S(2)}) collective-permute-start(bf16[224,512]{1,0:T(8,128)(2,1)} %get-tuple-element.25), channel_id=1, source_target_pairs={{0,384},{128,0},{256,128},{384,256},{1,385},{129,1},{257,129},{385... | collective-permute-start | bytes 688136 | tf_op jit(solution)/shard_map/ppermute | solution.py:40
  123.2 1.1 copy-start.4
  128.4 30.6 %all-to-all-start.2 = ((bf16[32,104,128]{2,1,0:T(8,128)(2,1)}), bf16[32,104,128]{2,1,0:T(8,128)(2,1)S(1)}, u32[]{:S(2)}, u32[]{:S(2)}) async-start(bf16[32,104,128]{2,1,0:T(8,128)(2,1)} %fusion.34), calls=%async_computation.2 | async-start | bytes 1703936 | tf_op jit(solution)/shard_map/all_to_all | solution.py:14
  138.8 12.7 %collective-permute-start.9 = (bf16[224,512]{1,0:T(8,128)(2,1)S(1)}, bf16[224,512]{1,0:T(8,128)(2,1)S(1)}, u32[]{:S(2)}, u32[]{:S(2)}) collective-permute-start(bf16[224,512]{1,0:T(8,128)(2,1)S(1)} %get-tuple-element.14), channel_id=1, source_target_pairs={{0,384},{128,0},{256,128},{384,256},{1,385},{129,1},{257,129},{385... | collective-permute-start | bytes 688136 | tf_op jit(solution)/shard_map/ppermute | solution.py:40
  143.3 10.4 %collective-permute-start.10 = (bf16[224,512]{1,0:T(8,128)(2,1)S(1)}, bf16[224,512]{1,0:T(8,128)(2,1)S(1)}, u32[]{:S(2)}, u32[]{:S(2)}) collective-permute-start(bf16[224,512]{1,0:T(8,128)(2,1)S(1)} %get-tuple-element.13), channel_id=1, source_target_pairs={{0,256},{128,384},{256,0},{384,128},{1,257},{129,385},{257,1},{385... | collective-permute-start | bytes 688136 | tf_op jit(solution)/shard_map/ppermute | solution.py:40
  145.7 13.1 %collective-permute-start.11 = (bf16[224,512]{1,0:T(8,128)(2,1)S(1)}, bf16[224,512]{1,0:T(8,128)(2,1)S(1)}, u32[]{:S(2)}, u32[]{:S(2)}) collective-permute-start(bf16[224,512]{1,0:T(8,128)(2,1)S(1)} %get-tuple-element.12), channel_id=1, source_target_pairs={{0,128},{128,256},{256,384},{384,0},{1,129},{129,257},{257,385},{3... | collective-permute-start | bytes 688136 | tf_op jit(solution)/shard_map/ppermute | solution.py:40
  160.1 17.9 %all-to-all-start.3 = ((bf16[16,32,128]{2,1,0:T(8,128)(2,1)}), bf16[16,32,128]{2,1,0:T(8,128)(2,1)S(1)}, u32[]{:S(2)}, u32[]{:S(2)}) async-start(bf16[16,32,128]{2,1,0:T(8,128)(2,1)} %pad_maximum_fusion.8), calls=%async_computation.3 | async-start | bytes 262144 | tf_op jit(solution)/shard_map/all_to_all | solution.py:14

commit v6 on v5

--- a/solution.py
+++ b/solution.py
@@ -114,7 +114,8 @@
 
     down_part = jnp.concatenate([quarter_at(w_down[0], (xi + nx - k) % nx, nx) for k in range(nx)], axis=1)
     up_part = [quarter_at(w_up[0], (xi + k) % nx, nx) for k in range(nx)]
-    up_part = jnp.concatenate(over_x(up_part, 1), axis=0)
+    up_part = over_x(up_part, 1)
+    up_part = jnp.concatenate(back_in_x(jnp.stack(up_part), xi), axis=0)
 
     own_rows = lax.dynamic_index_in_dim(local_rows, ei, 0, keepdims=False)
     own_rows = jnp.pad(own_rows, (0, lane - cap - PAD), constant_values=-1)
@@ -166,7 +167,7 @@
     up_grad = (hid_grad * active).astype(BF)
     gate_grad = (hid_grad * up_value * sig * (1.0 + gate_value * (1.0 - sig))).astype(BF)
     up_all = lax.all_gather(up_grad, X)
-    up_all = jnp.concatenate(back_in_x(up_all, xi), axis=0)
+    up_all = up_all.reshape(nx * units, slots)
 
     hidden_gated = (hidden.astype(BF).astype(F32) * gate_slot).astype(BF)
     grad_down = dot(hidden_gated, grads_slots, 1, 0).astype(BF)
@@ -182,7 +183,7 @@
     dx_back = exchange(jnp.concatenate([dx_rows, dots_rows], axis=1), (X, Y))
     inputs_slots = dot(place_inputs, joined(inputs_all, quarter), 0, 0).astype(BF)
     grad_up = dot(up_all, inputs_slots, 1, 0).astype(BF).reshape(nx, units, part)
-    up_home = over_x(grad_up, -1)
+    up_home = over_x(back_in_x(grad_up, xi), -1)
     dx_sum = jnp.sum(dx_back.reshape(nx, ny, -1, lane).astype(F32), axis=1)
     dots_sum = jnp.sum(dx_sum[:, quarter * cap], axis=0, keepdims=True)
     gate_tokens = lax.dot_general(

time: 181 us -> 174 us (0.961)
  waiting for transfers between devices: 53 us -> 42.8 us
    all_to_all x5, waiting for transfers between devices: 38.3 us -> 26.8 us  [exchange(): return lax.all_to_all(x, axis, 0, 0, tiled=True)]
  transfers between devices with their start and end apart: 17 -> 17, of which waited for: 6 -> 8; matrix products, arithmetic and copies ran while one was open for 11% -> 13% of each run, Pallas kernels for 0% -> 0%
where the time goes in v6:
time: 174 us; the launch traced here: 172 us
  starting transfers between devices  83.8 us (48%)
  waiting for transfers between devices  42.8 us (25%)
  matrix products  14.8 us (9%)
  blocking collectives  12.6 us (7%)
  other arithmetic  9.19 us (5%)
  local copies, waits for them, and re-layouts  7.88 us (5%)
    all_to_all x5, starting transfers between devices, exchange(): return lax.all_to_all(x, axis, 0, 0, tiled=True)  44.1 us
    ppermute x12, starting transfers between devices, shift(): return lax.ppermute(x, X, [(i, (i + by) % size) for i in range(size)])  39.7 us
    all_to_all x5, waiting for transfers between devices, exchange(): return lax.all_to_all(x, axis, 0, 0, tiled=True)  26.8 us
    ppermute x12, waiting for transfers between devices, shift(): return lax.ppermute(x, X, [(i, (i + by) % size) for i in range(size)])  16 us
    dot_general x10, matrix products, dot(): lax.dot_general(a, b, (((ca,), (cb,)), ((), ())), preferred_element_type=...  14.6 us
    all_gather x1, blocking collectives, local(): up_all = lax.all_gather(up_grad, X)  12.6 us
  transfers between devices with their start and end apart: 17, of which 8 were waited for; matrix products, arithmetic and copies ran while one was open for 13% of the time, Pallas kernels for 0%

profile of v6, /device:TPU:1, one launch (start us, length us, event | category | flops | bytes accessed | tf_op | source)
XLA Modules:
  0.0 172.4 jit_solution(7671446334222543335)
XLA Ops:
  0.7 0.9 convert_reduce_fusion.3
  1.6 1.2 select_reduce_fusion
  2.8 0.1 subtract_select_fusion
  2.9 0.1 iota_compare_fusion.15
  3.1 1.8 %convolution_convert_fusion.3 = bf16[384,256]{1,0:T(8,128)(2,1)} fusion(pred[384,256]{1,0:T(8,128)(4,1)S(1)} %bitcast.198, bf16[256,128]{1,0:T(8,128)(2,1)} %param.9, bf16[256,128]{1,0:T(8,128)(2,1)} %param.8), kind=kOutput, calls=%fused_computation.15 | convolution fusion | flops 50692096 | bytes 425984 | tf_op jit(solution)/shard_map/dot_general | solution.py:23
  4.9 11.8 %all-to-all-start = ((bf16[16,24,256]{2,1,0:T(8,128)(2,1)}), bf16[16,24,256]{2,1,0:T(8,128)(2,1)S(1)}, u32[]{:S(2)}, u32[]{:S(2)}) async-start(bf16[16,24,256]{2,1,0:T(8,128)(2,1)} %bitcast.4), calls=%async_computation | async-start | bytes 393216 | tf_op jit(solution)/shard_map/all_to_all | solution.py:14
  16.7 0.2 fusion.11
  16.9 10.0 %all-to-all-done = bf16[16,24,256]{2,1,0:T(8,128)(2,1)S(1)} async-done(((bf16[16,24,256]{2,1,0:T(8,128)(2,1)}), bf16[16,24,256]{2,1,0:T(8,128)(2,1)S(1)}, u32[]{:S(2)}, u32[]{:S(2)}) %all-to-all-start) | async-done | bytes 196640 | tf_op jit(solution)/shard_map/all_to_all | solution.py:14
  27.0 1.0 broadcast_in_dim.100
  28.0 9.8 %all-to-all-start.1 = ((bf16[32,104,128]{2,1,0:T(8,128)(2,1)}), bf16[32,104,128]{2,1,0:T(8,128)(2,1)S(1)}, u32[]{:S(2)}, u32[]{:S(2)}) async-start(bf16[32,104,128]{2,1,0:T(8,128)(2,1)} %bitcast.10), calls=%async_computation.1 | async-start | bytes 1703936 | tf_op jit(solution)/shard_map/all_to_all | solution.py:14
  37.9 0.8 constant_dynamic-slice_fusion.5
  38.6 3.1 %collective-permute-start.3 = (bf16[224,512]{1,0:T(8,128)(2,1)}, bf16[224,512]{1,0:T(8,128)(2,1)S(1)}, u32[]{:S(2)}, u32[]{:S(2)}) collective-permute-start(bf16[224,512]{1,0:T(8,128)(2,1)} %get-tuple-element.24), channel_id=1, source_target_pairs={{0,128},{128,256},{256,384},{384,0},{1,129},{129,257},{257,385},{3... | collective-permute-start | bytes 688136 | tf_op jit(solution)/shard_map/ppermute | solution.py:40
  41.8 4.3 %collective-permute-start.4 = (bf16[224,512]{1,0:T(8,128)(2,1)S(1)}, bf16[224,512]{1,0:T(8,128)(2,1)S(1)}, u32[]{:S(2)}, u32[]{:S(2)}) collective-permute-start(bf16[224,512]{1,0:T(8,128)(2,1)S(1)} %get-tuple-element.26), channel_id=1, source_target_pairs={{0,256},{128,384},{256,0},{384,128},{1,257},{129,385},{257,1},{385... | collective-permute-start | bytes 688136 | tf_op jit(solution)/shard_map/ppermute | solution.py:40
  46.1 3.1 %collective-permute-start.5 = (bf16[224,512]{1,0:T(8,128)(2,1)S(1)}, bf16[224,512]{1,0:T(8,128)(2,1)S(1)}, u32[]{:S(2)}, u32[]{:S(2)}) collective-permute-start(bf16[224,512]{1,0:T(8,128)(2,1)S(1)} %get-tuple-element.25), channel_id=1, source_target_pairs={{0,384},{128,0},{256,128},{384,256},{1,385},{129,1},{257,129},{385... | collective-permute-start | bytes 688136 | tf_op jit(solution)/shard_map/ppermute | solution.py:40
  49.3 0.7 and_select_fusion.3
  50.0 0.1 convert_reduce_fusion.1
  50.1 0.1 select_reduce_fusion.1
  50.2 0.9 dynamic-slice_bitcast_fusion.17
  51.2 0.8 multiply_add_fusion
  51.9 8.4 %all-to-all-done.1 = bf16[32,104,128]{2,1,0:T(8,128)(2,1)S(1)} async-done(((bf16[32,104,128]{2,1,0:T(8,128)(2,1)}), bf16[32,104,128]{2,1,0:T(8,128)(2,1)S(1)}, u32[]{:S(2)}, u32[]{:S(2)}) %all-to-all-start.1) | async-done | bytes 852000 | tf_op jit(solution)/shard_map/all_to_all | solution.py:14
  60.4 0.3 copy.29
  60.7 1.4 fusion.6
  62.1 1.9 %collective-permute-start = (bf16[512,512]{0,1:T(8,128)(2,1)}, bf16[512,512]{0,1:T(8,128)(2,1)}, u32[]{:S(2)}, u32[]{:S(2)}) collective-permute-start(bf16[512,512]{0,1:T(8,128)(2,1)} %fusion.6), channel_id=1, source_target_pairs={{0,128},{128,256},{256,384},{384,0},{1,129},{129,257},{257,385},{3... | collective-permute-start | bytes 1572872 | tf_op jit(solution)/shard_map/ppermute | solution.py:40
  64.0 3.9 %collective-permute-start.1 = (bf16[512,512]{0,1:T(8,128)(2,1)}, bf16[512,512]{0,1:T(8,128)(2,1)}, u32[]{:S(2)}, u32[]{:S(2)}) collective-permute-start(bf16[512,512]{0,1:T(8,128)(2,1)} %fusion.6), channel_id=1, source_target_pairs={{0,256},{128,384},{256,0},{384,128},{1,257},{129,385},{257,1},{385... | collective-permute-start | bytes 1572872 | tf_op jit(solution)/shard_map/ppermute | solution.py:40
  67.9 2.9 %collective-permute-start.2 = (bf16[512,512]{0,1:T(8,128)(2,1)}, bf16[512,512]{0,1:T(8,128)(2,1)}, u32[]{:S(2)}, u32[]{:S(2)}) collective-permute-start(bf16[512,512]{0,1:T(8,128)(2,1)} %fusion.6), channel_id=1, source_target_pairs={{0,384},{128,0},{256,128},{384,256},{1,385},{129,1},{257,129},{385... | collective-permute-start | bytes 1572872 | tf_op jit(solution)/shard_map/ppermute | solution.py:40
  70.9 2.4 %collective-permute-start.6 = (bf16[96,128]{1,0:T(8,128)(2,1)S(1)}, bf16[96,128]{1,0:T(8,128)(2,1)S(1)}, u32[]{:S(2)}, u32[]{:S(2)}) collective-permute-start(bf16[96,128]{1,0:T(8,128)(2,1)S(1)} %get-tuple-element.38), channel_id=1, source_target_pairs={{0,128},{128,256},{256,384},{384,0},{1,129},{129,257},{257,385},{3... | collective-permute-start | bytes 73736 | tf_op jit(solution)/shard_map/ppermute | solution.py:40
  73.3 0.1 pad_maximum_fusion.1
  73.4 3.5 %collective-permute-start.7 = (bf16[96,128]{1,0:T(8,128)(2,1)S(1)}, bf16[96,128]{1,0:T(8,128)(2,1)S(1)}, u32[]{:S(2)}, u32[]{:S(2)}) collective-permute-start(bf16[96,128]{1,0:T(8,128)(2,1)S(1)} %get-tuple-element.37), channel_id=1, source_target_pairs={{0,256},{128,384},{256,0},{384,128},{1,257},{129,385},{257,1},{385... | collective-permute-start | bytes 73736 | tf_op jit(solution)/shard_map/ppermute | solution.py:40
  76.9 8.1 %collective-permute-done.6 = bf16[96,128]{1,0:T(8,128)(2,1)S(1)} collective-permute-done((bf16[96,128]{1,0:T(8,128)(2,1)S(1)}, bf16[96,128]{1,0:T(8,128)(2,1)S(1)}, u32[]{:S(2)}, u32[]{:S(2)}) %collective-permute-start.6) | collective-permute-done | bytes 24608 | tf_op jit(solution)/shard_map/ppermute | solution.py:40
  85.0 5.1 %collective-permute-start.8 = (bf16[96,128]{1,0:T(8,128)(2,1)S(1)}, bf16[96,128]{1,0:T(8,128)(2,1)S(1)}, u32[]{:S(2)}, u32[]{:S(2)}) collective-permute-start(bf16[96,128]{1,0:T(8,128)(2,1)S(1)} %get-tuple-element.36), channel_id=1, source_target_pairs={{0,384},{128,0},{256,128},{384,256},{1,385},{129,1},{257,129},{385... | collective-permute-start | bytes 73736 | tf_op jit(solution)/shard_map/ppermute | solution.py:40
  90.1 0.9 dynamic-slice_bitcast_fusion.10
  91.1 1.5 collective-permute-done.8
  92.6 1.0 broadcast_in_dim.106
  93.6 5.7 %all-to-all-start.4 = ((bf16[8,384,128]{2,1,0:T(8,128)(2,1)}), bf16[8,384,128]{2,1,0:T(8,128)(2,1)S(1)}, u32[]{:S(2)}, u32[]{:S(2)}) async-start(bf16[8,384,128]{2,1,0:T(8,128)(2,1)} %broadcast_in_dim.106), calls=%async_computation.4 | async-start | bytes 1572864 | tf_op jit(solution)/shard_map/all_to_all | solution.py:14
  99.3 0.2 fusion.8
  99.6 3.0 %multiply_convert_fusion.1 = (bf16[224,512]{1,0:T(8,128)(2,1)S(1)}, bf16[512]{0:T(512)(128)(2,1)S(1)}, f32[224,512]{1,0:T(8,128)}) fusion(f32[512]{0:T(512)S(1)} %fusion.8, bf16[1,512,224]{1,2,0:T(8,128)(2,1)S(1)} %copy-done.3, bf16[1,512,224]{1,2,0:T(8,128)(2,1)S(1)} %copy-done.5, bf16[512,512]{0,1:T(8,128)(2,1)} %collective-permute-done.2, ...), kind=kOutput, calls=%fused_computation.75 | convolution fusion | flops 483196416 | bytes 4164608 | tf_op jit(solution)/shard_map/dot_general | solution.py:23
  102.6 12.6 %all-gather = bf16[896,512]{1,0:T(8,128)(2,1)S(1)} all-gather(bf16[224,512]{1,0:T(8,128)(2,1)S(1)} %get-tuple-element.31), channel_id=2, replica_groups=mesh['dp_0'=4,'dp_1'=8,'expert'=16] {'dp_0'}, dimensions={0}, use_global_device_ids=true | all-gather | bytes 1146880 | tf_op jit(solution)/shard_map/all_gather | solution.py:169
  115.2 2.1 %fusion.4 = bf16[768,512]{1,0:T(8,128)(2,1)S(1)} fusion(bf16[896,512]{1,0:T(8,128)(2,1)S(1)} %all-gather, bf16[224,512]{1,0:T(8,128)(2,1)S(1)} %copy-done.12, bf16[224,512]{1,0:T(8,128)(2,1)S(1)} %copy-done.13, bf16[224,512]{1,0:T(8,128)(2,1)} %get-tuple-element.22, bf16[224,512]{1,0:T(8,128)(2,1)S(1)} %copy-done.11, s32[512]{0:T(512)S(1)} %bitcast.207), kind=kOutput, calls=%fused_computation.11 | convolution fusion | flops 877133824 | bytes 2623488 | tf_op jit(solution)/shard_map/dot_general | solution.py:23
  117.3 0.2 reshape.198
  117.5 0.1 copy.30
  117.6 0.2 fusion.9
  117.8 1.0 fusion.34
  118.8 0.8 all-to-all-done.4
  119.6 8.4 %all-to-all-start.2 = ((bf16[32,104,128]{2,1,0:T(8,128)(2,1)}), bf16[32,104,128]{2,1,0:T(8,128)(2,1)S(1)}, u32[]{:S(2)}, u32[]{:S(2)}) async-start(bf16[32,104,128]{2,1,0:T(8,128)(2,1)} %fusion.34), calls=%async_computation.2 | async-start | bytes 1703936 | tf_op jit(solution)/shard_map/all_to_all | solution.py:14
  128.0 1.2 copy.32
  129.2 2.3 %convolution_convert_fusion.1 = bf16[896,512]{1,0:T(8,128)(2,1)S(1)} fusion(bf16[896,512]{1,0:T(8,128)(2,1)S(1)} %all-gather, bf16[96,8,4,128]{3,2,1,0:T(4,128)(2,1)} %bitcast.186, s32[512]{0:T(512)S(1)} %bitcast.205), kind=kOutput, calls=%fused_computation.10 | convolution fusion | flops 873529344 | bytes 2623488 | tf_op jit(solution)/shard_map/dot_general | solution.py:23
  131.6 4.5 %collective-permute-start.9 = (bf16[224,512]{1,0:T(8,128)(2,1)S(1)}, bf16[224,512]{1,0:T(8,128)(2,1)S(1)}, u32[]{:S(2)}, u32[]{:S(2)}) collective-permute-start(bf16[224,512]{1,0:T(8,128)(2,1)S(1)} %get-tuple-element.14), channel_id=1, source_target_pairs={{0,384},{128,0},{256,128},{384,256},{1,385},{129,1},{257,129},{385... | collective-permute-start | bytes 688136 | tf_op jit(solution)/shard_map/ppermute | solution.py:40
  136.1 2.4 %collective-permute-start.10 = (bf16[224,512]{1,0:T(8,128)(2,1)S(1)}, bf16[224,512]{1,0:T(8,128)(2,1)S(1)}, u32[]{:S(2)}, u32[]{:S(2)}) collective-permute-start(bf16[224,512]{1,0:T(8,128)(2,1)S(1)} %get-tuple-element.13), channel_id=1, source_target_pairs={{0,256},{128,384},{256,0},{384,128},{1,257},{129,385},{257,1},{385... | collective-permute-start | bytes 688136 | tf_op jit(solution)/shard_map/ppermute | solution.py:40
  138.6 2.5 %collective-permute-start.11 = (bf16[224,512]{1,0:T(8,128)(2,1)S(1)}, bf16[224,512]{1,0:T(8,128)(2,1)S(1)}, u32[]{:S(2)}, u32[]{:S(2)}) collective-permute-start(bf16[224,512]{1,0:T(8,128)(2,1)S(1)} %get-tuple-element.12), channel_id=1, source_target_pairs={{0,128},{128,256},{256,384},{384,0},{1,129},{129,257},{257,385},{3... | collective-permute-start | bytes 688136 | tf_op jit(solution)/shard_map/ppermute | solution.py:40
  141.1 2.3 %convolution_convert_fusion = bf16[224,2048]{1,0:T(8,128)(2,1)S(1)} fusion(bf16[512,512]{0,1:T(8,128)(2,1)} %collective-permute-done.2, bf16[512,512]{0,1:T(8,128)(2,1)} %collective-permute-done.1, bf16[512,512]{0,1:T(8,128)(2,1)} %collective-permute-done, bf16[512,512]{0,1:T(8,128)(2,1)} %fusion.6, bf16[1,512,224]{1,2,0:T(8,128)(2,1)S(1)} %copy-done.6, ...), kind=kOutput, calls=%fused_computation | convolution fusion | flops 479870976 | bytes 3475456 | tf_op jit(solution)/shard_map/dot_general | solution.py:23
  143.4 0.1 constant_dynamic-slice_fusion.4
  143.5 0.9 copy-done.2
  144.5 0.9 fusion.61
  145.4 1.3 collective-permute-done.10
  146.6 5.1 %collective-permute-done.11 = bf16[224,512]{1,0:T(8,128)(2,1)S(1)} collective-permute-done((bf16[224,512]{1,0:T(8,128)(2,1)S(1)}, bf16[224,512]{1,0:T(8,128)(2,1)S(1)}, u32[]{:S(2)}, u32[]{:S(2)}) %collective-permute-start.11) | collective-permute-done | bytes 229408 | tf_op jit(solution)/shard_map/ppermute | solution.py:40
  151.8 0.1 pad_maximum_fusion.2
  152.0 0.1 convert_reduce_fusion
  152.1 0.2 reduce-precision_convert_fusion
  152.4 0.7 pad_maximum_fusion.5
  153.1 8.4 %all-to-all-start.3 = ((bf16[16,32,128]{2,1,0:T(8,128)(2,1)}), bf16[16,32,128]{2,1,0:T(8,128)(2,1)S(1)}, u32[]{:S(2)}, u32[]{:S(2)}) async-start(bf16[16,32,128]{2,1,0:T(8,128)(2,1)} %pad_maximum_fusion.5), calls=%async_computation.3 | async-start | bytes 262144 | tf_op jit(solution)/shard_map/all_to_all | solution.py:14
  161.5 1.5 maximum_bitcast_fusion
  163.0 7.7 %all-to-all-done.3 = bf16[16,32,128]{2,1,0:T(8,128)(2,1)S(1)} async-done(((bf16[16,32,128]{2,1,0:T(8,128)(2,1)}), bf16[16,32,128]{2,1,0:T(8,128)(2,1)S(1)}, u32[]{:S(2)}, u32[]{:S(2)}) %all-to-all-start.3) | async-done | bytes 131104 | tf_op jit(solution)/shard_map/all_to_all | solution.py:14
  170.8 0.6 mul.112
  171.4 1.1 fusion.7
  (65 shorter events, 0.7 us)
Async XLA Ops:
  0.6 16.1 %copy-start.14 = (f32[1,256]{1,0:T(1,128)S(1)}, f32[1,256]{1,0:T(1,128)}, u32[]{:S(2)}) copy-start(f32[1,256]{1,0:T(1,128)} %param.10) | copy-start | bytes 3076
  4.9 22.0 %all-to-all-start = ((bf16[16,24,256]{2,1,0:T(8,128)(2,1)}), bf16[16,24,256]{2,1,0:T(8,128)(2,1)S(1)}, u32[]{:S(2)}, u32[]{:S(2)}) async-start(bf16[16,24,256]{2,1,0:T(8,128)(2,1)} %bitcast.4), calls=%async_computation | async-start | bytes 393216 | tf_op jit(solution)/shard_map/all_to_all | solution.py:14
  28.0 9.9 %copy-start = (bf16[1,224,2048]{2,1,0:T(8,128)(2,1)S(1)}, bf16[1,224,2048]{2,1,0:T(8,128)(2,1)}, u32[]{:S(2)}) copy-start(bf16[1,224,2048]{2,1,0:T(8,128)(2,1)} %param.15) | copy-start | bytes 2752516
  28.0 32.3 %all-to-all-start.1 = ((bf16[32,104,128]{2,1,0:T(8,128)(2,1)}), bf16[32,104,128]{2,1,0:T(8,128)(2,1)S(1)}, u32[]{:S(2)}, u32[]{:S(2)}) async-start(bf16[32,104,128]{2,1,0:T(8,128)(2,1)} %bitcast.10), calls=%async_computation.1 | async-start | bytes 1703936 | tf_op jit(solution)/shard_map/all_to_all | solution.py:14
  37.9 12.4 %copy-start.1 = (bf16[1,224,2048]{2,1,0:T(8,128)(2,1)S(1)}, bf16[1,224,2048]{2,1,0:T(8,128)(2,1)}, u32[]{:S(2)}) copy-start(bf16[1,224,2048]{2,1,0:T(8,128)(2,1)} %param.14) | copy-start | bytes 2752516
  38.6 29.3 %collective-permute-start.3 = (bf16[224,512]{1,0:T(8,128)(2,1)}, bf16[224,512]{1,0:T(8,128)(2,1)S(1)}, u32[]{:S(2)}, u32[]{:S(2)}) collective-permute-start(bf16[224,512]{1,0:T(8,128)(2,1)} %get-tuple-element.24), channel_id=1, source_target_pairs={{0,128},{128,256},{256,384},{384,0},{1,129},{129,257},{257,385},{3... | collective-permute-start | bytes 688136 | tf_op jit(solution)/shard_map/ppermute | solution.py:40
  41.8 29.1 %collective-permute-start.4 = (bf16[224,512]{1,0:T(8,128)(2,1)S(1)}, bf16[224,512]{1,0:T(8,128)(2,1)S(1)}, u32[]{:S(2)}, u32[]{:S(2)}) collective-permute-start(bf16[224,512]{1,0:T(8,128)(2,1)S(1)} %get-tuple-element.26), channel_id=1, source_target_pairs={{0,256},{128,384},{256,0},{384,128},{1,257},{129,385},{257,1},{385... | collective-permute-start | bytes 688136 | tf_op jit(solution)/shard_map/ppermute | solution.py:40
  46.1 27.1 %collective-permute-start.5 = (bf16[224,512]{1,0:T(8,128)(2,1)S(1)}, bf16[224,512]{1,0:T(8,128)(2,1)S(1)}, u32[]{:S(2)}, u32[]{:S(2)}) collective-permute-start(bf16[224,512]{1,0:T(8,128)(2,1)S(1)} %get-tuple-element.25), channel_id=1, source_target_pairs={{0,384},{128,0},{256,128},{384,256},{1,385},{129,1},{257,129},{385... | collective-permute-start | bytes 688136 | tf_op jit(solution)/shard_map/ppermute | solution.py:40
  62.1 37.4 %collective-permute-start = (bf16[512,512]{0,1:T(8,128)(2,1)}, bf16[512,512]{0,1:T(8,128)(2,1)}, u32[]{:S(2)}, u32[]{:S(2)}) collective-permute-start(bf16[512,512]{0,1:T(8,128)(2,1)} %fusion.6), channel_id=1, source_target_pairs={{0,128},{128,256},{256,384},{384,0},{1,129},{129,257},{257,385},{3... | collective-permute-start | bytes 1572872 | tf_op jit(solution)/shard_map/ppermute | solution.py:40
  64.0 35.5 %collective-permute-start.1 = (bf16[512,512]{0,1:T(8,128)(2,1)}, bf16[512,512]{0,1:T(8,128)(2,1)}, u32[]{:S(2)}, u32[]{:S(2)}) collective-permute-start(bf16[512,512]{0,1:T(8,128)(2,1)} %fusion.6), channel_id=1, source_target_pairs={{0,256},{128,384},{256,0},{384,128},{1,257},{129,385},{257,1},{385... | collective-permute-start | bytes 1572872 | tf_op jit(solution)/shard_map/ppermute | solution.py:40
  67.9 31.6 %collective-permute-start.2 = (bf16[512,512]{0,1:T(8,128)(2,1)}, bf16[512,512]{0,1:T(8,128)(2,1)}, u32[]{:S(2)}, u32[]{:S(2)}) collective-permute-start(bf16[512,512]{0,1:T(8,128)(2,1)} %fusion.6), channel_id=1, source_target_pairs={{0,384},{128,0},{256,128},{384,256},{1,385},{129,1},{257,129},{385... | collective-permute-start | bytes 1572872 | tf_op jit(solution)/shard_map/ppermute | solution.py:40
  70.9 14.1 %collective-permute-start.6 = (bf16[96,128]{1,0:T(8,128)(2,1)S(1)}, bf16[96,128]{1,0:T(8,128)(2,1)S(1)}, u32[]{:S(2)}, u32[]{:S(2)}) collective-permute-start(bf16[96,128]{1,0:T(8,128)(2,1)S(1)} %get-tuple-element.38), channel_id=1, source_target_pairs={{0,128},{128,256},{256,384},{384,0},{1,129},{129,257},{257,385},{3... | collective-permute-start | bytes 73736 | tf_op jit(solution)/shard_map/ppermute | solution.py:40
  73.4 17.7 %collective-permute-start.7 = (bf16[96,128]{1,0:T(8,128)(2,1)S(1)}, bf16[96,128]{1,0:T(8,128)(2,1)S(1)}, u32[]{:S(2)}, u32[]{:S(2)}) collective-permute-start(bf16[96,128]{1,0:T(8,128)(2,1)S(1)} %get-tuple-element.37), channel_id=1, source_target_pairs={{0,256},{128,384},{256,0},{384,128},{1,257},{129,385},{257,1},{385... | collective-permute-start | bytes 73736 | tf_op jit(solution)/shard_map/ppermute | solution.py:40
  85.0 7.6 %collective-permute-start.8 = (bf16[96,128]{1,0:T(8,128)(2,1)S(1)}, bf16[96,128]{1,0:T(8,128)(2,1)S(1)}, u32[]{:S(2)}, u32[]{:S(2)}) collective-permute-start(bf16[96,128]{1,0:T(8,128)(2,1)S(1)} %get-tuple-element.36), channel_id=1, source_target_pairs={{0,384},{128,0},{256,128},{384,256},{1,385},{129,1},{257,129},{385... | collective-permute-start | bytes 73736 | tf_op jit(solution)/shard_map/ppermute | solution.py:40
  93.6 6.0 %copy-start.3 = (bf16[1,512,224]{1,2,0:T(8,128)(2,1)S(1)}, bf16[1,512,224]{1,2,0:T(8,128)(2,1)}, u32[]{:S(2)}) copy-start(bf16[1,512,224]{1,2,0:T(8,128)(2,1)} %param.12) | copy-start | bytes 688132
  93.6 6.0 %copy-start.5 = (bf16[1,512,224]{1,2,0:T(8,128)(2,1)S(1)}, bf16[1,512,224]{1,2,0:T(8,128)(2,1)}, u32[]{:S(2)}) copy-start(bf16[1,512,224]{1,2,0:T(8,128)(2,1)} %param.13) | copy-start | bytes 688132
  93.6 6.0 %copy-start.7 = (bf16[224,512]{1,0:T(8,128)(2,1)S(1)}, bf16[224,512]{1,0:T(8,128)(2,1)}, u32[]{:S(2)}) copy-start(bf16[224,512]{1,0:T(8,128)(2,1)} %get-tuple-element.27) | copy-start | bytes 688132
  93.6 6.0 %copy-start.8 = (bf16[224,512]{1,0:T(8,128)(2,1)S(1)}, bf16[224,512]{1,0:T(8,128)(2,1)}, u32[]{:S(2)}) copy-start(bf16[224,512]{1,0:T(8,128)(2,1)} %get-tuple-element.28) | copy-start | bytes 688132
  93.6 6.0 %copy-start.9 = (bf16[224,512]{1,0:T(8,128)(2,1)S(1)}, bf16[224,512]{1,0:T(8,128)(2,1)}, u32[]{:S(2)}) copy-start(bf16[224,512]{1,0:T(8,128)(2,1)} %get-tuple-element.29) | copy-start | bytes 688132
  93.6 6.0 %copy-start.10 = (bf16[224,512]{1,0:T(8,128)(2,1)S(1)}, bf16[224,512]{1,0:T(8,128)(2,1)}, u32[]{:S(2)}) copy-start(bf16[224,512]{1,0:T(8,128)(2,1)} %get-tuple-element.30) | copy-start | bytes 688132
  93.6 26.0 %all-to-all-start.4 = ((bf16[8,384,128]{2,1,0:T(8,128)(2,1)}), bf16[8,384,128]{2,1,0:T(8,128)(2,1)S(1)}, u32[]{:S(2)}, u32[]{:S(2)}) async-start(bf16[8,384,128]{2,1,0:T(8,128)(2,1)} %broadcast_in_dim.106), calls=%async_computation.4 | async-start | bytes 1572864 | tf_op jit(solution)/shard_map/all_to_all | solution.py:14
  102.6 12.6 %copy-start.11 = (bf16[224,512]{1,0:T(8,128)(2,1)S(1)}, bf16[224,512]{1,0:T(8,128)(2,1)}, u32[]{:S(2)}) copy-start(bf16[224,512]{1,0:T(8,128)(2,1)} %get-tuple-element.19) | copy-start | bytes 688132
  102.6 12.6 %copy-start.12 = (bf16[224,512]{1,0:T(8,128)(2,1)S(1)}, bf16[224,512]{1,0:T(8,128)(2,1)}, u32[]{:S(2)}) copy-start(bf16[224,512]{1,0:T(8,128)(2,1)} %get-tuple-element.20) | copy-start | bytes 688132
  102.6 12.6 %copy-start.13 = (bf16[224,512]{1,0:T(8,128)(2,1)S(1)}, bf16[224,512]{1,0:T(8,128)(2,1)}, u32[]{:S(2)}) copy-start(bf16[224,512]{1,0:T(8,128)(2,1)} %get-tuple-element.21) | copy-start | bytes 688132
  119.6 32.4 %all-to-all-start.2 = ((bf16[32,104,128]{2,1,0:T(8,128)(2,1)}), bf16[32,104,128]{2,1,0:T(8,128)(2,1)S(1)}, u32[]{:S(2)}, u32[]{:S(2)}) async-start(bf16[32,104,128]{2,1,0:T(8,128)(2,1)} %fusion.34), calls=%async_computation.2 | async-start | bytes 1703936 | tf_op jit(solution)/shard_map/all_to_all | solution.py:14
  131.5 9.6 %copy-start.4 = (bf16[1,512,224]{1,2,0:T(8,128)(2,1)S(1)}, bf16[1,512,224]{1,2,0:T(8,128)(2,1)}, u32[]{:S(2)}) copy-start(bf16[1,512,224]{1,2,0:T(8,128)(2,1)} %param.12) | copy-start | bytes 688132
  131.5 9.6 %copy-start.6 = (bf16[1,512,224]{1,2,0:T(8,128)(2,1)S(1)}, bf16[1,512,224]{1,2,0:T(8,128)(2,1)}, u32[]{:S(2)}) copy-start(bf16[1,512,224]{1,2,0:T(8,128)(2,1)} %param.13) | copy-start | bytes 688132
  131.6 13.8 %collective-permute-start.9 = (bf16[224,512]{1,0:T(8,128)(2,1)S(1)}, bf16[224,512]{1,0:T(8,128)(2,1)S(1)}, u32[]{:S(2)}, u32[]{:S(2)}) collective-permute-start(bf16[224,512]{1,0:T(8,128)(2,1)S(1)} %get-tuple-element.14), channel_id=1, source_target_pairs={{0,384},{128,0},{256,128},{384,256},{1,385},{129,1},{257,129},{385... | collective-permute-start | bytes 688136 | tf_op jit(solution)/shard_map/ppermute | solution.py:40
  136.1 10.5 %collective-permute-start.10 = (bf16[224,512]{1,0:T(8,128)(2,1)S(1)}, bf16[224,512]{1,0:T(8,128)(2,1)S(1)}, u32[]{:S(2)}, u32[]{:S(2)}) collective-permute-start(bf16[224,512]{1,0:T(8,128)(2,1)S(1)} %get-tuple-element.13), channel_id=1, source_target_pairs={{0,256},{128,384},{256,0},{384,128},{1,257},{129,385},{257,1},{385... | collective-permute-start | bytes 688136 | tf_op jit(solution)/shard_map/ppermute | solution.py:40
  138.6 13.2 %collective-permute-start.11 = (bf16[224,512]{1,0:T(8,128)(2,1)S(1)}, bf16[224,512]{1,0:T(8,128)(2,1)S(1)}, u32[]{:S(2)}, u32[]{:S(2)}) collective-permute-start(bf16[224,512]{1,0:T(8,128)(2,1)S(1)} %get-tuple-element.12), channel_id=1, source_target_pairs={{0,128},{128,256},{256,384},{384,0},{1,129},{129,257},{257,385},{3... | collective-permute-start | bytes 688136 | tf_op jit(solution)/shard_map/ppermute | solution.py:40
  143.4 1.0 copy-start.2
  153.1 17.6 %all-to-all-start.3 = ((bf16[16,32,128]{2,1,0:T(8,128)(2,1)}), bf16[16,32,128]{2,1,0:T(8,128)(2,1)S(1)}, u32[]{:S(2)}, u32[]{:S(2)}) async-start(bf16[16,32,128]{2,1,0:T(8,128)(2,1)} %pad_maximum_fusion.5), calls=%async_computation.3 | async-start | bytes 262144 | tf_op jit(solution)/shard_map/all_to_all | solution.py:14

commit v7 on v6

--- a/solution.py
+++ b/solution.py
@@ -112,7 +112,8 @@
     sent = dot(sent_pick, both, 1, 0).astype(BF).reshape(ne, cap, 2 * width_dev)
     rows = exchange(sent, E).reshape(nx, quarter, cap, 2 * width_dev)
 
-    down_part = jnp.concatenate([quarter_at(w_down[0], (xi + nx - k) % nx, nx) for k in range(nx)], axis=1)
+    down_part = [quarter_at(w_down[0], (xi + nx - k) % nx, nx) for k in range(nx)]
+    down_near = jnp.concatenate(down_part[:-1], axis=1)
     up_part = [quarter_at(w_up[0], (xi + k) % nx, nx) for k in range(nx)]
     up_part = over_x(up_part, 1)
     up_part = jnp.concatenate(back_in_x(jnp.stack(up_part), xi), axis=0)
@@ -160,8 +161,10 @@
     gate_slot = jnp.sum(
         jnp.where(owner_hit, dot(gates_all, within_hit, 1, 0), 0.0), axis=0, keepdims=True
     )
-    grads_slots = jnp.concatenate(over_x([grads_slots] * nx, 1), axis=1)
-    raw_grad = dot(down_part, grads_slots, 1, 1)
+    grads_slots = over_x([grads_slots] * nx, 1)
+    raw_near = dot(down_near, jnp.concatenate(grads_slots[:-1], axis=1), 1, 1)
+    raw_grad = lax.optimization_barrier(raw_near) + dot(down_part[-1], grads_slots[-1], 1, 1)
+    grads_slots = jnp.concatenate(grads_slots, axis=1)
     dots = jnp.sum(hidden * raw_grad, axis=0, keepdims=True)
     hid_grad = gate_slot * raw_grad
     up_grad = (hid_grad * active).astype(BF)

time: 174 us -> 170 us (0.977)
  starting transfers between devices: 83.8 us -> 75.9 us
  waiting for transfers between devices: 42.8 us -> 49 us
  matrix products: 14.8 us -> 12.8 us
    all_to_all x5, starting transfers between devices: 44.1 us -> 36.8 us  [exchange(): return lax.all_to_all(x, axis, 0, 0, tiled=True)]
    ppermute x12, waiting for transfers between devices: 16 us -> 19.2 us  [shift(): return lax.ppermute(x, X, [(i, (i + by) % size) for i in range(size)])]
    all_to_all x5, waiting for transfers between devices: 26.8 us -> 29.8 us  [exchange(): return lax.all_to_all(x, axis, 0, 0, tiled=True)]
    dot_general x10 -> x11, matrix products: 14.6 us -> 12.6 us  [dot(): lax.dot_general(a, b, (((ca,), (cb,)), ((), ())), preferred_element_type=...]
  transfers between devices with their start and end apart: 17 -> 17, of which waited for: 8 -> 8; matrix products, arithmetic and copies ran while one was open for 13% -> 12% of each run, Pallas kernels for 0% -> 0%
where the time goes in v7:
time: 170 us; the launch traced here: 169 us
  starting transfers between devices  75.9 us (45%)
  waiting for transfers between devices  49 us (29%)
  matrix products  12.8 us (8%)
  blocking collectives  11.7 us (7%)
  other arithmetic  9.87 us (6%)
  local copies, waits for them, and re-layouts  7.76 us (5%)
    ppermute x12, starting transfers between devices, shift(): return lax.ppermute(x, X, [(i, (i + by) % size) for i in range(size)])  39.1 us
    all_to_all x5, starting transfers between devices, exchange(): return lax.all_to_all(x, axis, 0, 0, tiled=True)  36.8 us
    all_to_all x5, waiting for transfers between devices, exchange(): return lax.all_to_all(x, axis, 0, 0, tiled=True)  29.8 us
    ppermute x12, waiting for transfers between devices, shift(): return lax.ppermute(x, X, [(i, (i + by) % size) for i in range(size)])  19.2 us
    dot_general x11, matrix products, dot(): lax.dot_general(a, b, (((ca,), (cb,)), ((), ())), preferred_element_type=...  12.6 us
    all_gather x1, blocking collectives, local(): up_all = lax.all_gather(up_grad, X)  11.7 us
  transfers between devices with their start and end apart: 17, of which 8 were waited for; matrix products, arithmetic and copies ran while one was open for 12% of the time, Pallas kernels for 0%

profile of v7, /device:TPU:1, one launch (start us, length us, event | category | flops | bytes accessed | tf_op | source)
XLA Modules:
  0.0 168.5 jit_solution(3653155663371587274)
XLA Ops:
  0.7 0.9 convert_reduce_fusion.3
  1.6 1.2 select_reduce_fusion
  2.9 0.1 iota_compare_fusion.15
  3.1 1.8 %convolution_convert_fusion.3 = bf16[384,256]{1,0:T(8,128)(2,1)} fusion(pred[384,256]{1,0:T(8,128)(4,1)S(1)} %bitcast.218, bf16[256,128]{1,0:T(8,128)(2,1)} %param.9, bf16[256,128]{1,0:T(8,128)(2,1)} %param.8), kind=kOutput, calls=%fused_computation.27 | convolution fusion | flops 50692096 | bytes 425984 | tf_op jit(solution)/shard_map/dot_general | solution.py:23
  4.9 11.8 %all-to-all-start = ((bf16[16,24,256]{2,1,0:T(8,128)(2,1)}), bf16[16,24,256]{2,1,0:T(8,128)(2,1)S(1)}, u32[]{:S(2)}, u32[]{:S(2)}) async-start(bf16[16,24,256]{2,1,0:T(8,128)(2,1)} %bitcast.4), calls=%async_computation | async-start | bytes 393216 | tf_op jit(solution)/shard_map/all_to_all | solution.py:14
  16.7 0.2 fusion.24
  16.9 9.9 %all-to-all-done = bf16[16,24,256]{2,1,0:T(8,128)(2,1)S(1)} async-done(((bf16[16,24,256]{2,1,0:T(8,128)(2,1)}), bf16[16,24,256]{2,1,0:T(8,128)(2,1)S(1)}, u32[]{:S(2)}, u32[]{:S(2)}) %all-to-all-start) | async-done | bytes 196640 | tf_op jit(solution)/shard_map/all_to_all | solution.py:14
  27.0 1.0 broadcast_in_dim.100
  28.0 9.8 %all-to-all-start.1 = ((bf16[32,104,128]{2,1,0:T(8,128)(2,1)}), bf16[32,104,128]{2,1,0:T(8,128)(2,1)S(1)}, u32[]{:S(2)}, u32[]{:S(2)}) async-start(bf16[32,104,128]{2,1,0:T(8,128)(2,1)} %bitcast.10), calls=%async_computation.1 | async-start | bytes 1703936 | tf_op jit(solution)/shard_map/all_to_all | solution.py:14
  37.9 0.8 constant_dynamic-slice_fusion.5
  38.7 3.1 %collective-permute-start.3 = (bf16[224,512]{1,0:T(8,128)(2,1)}, bf16[224,512]{1,0:T(8,128)(2,1)S(1)}, u32[]{:S(2)}, u32[]{:S(2)}) collective-permute-start(bf16[224,512]{1,0:T(8,128)(2,1)} %get-tuple-element.27), channel_id=1, source_target_pairs={{0,128},{128,256},{256,384},{384,0},{1,129},{129,257},{257,385},{3... | collective-permute-start | bytes 688136 | tf_op jit(solution)/shard_map/ppermute | solution.py:40
  41.8 3.4 %collective-permute-start.5 = (bf16[224,512]{1,0:T(8,128)(2,1)S(1)}, bf16[224,512]{1,0:T(8,128)(2,1)S(1)}, u32[]{:S(2)}, u32[]{:S(2)}) collective-permute-start(bf16[224,512]{1,0:T(8,128)(2,1)S(1)} %get-tuple-element.28), channel_id=1, source_target_pairs={{0,384},{128,0},{256,128},{384,256},{1,385},{129,1},{257,129},{385... | collective-permute-start | bytes 688136 | tf_op jit(solution)/shard_map/ppermute | solution.py:40
  45.2 3.4 %collective-permute-start.4 = (bf16[224,512]{1,0:T(8,128)(2,1)S(1)}, bf16[224,512]{1,0:T(8,128)(2,1)S(1)}, u32[]{:S(2)}, u32[]{:S(2)}) collective-permute-start(bf16[224,512]{1,0:T(8,128)(2,1)S(1)} %get-tuple-element.29), channel_id=1, source_target_pairs={{0,256},{128,384},{256,0},{384,128},{1,257},{129,385},{257,1},{385... | collective-permute-start | bytes 688136 | tf_op jit(solution)/shard_map/ppermute | solution.py:40
  48.7 0.7 and_select_fusion.3
  49.4 0.1 convert_reduce_fusion.1
  49.6 0.9 dynamic-slice_bitcast_fusion.16
  50.5 1.3 multiply_add_fusion
  51.8 8.5 %all-to-all-done.1 = bf16[32,104,128]{2,1,0:T(8,128)(2,1)S(1)} async-done(((bf16[32,104,128]{2,1,0:T(8,128)(2,1)}), bf16[32,104,128]{2,1,0:T(8,128)(2,1)S(1)}, u32[]{:S(2)}, u32[]{:S(2)}) %all-to-all-start.1) | async-done | bytes 852000 | tf_op jit(solution)/shard_map/all_to_all | solution.py:14
  60.4 0.3 copy.29
  60.7 1.5 fusion.19
  62.1 2.8 %collective-permute-start.1 = (bf16[512,512]{0,1:T(8,128)(2,1)}, bf16[512,512]{0,1:T(8,128)(2,1)}, u32[]{:S(2)}, u32[]{:S(2)}) collective-permute-start(bf16[512,512]{0,1:T(8,128)(2,1)} %fusion.19), channel_id=1, source_target_pairs={{0,256},{128,384},{256,0},{384,128},{1,257},{129,385},{257,1},{385... | collective-permute-start | bytes 1572872 | tf_op jit(solution)/shard_map/ppermute | solution.py:40
  65.0 2.4 %collective-permute-start = (bf16[512,512]{0,1:T(8,128)(2,1)}, bf16[512,512]{0,1:T(8,128)(2,1)}, u32[]{:S(2)}, u32[]{:S(2)}) collective-permute-start(bf16[512,512]{0,1:T(8,128)(2,1)} %fusion.19), channel_id=1, source_target_pairs={{0,128},{128,256},{256,384},{384,0},{1,129},{129,257},{257,385},{3... | collective-permute-start | bytes 1572872 | tf_op jit(solution)/shard_map/ppermute | solution.py:40
  67.4 4.1 %collective-permute-start.8 = (bf16[96,128]{1,0:T(8,128)(2,1)S(1)}, bf16[96,128]{1,0:T(8,128)(2,1)S(1)}, u32[]{:S(2)}, u32[]{:S(2)}) collective-permute-start(bf16[96,128]{1,0:T(8,128)(2,1)S(1)} %get-tuple-element.36), channel_id=1, source_target_pairs={{0,384},{128,0},{256,128},{384,256},{1,385},{129,1},{257,129},{385... | collective-permute-start | bytes 73736 | tf_op jit(solution)/shard_map/ppermute | solution.py:40
  71.5 0.1 pad_maximum_fusion
  71.7 2.8 %collective-permute-start.7 = (bf16[96,128]{1,0:T(8,128)(2,1)S(1)}, bf16[96,128]{1,0:T(8,128)(2,1)S(1)}, u32[]{:S(2)}, u32[]{:S(2)}) collective-permute-start(bf16[96,128]{1,0:T(8,128)(2,1)S(1)} %get-tuple-element.37), channel_id=1, source_target_pairs={{0,256},{128,384},{256,0},{384,128},{1,257},{129,385},{257,1},{385... | collective-permute-start | bytes 73736 | tf_op jit(solution)/shard_map/ppermute | solution.py:40
  74.4 1.9 %collective-permute-start.6 = (bf16[96,128]{1,0:T(8,128)(2,1)S(1)}, bf16[96,128]{1,0:T(8,128)(2,1)S(1)}, u32[]{:S(2)}, u32[]{:S(2)}) collective-permute-start(bf16[96,128]{1,0:T(8,128)(2,1)S(1)} %get-tuple-element.38), channel_id=1, source_target_pairs={{0,128},{128,256},{256,384},{384,0},{1,129},{129,257},{257,385},{3... | collective-permute-start | bytes 73736 | tf_op jit(solution)/shard_map/ppermute | solution.py:40
  76.4 4.6 %collective-permute-start.2 = (bf16[512,512]{0,1:T(8,128)(2,1)}, bf16[512,512]{0,1:T(8,128)(2,1)S(1)}, u32[]{:S(2)}, u32[]{:S(2)}) collective-permute-start(bf16[512,512]{0,1:T(8,128)(2,1)} %fusion.19), channel_id=1, source_target_pairs={{0,384},{128,0},{256,128},{384,256},{1,385},{129,1},{257,129},{385... | collective-permute-start | bytes 1572872 | tf_op jit(solution)/shard_map/ppermute | solution.py:40
  80.9 1.0 dynamic-slice_bitcast_fusion.10
  81.9 6.3 %collective-permute-done.7 = bf16[96,128]{1,0:T(8,128)(2,1)S(1)} collective-permute-done((bf16[96,128]{1,0:T(8,128)(2,1)S(1)}, bf16[96,128]{1,0:T(8,128)(2,1)S(1)}, u32[]{:S(2)}, u32[]{:S(2)}) %collective-permute-start.7) | collective-permute-done | bytes 24608 | tf_op jit(solution)/shard_map/ppermute | solution.py:40
  88.2 3.7 %collective-permute-done.6 = bf16[96,128]{1,0:T(8,128)(2,1)S(1)} collective-permute-done((bf16[96,128]{1,0:T(8,128)(2,1)S(1)}, bf16[96,128]{1,0:T(8,128)(2,1)S(1)}, u32[]{:S(2)}, u32[]{:S(2)}) %collective-permute-start.6) | collective-permute-done | bytes 24608 | tf_op jit(solution)/shard_map/ppermute | solution.py:40
  91.9 1.0 broadcast_in_dim.106
  92.9 4.9 %all-to-all-start.4 = ((bf16[8,384,128]{2,1,0:T(8,128)(2,1)}), bf16[8,384,128]{2,1,0:T(8,128)(2,1)S(1)}, u32[]{:S(2)}, u32[]{:S(2)}) async-start(bf16[8,384,128]{2,1,0:T(8,128)(2,1)} %broadcast_in_dim.106), calls=%async_computation.4 | async-start | bytes 1572864 | tf_op jit(solution)/shard_map/all_to_all | solution.py:14
  97.8 0.2 fusion.21
  98.1 2.0 %fusion.8 = f32[224,512]{1,0:T(8,128)S(1)} fusion(bf16[512,512]{0,1:T(8,128)(2,1)} %collective-permute-done.1, bf16[512,512]{0,1:T(8,128)(2,1)} %collective-permute-done, bf16[512,512]{0,1:T(8,128)(2,1)} %fusion.19, bf16[224,512]{1,0:T(8,128)(2,1)} %get-tuple-element.32, bf16[224,512]{1,0:T(8,128)(2,1)S(1)} %copy-done.9, bf16[224,512]{1,0:T(8,128)(2,1)S(1)} %copy-done.8), kind=kOutput, calls=%fused_computation.11 | convolution fusion | flops 359104512 | bytes 2719744 | tf_op jit(solution)/shard_map/dot_general | solution.py:23
  100.1 0.3 fusion.69
  100.4 0.7 copy-done.4
  101.1 0.2 copy-done.6
  101.3 1.0 fusion.73
  102.4 0.2 fusion.22
  102.5 11.7 %all-gather = bf16[896,512]{1,0:T(8,128)(2,1)S(1)} all-gather(bf16[224,512]{1,0:T(8,128)(2,1)S(1)} %get-tuple-element.9), channel_id=2, replica_groups=mesh['dp_0'=4,'dp_1'=8,'expert'=16] {'dp_0'}, dimensions={0}, use_global_device_ids=true | all-gather | bytes 1146880 | tf_op jit(solution)/shard_map/all_gather | solution.py:172
  114.3 2.1 %fusion.17 = bf16[768,512]{1,0:T(8,128)(2,1)S(1)} fusion(bf16[896,512]{1,0:T(8,128)(2,1)S(1)} %all-gather, bf16[224,512]{1,0:T(8,128)(2,1)S(1)} %copy-done.11, bf16[224,512]{1,0:T(8,128)(2,1)S(1)} %copy-done.12, bf16[224,512]{1,0:T(8,128)(2,1)} %get-tuple-element.25, bf16[224,512]{1,0:T(8,128)(2,1)S(1)} %copy-done.10, s32[512]{0:T(512)S(1)} %bitcast.227), kind=kOutput, calls=%fused_computation.23 | convolution fusion | flops 877133824 | bytes 2623488 | tf_op jit(solution)/shard_map/dot_general | solution.py:23
  116.4 0.2 reshape.194
  116.7 1.0 fusion.39
  117.7 3.7 %all-to-all-done.4 = bf16[8,384,128]{2,1,0:T(8,128)(2,1)S(1)} async-done(((bf16[8,384,128]{2,1,0:T(8,128)(2,1)}), bf16[8,384,128]{2,1,0:T(8,128)(2,1)S(1)}, u32[]{:S(2)}, u32[]{:S(2)}) %all-to-all-start.4) | async-done | bytes 786464 | tf_op jit(solution)/shard_map/all_to_all | solution.py:14
  121.4 4.5 %all-to-all-start.2 = ((bf16[32,104,128]{2,1,0:T(8,128)(2,1)}), bf16[32,104,128]{2,1,0:T(8,128)(2,1)S(1)}, u32[]{:S(2)}, u32[]{:S(2)}) async-start(bf16[32,104,128]{2,1,0:T(8,128)(2,1)} %fusion.39), calls=%async_computation.2 | async-start | bytes 1703936 | tf_op jit(solution)/shard_map/all_to_all | solution.py:14
  125.9 0.3 copy.32
  126.2 0.3 copy-done.13
  126.5 1.2 convolution_convert_fusion.1
  127.8 3.3 %collective-permute-start.11 = (bf16[224,512]{1,0:T(8,128)(2,1)S(1)}, bf16[224,512]{1,0:T(8,128)(2,1)S(1)}, u32[]{:S(2)}, u32[]{:S(2)}) collective-permute-start(bf16[224,512]{1,0:T(8,128)(2,1)S(1)} %get-tuple-element.15), channel_id=1, source_target_pairs={{0,128},{128,256},{256,384},{384,0},{1,129},{129,257},{257,385},{3... | collective-permute-start | bytes 688136 | tf_op jit(solution)/shard_map/ppermute | solution.py:40
  131.1 4.3 %collective-permute-start.10 = (bf16[224,512]{1,0:T(8,128)(2,1)S(1)}, bf16[224,512]{1,0:T(8,128)(2,1)S(1)}, u32[]{:S(2)}, u32[]{:S(2)}) collective-permute-start(bf16[224,512]{1,0:T(8,128)(2,1)S(1)} %get-tuple-element.16), channel_id=1, source_target_pairs={{0,256},{128,384},{256,0},{384,128},{1,257},{129,385},{257,1},{385... | collective-permute-start | bytes 688136 | tf_op jit(solution)/shard_map/ppermute | solution.py:40
  135.5 3.0 %collective-permute-start.9 = (bf16[224,512]{1,0:T(8,128)(2,1)S(1)}, bf16[224,512]{1,0:T(8,128)(2,1)S(1)}, u32[]{:S(2)}, u32[]{:S(2)}) collective-permute-start(bf16[224,512]{1,0:T(8,128)(2,1)S(1)} %get-tuple-element.17), channel_id=1, source_target_pairs={{0,384},{128,0},{256,128},{384,256},{1,385},{129,1},{257,129},{385... | collective-permute-start | bytes 688136 | tf_op jit(solution)/shard_map/ppermute | solution.py:40
  138.6 2.2 %convolution_convert_fusion = bf16[224,2048]{1,0:T(8,128)(2,1)S(1)} fusion(bf16[512,512]{0,1:T(8,128)(2,1)S(1)} %copy-done.3, bf16[512,512]{0,1:T(8,128)(2,1)} %collective-permute-done.1, bf16[512,512]{0,1:T(8,128)(2,1)} %collective-permute-done, bf16[512,512]{0,1:T(8,128)(2,1)} %fusion.19, bf16[1,512,224]{1,2,0:T(8,128)(2,1)S(1)} %copy-done.7, ...), kind=kOutput, calls=%fused_computation | convolution fusion | flops 479870976 | bytes 3475456 | tf_op jit(solution)/shard_map/dot_general | solution.py:23
  140.8 8.5 %collective-permute-done.10 = bf16[224,512]{1,0:T(8,128)(2,1)S(1)} collective-permute-done((bf16[224,512]{1,0:T(8,128)(2,1)S(1)}, bf16[224,512]{1,0:T(8,128)(2,1)S(1)}, u32[]{:S(2)}, u32[]{:S(2)}) %collective-permute-start.10) | collective-permute-done | bytes 229408 | tf_op jit(solution)/shard_map/ppermute | solution.py:40
  149.3 0.7 collective-permute-done.9
  150.0 0.1 pad_maximum_fusion.1
  150.3 0.1 convert_reduce_fusion
  150.4 0.5 copy-done.19
  150.9 0.2 reduce-precision_convert_fusion
  151.2 0.7 pad_maximum_fusion.2
  151.9 5.7 %all-to-all-start.3 = ((bf16[16,32,128]{2,1,0:T(8,128)(2,1)}), bf16[16,32,128]{2,1,0:T(8,128)(2,1)S(1)}, u32[]{:S(2)}, u32[]{:S(2)}) async-start(bf16[16,32,128]{2,1,0:T(8,128)(2,1)} %pad_maximum_fusion.2), calls=%async_computation.3 | async-start | bytes 262144 | tf_op jit(solution)/shard_map/all_to_all | solution.py:14
  157.6 1.5 maximum_bitcast_fusion
  159.1 7.7 %all-to-all-done.3 = bf16[16,32,128]{2,1,0:T(8,128)(2,1)S(1)} async-done(((bf16[16,32,128]{2,1,0:T(8,128)(2,1)}), bf16[16,32,128]{2,1,0:T(8,128)(2,1)S(1)}, u32[]{:S(2)}, u32[]{:S(2)}) %all-to-all-start.3) | async-done | bytes 131104 | tf_op jit(solution)/shard_map/all_to_all | solution.py:14
  166.9 0.6 mul.104
  167.4 1.1 fusion.20
  (80 shorter events, 1.1 us)
Async XLA Ops:
  0.6 16.1 %copy-start.18 = (f32[1,256]{1,0:T(1,128)S(1)}, f32[1,256]{1,0:T(1,128)}, u32[]{:S(2)}) copy-start(f32[1,256]{1,0:T(1,128)} %param.10) | copy-start | bytes 3076
  4.9 22.0 %all-to-all-start = ((bf16[16,24,256]{2,1,0:T(8,128)(2,1)}), bf16[16,24,256]{2,1,0:T(8,128)(2,1)S(1)}, u32[]{:S(2)}, u32[]{:S(2)}) async-start(bf16[16,24,256]{2,1,0:T(8,128)(2,1)} %bitcast.4), calls=%async_computation | async-start | bytes 393216 | tf_op jit(solution)/shard_map/all_to_all | solution.py:14
  16.7 11.3 %copy-start.20 = (s32[128]{0:T(128)}, s32[128]{0:T(128)S(1)}, u32[]{:S(2)}) copy-start(s32[128]{0:T(128)S(1)} %pad.16) | copy-start | bytes 1540
  28.0 9.9 %copy-start = (bf16[1,224,2048]{2,1,0:T(8,128)(2,1)S(1)}, bf16[1,224,2048]{2,1,0:T(8,128)(2,1)}, u32[]{:S(2)}) copy-start(bf16[1,224,2048]{2,1,0:T(8,128)(2,1)} %param.15) | copy-start | bytes 2752516
  28.0 32.3 %all-to-all-start.1 = ((bf16[32,104,128]{2,1,0:T(8,128)(2,1)}), bf16[32,104,128]{2,1,0:T(8,128)(2,1)S(1)}, u32[]{:S(2)}, u32[]{:S(2)}) async-start(bf16[32,104,128]{2,1,0:T(8,128)(2,1)} %bitcast.10), calls=%async_computation.1 | async-start | bytes 1703936 | tf_op jit(solution)/shard_map/all_to_all | solution.py:14
  37.9 11.7 %copy-start.1 = (bf16[1,224,2048]{2,1,0:T(8,128)(2,1)S(1)}, bf16[1,224,2048]{2,1,0:T(8,128)(2,1)}, u32[]{:S(2)}) copy-start(bf16[1,224,2048]{2,1,0:T(8,128)(2,1)} %param.14) | copy-start | bytes 2752516
  38.7 28.7 %collective-permute-start.3 = (bf16[224,512]{1,0:T(8,128)(2,1)}, bf16[224,512]{1,0:T(8,128)(2,1)S(1)}, u32[]{:S(2)}, u32[]{:S(2)}) collective-permute-start(bf16[224,512]{1,0:T(8,128)(2,1)} %get-tuple-element.27), channel_id=1, source_target_pairs={{0,128},{128,256},{256,384},{384,0},{1,129},{129,257},{257,385},{3... | collective-permute-start | bytes 688136 | tf_op jit(solution)/shard_map/ppermute | solution.py:40
  41.8 29.7 %collective-permute-start.5 = (bf16[224,512]{1,0:T(8,128)(2,1)S(1)}, bf16[224,512]{1,0:T(8,128)(2,1)S(1)}, u32[]{:S(2)}, u32[]{:S(2)}) collective-permute-start(bf16[224,512]{1,0:T(8,128)(2,1)S(1)} %get-tuple-element.28), channel_id=1, source_target_pairs={{0,384},{128,0},{256,128},{384,256},{1,385},{129,1},{257,129},{385... | collective-permute-start | bytes 688136 | tf_op jit(solution)/shard_map/ppermute | solution.py:40
  45.2 26.4 %collective-permute-start.4 = (bf16[224,512]{1,0:T(8,128)(2,1)S(1)}, bf16[224,512]{1,0:T(8,128)(2,1)S(1)}, u32[]{:S(2)}, u32[]{:S(2)}) collective-permute-start(bf16[224,512]{1,0:T(8,128)(2,1)S(1)} %get-tuple-element.29), channel_id=1, source_target_pairs={{0,256},{128,384},{256,0},{384,128},{1,257},{129,385},{257,1},{385... | collective-permute-start | bytes 688136 | tf_op jit(solution)/shard_map/ppermute | solution.py:40
  51.8 8.9 %copy-start.14 = (s32[1,512]{1,0:T(1,128)}, s32[1,512]{1,0:T(1,128)S(1)}, u32[]{:S(2)}) copy-start(s32[1,512]{1,0:T(1,128)S(1)} %get-tuple-element.40) | copy-start | bytes 6148
  62.1 35.9 %collective-permute-start.1 = (bf16[512,512]{0,1:T(8,128)(2,1)}, bf16[512,512]{0,1:T(8,128)(2,1)}, u32[]{:S(2)}, u32[]{:S(2)}) collective-permute-start(bf16[512,512]{0,1:T(8,128)(2,1)} %fusion.19), channel_id=1, source_target_pairs={{0,256},{128,384},{256,0},{384,128},{1,257},{129,385},{257,1},{385... | collective-permute-start | bytes 1572872 | tf_op jit(solution)/shard_map/ppermute | solution.py:40
  65.0 33.1 %collective-permute-start = (bf16[512,512]{0,1:T(8,128)(2,1)}, bf16[512,512]{0,1:T(8,128)(2,1)}, u32[]{:S(2)}, u32[]{:S(2)}) collective-permute-start(bf16[512,512]{0,1:T(8,128)(2,1)} %fusion.19), channel_id=1, source_target_pairs={{0,128},{128,256},{256,384},{384,0},{1,129},{129,257},{257,385},{3... | collective-permute-start | bytes 1572872 | tf_op jit(solution)/shard_map/ppermute | solution.py:40
  67.4 9.0 %collective-permute-start.8 = (bf16[96,128]{1,0:T(8,128)(2,1)S(1)}, bf16[96,128]{1,0:T(8,128)(2,1)S(1)}, u32[]{:S(2)}, u32[]{:S(2)}) collective-permute-start(bf16[96,128]{1,0:T(8,128)(2,1)S(1)} %get-tuple-element.36), channel_id=1, source_target_pairs={{0,384},{128,0},{256,128},{384,256},{1,385},{129,1},{257,129},{385... | collective-permute-start | bytes 73736 | tf_op jit(solution)/shard_map/ppermute | solution.py:40
  71.7 16.5 %collective-permute-start.7 = (bf16[96,128]{1,0:T(8,128)(2,1)S(1)}, bf16[96,128]{1,0:T(8,128)(2,1)S(1)}, u32[]{:S(2)}, u32[]{:S(2)}) collective-permute-start(bf16[96,128]{1,0:T(8,128)(2,1)S(1)} %get-tuple-element.37), channel_id=1, source_target_pairs={{0,256},{128,384},{256,0},{384,128},{1,257},{129,385},{257,1},{385... | collective-permute-start | bytes 73736 | tf_op jit(solution)/shard_map/ppermute | solution.py:40
  74.4 17.5 %collective-permute-start.6 = (bf16[96,128]{1,0:T(8,128)(2,1)S(1)}, bf16[96,128]{1,0:T(8,128)(2,1)S(1)}, u32[]{:S(2)}, u32[]{:S(2)}) collective-permute-start(bf16[96,128]{1,0:T(8,128)(2,1)S(1)} %get-tuple-element.38), channel_id=1, source_target_pairs={{0,128},{128,256},{256,384},{384,0},{1,129},{129,257},{257,385},{3... | collective-permute-start | bytes 73736 | tf_op jit(solution)/shard_map/ppermute | solution.py:40
  76.4 23.7 %collective-permute-start.2 = (bf16[512,512]{0,1:T(8,128)(2,1)}, bf16[512,512]{0,1:T(8,128)(2,1)S(1)}, u32[]{:S(2)}, u32[]{:S(2)}) collective-permute-start(bf16[512,512]{0,1:T(8,128)(2,1)} %fusion.19), channel_id=1, source_target_pairs={{0,384},{128,0},{256,128},{384,256},{1,385},{129,1},{257,129},{385... | collective-permute-start | bytes 1572872 | tf_op jit(solution)/shard_map/ppermute | solution.py:40
  92.9 5.2 %copy-start.8 = (bf16[224,512]{1,0:T(8,128)(2,1)S(1)}, bf16[224,512]{1,0:T(8,128)(2,1)}, u32[]{:S(2)}) copy-start(bf16[224,512]{1,0:T(8,128)(2,1)} %get-tuple-element.30) | copy-start | bytes 688132
  92.9 5.2 %copy-start.9 = (bf16[224,512]{1,0:T(8,128)(2,1)S(1)}, bf16[224,512]{1,0:T(8,128)(2,1)}, u32[]{:S(2)}) copy-start(bf16[224,512]{1,0:T(8,128)(2,1)} %get-tuple-element.31) | copy-start | bytes 688132
  92.9 28.5 %all-to-all-start.4 = ((bf16[8,384,128]{2,1,0:T(8,128)(2,1)}), bf16[8,384,128]{2,1,0:T(8,128)(2,1)S(1)}, u32[]{:S(2)}, u32[]{:S(2)}) async-start(bf16[8,384,128]{2,1,0:T(8,128)(2,1)} %broadcast_in_dim.106), calls=%async_computation.4 | async-start | bytes 1572864 | tf_op jit(solution)/shard_map/all_to_all | solution.py:14
  98.0 2.4 %copy-start.16 = (f32[512]{0:T(512)}, f32[512]{0:T(512)S(1)}, u32[]{:S(2)}) copy-start(f32[512]{0:T(512)S(1)} %fusion.21) | copy-start | bytes 6148
  100.1 1.1 copy-start.4
  100.1 1.2 copy-start.6
  100.1 2.2 %copy-start.2 = (bf16[512,512]{0,1:T(8,128)(2,1)}, bf16[512,512]{0,1:T(8,128)(2,1)S(1)}, u32[]{:S(2)}) copy-start(bf16[512,512]{0,1:T(8,128)(2,1)S(1)} %collective-permute-done.2) | copy-start | bytes 1572868
  102.3 11.9 %copy-start.10 = (bf16[224,512]{1,0:T(8,128)(2,1)S(1)}, bf16[224,512]{1,0:T(8,128)(2,1)}, u32[]{:S(2)}) copy-start(bf16[224,512]{1,0:T(8,128)(2,1)} %get-tuple-element.22) | copy-start | bytes 688132
  102.3 11.9 %copy-start.11 = (bf16[224,512]{1,0:T(8,128)(2,1)S(1)}, bf16[224,512]{1,0:T(8,128)(2,1)}, u32[]{:S(2)}) copy-start(bf16[224,512]{1,0:T(8,128)(2,1)} %get-tuple-element.23) | copy-start | bytes 688132
  102.3 11.9 %copy-start.12 = (bf16[224,512]{1,0:T(8,128)(2,1)S(1)}, bf16[224,512]{1,0:T(8,128)(2,1)}, u32[]{:S(2)}) copy-start(bf16[224,512]{1,0:T(8,128)(2,1)} %get-tuple-element.24) | copy-start | bytes 688132
  102.3 11.9 %copy-start.15 = (s32[1,512]{1,0:T(1,128)S(1)}, s32[1,512]{1,0:T(1,128)}, u32[]{:S(2)}) copy-start(s32[1,512]{1,0:T(1,128)} %copy-done.14) | copy-start | bytes 6148
  121.4 28.9 %all-to-all-start.2 = ((bf16[32,104,128]{2,1,0:T(8,128)(2,1)}), bf16[32,104,128]{2,1,0:T(8,128)(2,1)S(1)}, u32[]{:S(2)}, u32[]{:S(2)}) async-start(bf16[32,104,128]{2,1,0:T(8,128)(2,1)} %fusion.39), calls=%async_computation.2 | async-start | bytes 1703936 | tf_op jit(solution)/shard_map/all_to_all | solution.py:14
  125.9 0.7 copy-start.13
  127.7 10.8 %copy-start.3 = (bf16[512,512]{0,1:T(8,128)(2,1)S(1)}, bf16[512,512]{0,1:T(8,128)(2,1)}, u32[]{:S(2)}) copy-start(bf16[512,512]{0,1:T(8,128)(2,1)} %copy-done.2) | copy-start | bytes 1572868
  127.7 10.8 %copy-start.5 = (bf16[1,512,224]{1,2,0:T(8,128)(2,1)S(1)}, bf16[1,512,224]{1,2,0:T(8,128)(2,1)}, u32[]{:S(2)}) copy-start(bf16[1,512,224]{1,2,0:T(8,128)(2,1)} %param.12) | copy-start | bytes 688132
  127.7 10.8 %copy-start.7 = (bf16[1,512,224]{1,2,0:T(8,128)(2,1)S(1)}, bf16[1,512,224]{1,2,0:T(8,128)(2,1)}, u32[]{:S(2)}) copy-start(bf16[1,512,224]{1,2,0:T(8,128)(2,1)} %param.13) | copy-start | bytes 688132
  127.7 10.8 %copy-start.17 = (f32[512]{0:T(512)S(1)}, f32[512]{0:T(512)}, u32[]{:S(2)}) copy-start(f32[512]{0:T(512)} %copy-done.16) | copy-start | bytes 6148
  127.8 13.0 %collective-permute-start.11 = (bf16[224,512]{1,0:T(8,128)(2,1)S(1)}, bf16[224,512]{1,0:T(8,128)(2,1)S(1)}, u32[]{:S(2)}, u32[]{:S(2)}) collective-permute-start(bf16[224,512]{1,0:T(8,128)(2,1)S(1)} %get-tuple-element.15), channel_id=1, source_target_pairs={{0,128},{128,256},{256,384},{384,0},{1,129},{129,257},{257,385},{3... | collective-permute-start | bytes 688136 | tf_op jit(solution)/shard_map/ppermute | solution.py:40
  131.1 18.2 %collective-permute-start.10 = (bf16[224,512]{1,0:T(8,128)(2,1)S(1)}, bf16[224,512]{1,0:T(8,128)(2,1)S(1)}, u32[]{:S(2)}, u32[]{:S(2)}) collective-permute-start(bf16[224,512]{1,0:T(8,128)(2,1)S(1)} %get-tuple-element.16), channel_id=1, source_target_pairs={{0,256},{128,384},{256,0},{384,128},{1,257},{129,385},{257,1},{385... | collective-permute-start | bytes 688136 | tf_op jit(solution)/shard_map/ppermute | solution.py:40
  135.5 14.6 %collective-permute-start.9 = (bf16[224,512]{1,0:T(8,128)(2,1)S(1)}, bf16[224,512]{1,0:T(8,128)(2,1)S(1)}, u32[]{:S(2)}, u32[]{:S(2)}) collective-permute-start(bf16[224,512]{1,0:T(8,128)(2,1)S(1)} %get-tuple-element.17), channel_id=1, source_target_pairs={{0,384},{128,0},{256,128},{384,256},{1,385},{129,1},{257,129},{385... | collective-permute-start | bytes 688136 | tf_op jit(solution)/shard_map/ppermute | solution.py:40
  150.2 0.7 copy-start.19
  150.3 0.7 copy-start.21
  151.9 14.9 %all-to-all-start.3 = ((bf16[16,32,128]{2,1,0:T(8,128)(2,1)}), bf16[16,32,128]{2,1,0:T(8,128)(2,1)S(1)}, u32[]{:S(2)}, u32[]{:S(2)}) async-start(bf16[16,32,128]{2,1,0:T(8,128)(2,1)} %pad_maximum_fusion.2), calls=%async_computation.3 | async-start | bytes 262144 | tf_op jit(solution)/shard_map/all_to_all | solution.py:14
